TPU v7x, 32 devices: a whole 2x2x4 slice. The times are simulated.
32 devices in a mesh: groups: 2 (over x), inst: 4 (over z), tp: 4 (over y, core).
Axes of the slice: x: 2, y: 2, z: 4, core: 2. Of those that a mesh axis runs over, the one named last changes fastest.
Arguments:
- qkv_first: bfloat16 [48, 10240], P(('groups', 'inst'), 'tp'), parts along dimension 0, may hold values from -5 to 5
- qkv_second: bfloat16 [48, 10240], P(('groups', 'inst'), 'tp'), parts along dimension 0, may hold values from -5 to 5
- w_out: bfloat16 [8192, 8192], P(None, 'tp'), may hold values from -0.5 to 0.5
- kv_cache: bfloat16 [512, 2, 16, 1024], P(('groups', 'inst', 'tp')), parts along dimension 0, may hold values from -4096 to 4096
- lengths: int32 [48], P('groups'), parts along dimension 0, may hold values from 4 to 126, as said below
- page_table: int32 [48, 8], P(('groups', 'inst')), parts along dimension 0, may hold values from -1 to 63, as said below
- moves: int32 [8, 2], P('groups'), parts along dimension 0, may hold values from 0 to 23, as said below
- dest_pages: int32 [8, 8], P('groups'), parts along dimension 0, may hold values from 0 to 63, as said below
Outputs:
- out_first: bfloat16 [48, 8192], P(('groups', 'inst'), 'tp'), parts along dimension 0
- out_second: bfloat16 [48, 8192], P(('groups', 'inst'), 'tp'), parts along dimension 0
- kv_out: bfloat16 [512, 2, 16, 1024], P(('groups', 'inst', 'tp')), parts along dimension 0
There are 2 independent parts, one for each index of `groups`. A program takes and returns all parts, laid end to end along the dimension named above; an argument that names none is the same for every part. Nothing has to cross between parts.
Inputs may be any that keep to these rules, and one draw needn't show every extreme that they name: Half of the instances, drawn afresh, are heavy: lengths of their requests run from 64 to 126, those of the other instances from 4 to 16. Entry j of request r is a page of its instance's pool for j < ceil((lengths[r] + 2) / 16) and -1 after; such a page p has floor(p / 16) = j mod (4); no pool page is named twice by page_table and dest_pages together. Row i moves request moves[i, 0], a number from 0 to 23, to instance moves[i, 1], a number from 0 to 3; every heavy instance sends exactly one request to every other instance, those are the light ones, and a moved request's length is at least (7) * 16 - 1. `dest_pages`: entry j of row i, for every j < 8, is a page p of the destination's pool that page_table leaves free, with floor(p / 16) = j mod (4).
All inputs are finite; a program needn't handle non-finite values.
Results may differ from a plain program's by a relative error of at most 0.015.
Values may be sent and summed in bfloat16 or wider, within the bound.
No kernel may reach another device: no remote copies, remote signals or barrier semaphores. Data moves between devices by JAX's collectives and lax.ppermute only.
A program may use at most 64 MiB of HBM per device.

v0:
```python
import math

import jax
import jax.numpy as jnp
from jax import lax
from jax.sharding import PartitionSpec as P

QUERY_HEADS = 64
KEY_VALUE_HEADS = 8
HEAD_SIZE = 128


NEG_LARGE = -1e30


def merged(x, axis, combine):
    everything = jax.tree.map(lambda part: lax.all_gather(part, axis), x)
    initial = jax.tree.map(lambda part: part[0], everything)

    def step(k, so_far):
        return combine(so_far, jax.tree.map(lambda part: part[k], everything))

    return lax.fori_loop(1, lax.axis_size(axis), step, initial)


def gather_rows(token_rows):
    return lax.all_gather(token_rows, "tp", axis=1, tiled=True)


def ownership(index_table, tp_rank, shared_pages):
    page_ids = tp_rank * shared_pages + jnp.arange(shared_pages, dtype=jnp.int32)
    matches = index_table[None, :, :] == page_ids[:, None, None]
    owner_int = jnp.any(matches, axis=2).astype(jnp.int32)
    slot_ids = jnp.arange(index_table.shape[1], dtype=jnp.int32)
    page_number = jnp.sum(jnp.where(matches, slot_ids[None, None, :], 0), axis=(1, 2))
    page_owned = jnp.sum(owner_int, axis=1) > 0
    return (owner_int, page_number, page_owned)


def write_tokens(paged_memory, owners, positions, full_rows):
    owner_int, page_number, page_owned = owners
    shared_pages = paged_memory.shape[0]
    page_extent = paged_memory.shape[2]
    key_value_width = paged_memory.shape[3]
    kv_start = QUERY_HEADS * HEAD_SIZE
    fresh = full_rows[:, kv_start : kv_start + 2 * key_value_width]
    placed = jnp.dot(
        owner_int.astype(jnp.bfloat16), fresh, preferred_element_type=jnp.float32
    ).astype(jnp.bfloat16)
    placed = placed.reshape(shared_pages, 2, 1, key_value_width)
    page_target = jnp.sum(owner_int * positions[None, :], axis=1)
    offsets = page_number[:, None] * page_extent + jnp.arange(page_extent, dtype=jnp.int32)[None, :]
    page_hit = page_owned[:, None] & (offsets == page_target[:, None])
    return jnp.where(page_hit[:, None, :, None], placed, paged_memory)


def partials(paged_memory, owners, counts, full_rows):
    owner_int, page_number, page_owned = owners
    shared_pages = paged_memory.shape[0]
    page_extent = paged_memory.shape[2]
    group_width = QUERY_HEADS // KEY_VALUE_HEADS
    query_per_page = jnp.dot(
        owner_int.astype(jnp.bfloat16),
        full_rows[:, : QUERY_HEADS * HEAD_SIZE],
        preferred_element_type=jnp.float32,
    ).astype(jnp.bfloat16)
    heads_of_query = query_per_page.reshape(shared_pages, KEY_VALUE_HEADS, group_width, HEAD_SIZE)
    gathered_keys = paged_memory[:, 0].reshape(
        shared_pages, page_extent, KEY_VALUE_HEADS, HEAD_SIZE
    )
    gathered_values = paged_memory[:, 1].reshape(
        shared_pages, page_extent, KEY_VALUE_HEADS, HEAD_SIZE
    )
    logit_scores = jnp.einsum(
        "pkgd,ptkd->pkgt", heads_of_query, gathered_keys, preferred_element_type=jnp.float32
    ) / math.sqrt(HEAD_SIZE)
    page_count = jnp.sum(owner_int * counts[None, :], axis=1)
    offsets = page_number[:, None] * page_extent + jnp.arange(page_extent, dtype=jnp.int32)[None, :]
    visible = page_owned[:, None] & (offsets < page_count[:, None])
    position_mask = visible[:, None, None, :]
    logit_scores = jnp.where(position_mask, logit_scores, NEG_LARGE)
    page_top = jnp.max(logit_scores, axis=3).reshape(shared_pages, QUERY_HEADS)
    owner_mask = owner_int[:, :, None] > 0
    row_top = jnp.max(jnp.where(owner_mask, page_top[:, None, :], NEG_LARGE), axis=0)
    page_pointer = jnp.max(jnp.where(owner_mask, row_top[None, :, :], NEG_LARGE), axis=1)
    exponent = jnp.where(
        position_mask,
        jnp.exp(logit_scores - page_pointer.reshape(shared_pages, KEY_VALUE_HEADS, group_width, 1)),
        0.0,
    )
    page_total = jnp.sum(exponent, axis=3).reshape(shared_pages, QUERY_HEADS)
    weights = exponent.astype(jnp.bfloat16)
    page_sums = jnp.einsum(
        "pkgt,ptkd->pkgd", weights, gathered_values, preferred_element_type=jnp.float32
    ).reshape(shared_pages, QUERY_HEADS * HEAD_SIZE)
    owner_float = owner_int.astype(jnp.float32)
    totals = jnp.einsum("pr,ph->rh", owner_float, page_total, precision=lax.Precision.HIGHEST)
    accumulated = jnp.einsum("pr,ph->rh", owner_float, page_sums, precision=lax.Precision.HIGHEST)
    return (row_top, totals, accumulated)


def join_parts(former, latter):
    top_former, total_former, summed_former = former
    top_latter, total_latter, summed_latter = latter
    row_top = jnp.maximum(top_former, top_latter)
    scale_former = jnp.exp(top_former - row_top)
    scale_latter = jnp.exp(top_latter - row_top)
    row_total = total_former * scale_former + total_latter * scale_latter
    row_count = summed_former.shape[0]
    joined = (
        summed_former.reshape(row_count, -1, HEAD_SIZE) * scale_former[:, :, None]
        + summed_latter.reshape(row_count, -1, HEAD_SIZE) * scale_latter[:, :, None]
    )
    return (row_top, row_total, joined.reshape(row_count, -1))


def safe_total(row_total):
    return jnp.where(row_total > 0.0, row_total, 1.0)


def mixed_heads(parts):
    maxima, totals, accumulated = parts
    row_top, row_total, summed = merged((maxima, totals, accumulated), "tp", join_parts)
    row_count = summed.shape[0]
    return (
        (summed.reshape(row_count, -1, HEAD_SIZE) / safe_total(row_total)[..., None])
        .reshape(row_count, -1)
        .astype(jnp.bfloat16)
    )


def project(mixed, w_out):
    return jnp.dot(mixed, w_out, preferred_element_type=jnp.float32).astype(jnp.bfloat16)


def local(qkv_first, qkv_second, w_out, kv_cache, lengths, page_table, moves, dest_pages):
    tp_count = lax.axis_size("tp")
    inst_count = lax.axis_size("inst")
    tp_rank = lax.axis_index("tp")
    inst_index = lax.axis_index("inst")
    row_count = page_table.shape[0]
    shared_pages = kv_cache.shape[0]
    max_pages = page_table.shape[1]
    per_rank = max_pages // tp_count
    my_lengths = lax.dynamic_slice_in_dim(lengths, inst_index * row_count, row_count)
    first_full = gather_rows(qkv_first)
    owners_one = ownership(page_table, tp_rank, shared_pages)
    cache_one = write_tokens(kv_cache, owners_one, my_lengths, first_full)
    out_first = project(
        mixed_heads(partials(cache_one, owners_one, my_lengths + 1, first_full)), w_out
    )
    move_request = moves[:, 0]
    move_dest = moves[:, 1]
    move_source = move_request // row_count
    instances = jnp.arange(inst_count, dtype=jnp.int32)
    move_ids = jnp.arange(moves.shape[0], dtype=jnp.int32)
    send_match = (move_source[None, :] == inst_index) & (move_dest[None, :] == instances[:, None])
    send_has = jnp.any(send_match, axis=1)
    send_move = jnp.sum(jnp.where(send_match, move_ids[None, :], 0), axis=1)
    send_rows = jnp.where(send_has, move_request[send_move] - inst_index * row_count, 0)
    rank_cols = tp_rank + tp_count * jnp.arange(per_rank, dtype=jnp.int32)
    send_pages = jnp.clip(
        page_table[send_rows][:, rank_cols] - tp_rank * shared_pages, 0, shared_pages - 1
    )
    recv_match = (move_source[None, :] == instances[:, None]) & (move_dest[None, :] == inst_index)
    recv_has = jnp.any(recv_match, axis=1)
    recv_move = jnp.sum(jnp.where(recv_match, move_ids[None, :], 0), axis=1)
    recv_table = jnp.where(recv_has[:, None], dest_pages[recv_move], -1)
    recv_pages = recv_table[:, rank_cols] - tp_rank * shared_pages
    second_full = gather_rows(qkv_second)
    positions = my_lengths + 1
    cache_pre = write_tokens(cache_one, owners_one, positions, second_full)
    out_second = project(
        mixed_heads(partials(cache_pre, owners_one, positions + 1, second_full)), w_out
    )
    paged_memory = cache_pre
    outgoing = jnp.where(
        send_has[:, None, None, None, None], paged_memory[send_pages], jnp.zeros((), jnp.bfloat16)
    )
    arrived = lax.all_to_all(outgoing, "inst", split_axis=0, concat_axis=0, tiled=True)
    targets = jnp.where(recv_has[:, None], recv_pages, shared_pages).reshape(-1)
    paged_memory = paged_memory.at[targets].set(
        arrived.reshape((-1,) + paged_memory.shape[1:]), mode="drop"
    )
    freed_rows = jnp.where(send_has[:, None], send_pages, shared_pages).reshape(-1)
    cleared = jnp.zeros((freed_rows.shape[0],) + paged_memory.shape[1:], jnp.bfloat16)
    kv_out = paged_memory.at[freed_rows].set(cleared, mode="drop")
    return (out_first, out_second, kv_out)


def solution(mesh):
    placed = (
        P(("groups", "inst"), "tp"),
        P(("groups", "inst"), "tp"),
        P(None, "tp"),
        P(("groups", "inst", "tp"), None, None, None),
        P("groups"),
        P(("groups", "inst"), None),
        P("groups", None),
        P("groups", None),
    )
    return jax.shard_map(
        local,
        mesh=mesh,
        in_specs=placed,
        out_specs=(
            P(("groups", "inst"), "tp"),
            P(("groups", "inst"), "tp"),
            P(("groups", "inst", "tp"), None, None, None),
        ),
        check_vma=False,
    )
```

profile of v0, /device:TPU:0, one launch (start us, length us, event | category | flops | bytes accessed | tf_op | source)
XLA Modules:
  0.0 124.2 jit_solution(9361369197054579896)
XLA Ops:
  0.7 0.8 compare_reduce_fusion
  1.4 0.8 fusion.42
  2.2 0.8 slice_bitcast_fusion.7
  3.0 0.8 broadcast_compare_fusion
  4.0 0.7 broadcast_add_fusion.1
  4.9 6.9 %all_gather.42 = bf16[6,10240]{1,0:T(8,128)(2,1)S(1)} all-gather(bf16[6,2560]{1,0:T(8,128)(2,1)} %param.12), channel_id=1, replica_groups=mesh['groups'=2,'inst'=4,'tp'=4] {'tp'}, dimensions={1}, use_global_device_ids=true | all-gather | bytes 153600 | tf_op jit(solution)/shard_map/all_gather | solution.py:27
  11.8 0.2 convolution_convert_fusion.3
  12.0 5.8 %all_gather.49 = bf16[6,10240]{1,0:T(8,128)(2,1)S(1)} all-gather(bf16[6,2560]{1,0:T(8,128)(2,1)} %param.13), channel_id=1, replica_groups=mesh['groups'=2,'inst'=4,'tp'=4] {'tp'}, dimensions={1}, use_global_device_ids=true | all-gather | bytes 153600 | tf_op jit(solution)/shard_map/all_gather | solution.py:27
  17.8 0.2 convolution_convert_fusion.2
  18.1 0.6 gather_fusion.2
  18.8 1.2 %gather_fusion.3 = s32[4,8]{1,0:T(4,128)S(1)} fusion(s32[6,8]{1,0:T(8,128)} %param.17, s32[1024]{0:T(1024)S(1)} %pad_clamp_fusion.1), kind=kCustom, calls=%fused_computation.3 | custom fusion | bytes 272 | tf_op jit(solution)/shard_map/gather | solution.py:163
  20.1 0.6 gather_fusion.4
  21.0 1.5 %broadcast_select_fusion = (bf16[16,2,16,1024]{3,2,1,0:T(8,128)(2,1)S(1)}, bf16[16,2,16,1024]{3,2,1,0:T(8,128)(2,1)S(1)}) fusion(pred[16,16]{1,0:T(8,128)(4,1)S(1)} %get-tuple-element.420, bf16[16,2,1024]{2,1,0:T(2,128)(2,1)S(1)} %broadcast_in_dim.281, bf16[16,2,16,1024]{3,2,1,0:T(8,128)(2,1)} %param.15, bf16[16,2,1024]{2,1,0:T(2,128)(2,1)S(1)} %broadcast_in_dim.270, ...), kind=kLoop, calls=%fused_computation.46 | loop fusion | flops 1048576 | bytes 3277312 | tf_op jit(solution)/shard_map/jit(_where)/select_n | solution.py:54
  22.5 0.6 gather_fusion.5
  23.1 0.9 broadcast_select_fusion.2
  24.0 5.1 %all-to-all-start = ((bf16[4,2,2,16,1024]{4,3,2,1,0:T(8,128)(2,1)}), bf16[4,2,2,16,1024]{4,3,2,1,0:T(8,128)(2,1)}, u32[]{:S(2)}, u32[]{:S(2)}) async-start(bf16[4,2,2,16,1024]{4,3,2,1,0:T(8,128)(2,1)} %broadcast_select_fusion.2), calls=%async_computation | async-start | bytes 1048576 | tf_op jit(solution)/shard_map/all_to_all | solution.py:180
  29.1 0.3 fusion.8
  29.4 1.9 %fusion.9 = bf16[2,8,64,128]{3,1,2,0:T(8,128)(2,1)} fusion(bf16[6,10240]{1,0:T(8,128)(2,1)} %copy-done.2, pred[16,6]{0,1:T(8,128)(4,1)S(1)} %compare_reduce_fusion), kind=kOutput, calls=%fused_computation.43 | convolution fusion | flops 1704128 | bytes 393312 | tf_op jit(solution)/shard_map/dot_general | solution.py:62
  31.3 0.7 fusion.54
  32.0 0.7 select_reduce_fusion.8
  32.7 0.9 fusion.66
  33.7 0.5 fusion.68
  34.5 1.0 copy.74
  35.5 0.5 fusion.67
  36.6 0.3 fusion.14
  36.9 0.7 convolution_bitcast_fusion
  37.6 10.1 %all-gather.11 = f32[4,6,8192]{2,1,0:T(8,128)S(1)} all-gather(f32[1,6,8192]{2,1,0:T(8,128)S(1)} %convolution_bitcast_fusion), channel_id=7, replica_groups=mesh['groups'=2,'inst'=4,'tp'=4] {'tp'}, dimensions={0}, use_global_device_ids=true | all-gather | bytes 983040 | tf_op jit(solution)/shard_map/all_gather | solution.py:17
  47.7 0.7 copy.49
  48.4 0.8 copy.50
  49.2 2.0 %fusion.21 = (f32[16,8,8]{2,1,0:T(8,128)}, f32[16,8,8]{2,1,0:T(8,128)}) fusion(f32[16,8,8,16]{3,2,1,0:T(8,128)S(1)} %get-tuple-element.429, f32[16,8,8]{2,1,0:T(8,128)S(1)} %copy.50, pred[16,16]{1,0:T(8,128)(4,1)} %copy-done.3, f32[16,8,8,16]{3,2,1,0:T(8,128)S(1)} %get-tuple-element.427, f32[16,8,8]{2,1,0:T(8,128)S(1)} %copy.57, pred[16,16]{1,0:T(8,128)(4,1)} %copy-done.4), kind=kLoop, calls=%fused_computation.62 | loop fusion | flops 96256 | bytes 147968 | tf_op jit(solution)/shard_map/reduce_sum | solution.py:91
  51.2 0.9 copy.58
  52.3 5.2 %all-gather.10 = f32[4,6,64]{2,1,0:T(8,128)S(1)} all-gather(f32[1,6,64]{2,1,0:T(8,128)S(1)} %convolution_bitcast_fusion.2), channel_id=6, replica_groups=mesh['groups'=2,'inst'=4,'tp'=4] {'tp'}, dimensions={0}, use_global_device_ids=true | all-gather | bytes 7680 | tf_op jit(solution)/shard_map/all_gather | solution.py:17
  57.5 5.2 %all-gather.9 = f32[4,6,64]{2,1,0:T(8,128)S(1)} all-gather(f32[1,6,64]{2,1,0:T(8,128)S(1)} %bitcast.214), channel_id=5, replica_groups=mesh['groups'=2,'inst'=4,'tp'=4] {'tp'}, dimensions={0}, use_global_device_ids=true | all-gather | bytes 7680 | tf_op jit(solution)/shard_map/all_gather | solution.py:17
  62.7 1.5 %while.39 = (s32[]{:T(128)}, f32[6,64]{1,0:T(8,128)S(1)}, f32[6,64]{1,0:T(8,128)S(1)}, f32[6,8192]{1,0:T(8,128)S(1)}, f32[4,6,64]{2,1,0:T(8,128)S(1)}, /*index=5...) while((s32[]{:T(128)}, f32[6,64]{1,0:T(8,128)S(1)}, ...), condition=%wide.region_17.18_spmd, body=%wide.region_16.17_spmd.sunk | while | flops 149765 | bytes 1391767 | solution.py:23
  62.7 0.2 broadcast_bitcast_fusion.9
  62.9 0.3 fusion.80
  63.2 0.2 broadcast_bitcast_fusion.9
  63.4 0.3 fusion.80
  63.7 0.2 broadcast_bitcast_fusion.9
  63.9 0.3 fusion.80
  64.3 1.1 copy.71
  65.4 1.0 fusion.17
  66.4 0.7 convolution_bitcast_fusion.1
  67.1 10.1 %all-gather.8 = f32[4,6,8192]{2,1,0:T(8,128)S(1)} all-gather(f32[1,6,8192]{2,1,0:T(8,128)S(1)} %convolution_bitcast_fusion.1), channel_id=4, replica_groups=mesh['groups'=2,'inst'=4,'tp'=4] {'tp'}, dimensions={0}, use_global_device_ids=true | all-gather | bytes 983040 | tf_op jit(solution)/shard_map/all_gather | solution.py:17
  77.3 0.9 copy.51
  78.2 0.1 convolution_bitcast_fusion.3
  78.3 5.2 %all-gather.7 = f32[4,6,64]{2,1,0:T(8,128)S(1)} all-gather(f32[1,6,64]{2,1,0:T(8,128)S(1)} %convolution_bitcast_fusion.3), channel_id=3, replica_groups=mesh['groups'=2,'inst'=4,'tp'=4] {'tp'}, dimensions={0}, use_global_device_ids=true | all-gather | bytes 7680 | tf_op jit(solution)/shard_map/all_gather | solution.py:17
  83.5 5.4 %all-gather.6 = f32[4,6,64]{2,1,0:T(8,128)S(1)} all-gather(f32[1,6,64]{2,1,0:T(8,128)S(1)} %bitcast.213), channel_id=2, replica_groups=mesh['groups'=2,'inst'=4,'tp'=4] {'tp'}, dimensions={0}, use_global_device_ids=true | all-gather | bytes 7680 | tf_op jit(solution)/shard_map/all_gather | solution.py:17
  88.9 1.5 %while.38 = (s32[]{:T(128)}, f32[6,64]{1,0:T(8,128)S(1)}, f32[6,64]{1,0:T(8,128)S(1)}, f32[6,8192]{1,0:T(8,128)S(1)}, f32[4,6,64]{2,1,0:T(8,128)S(1)}, /*index=5...) while((s32[]{:T(128)}, f32[6,64]{1,0:T(8,128)S(1)}, ...), condition=%wide.region_10.11_spmd, body=%wide.region_9.10_spmd.sunk | while | flops 149765 | bytes 1391767 | solution.py:23
  88.9 0.2 broadcast_bitcast_fusion.8
  89.1 0.3 fusion.78
  89.4 0.2 broadcast_bitcast_fusion.8
  89.6 0.3 fusion.78
  89.9 0.2 broadcast_bitcast_fusion.8
  90.1 0.3 fusion.78
  90.5 0.7 fusion.55
  91.2 0.6 gather_fusion
  91.8 0.7 broadcast_select_fusion.3
  92.5 0.7 gather_fusion.1
  93.2 13.5 %convolution_convert_fusion.4 = bf16[6,2048]{1,0:T(8,128)(2,1)} fusion(bf16[8192,2048]{1,0:T(8,128)(2,1)} %param.14, f32[6,8192]{1,0:T(8,128)S(1)} %get-tuple-element.359, f32[1,6,64,128]{3,2,1,0:T(8,128)S(1)} %broadcast_bitcast_fusion.4), kind=kOutput, calls=%fused_computation.36 | convolution fusion | flops 201437184 | bytes 33972224 | tf_op jit(solution)/shard_map/dot_general | solution.py:133
  106.7 13.5 %convolution_convert_fusion.5 = bf16[6,2048]{1,0:T(8,128)(2,1)} fusion(bf16[8192,2048]{1,0:T(8,128)(2,1)} %param.14, f32[6,8192]{1,0:T(8,128)S(1)} %get-tuple-element.357, f32[1,6,64,128]{3,2,1,0:T(8,128)S(1)} %broadcast_bitcast_fusion.5), kind=kOutput, calls=%fused_computation.37 | convolution fusion | flops 201437184 | bytes 33972224 | tf_op jit(solution)/shard_map/dot_general | solution.py:133
  120.6 1.8 %scatter_fusion = bf16[16,2,16,1024]{3,2,1,0:T(8,128)(2,1)S(1)} fusion(bf16[16,2,16,1024]{3,2,1,0:T(8,128)(2,1)S(1)} %get-tuple-element.407, s32[8]{0:T(128)S(1)} %fusion.57, bf16[8,2,16,1024]{3,2,1,0:T(8,128)(2,1)} %bitcast.39), kind=kCustom, calls=%fused_computation.6 | custom fusion | bytes 1572896 | tf_op jit(solution)/shard_map/scatter | solution.py:182
  122.4 0.8 scatter_fusion.1
  123.2 1.0 copy-done.1
  (85 shorter events, 3.0 us)
Async XLA Ops:
  0.6 90.6 %copy-start = (s32[4,8]{1,0:T(4,128)S(1)}, s32[4,8]{1,0:T(4,128)}, u32[]{:S(2)}) copy-start(s32[4,8]{1,0:T(4,128)} %param.19) | copy-start | bytes 388
  3.9 32.1 %copy-start.8 = (pred[4]{0:T(512)(128)(4,1)}, pred[4]{0:T(512)(128)(4,1)S(1)}, u32[]{:S(2)}) copy-start(pred[4]{0:T(512)(128)(4,1)S(1)} %fusion.53) | copy-start | bytes 16
  17.8 3.2 %copy-start.2 = (bf16[6,10240]{1,0:T(8,128)(2,1)}, bf16[6,10240]{1,0:T(8,128)(2,1)S(1)}, u32[]{:S(2)}) copy-start(bf16[6,10240]{1,0:T(8,128)(2,1)S(1)} %all_gather.49) | copy-start | bytes 368644
  20.1 2.4 %copy-start.7 = (s32[1024]{0:T(1024)}, s32[1024]{0:T(1024)S(1)}, u32[]{:S(2)}) copy-start(s32[1024]{0:T(1024)S(1)} %pad_clamp_fusion.3) | copy-start | bytes 12292
  20.7 1.8 %copy-start.5 = (s32[2,4]{1,0:T(2,128)}, s32[2,4]{1,0:T(2,128)S(1)}, u32[]{:S(2)}) copy-start(s32[2,4]{1,0:T(2,128)S(1)} %gather_fusion.4) | copy-start | bytes 100
  21.0 15.3 %copy-start.3 = (pred[16,16]{1,0:T(8,128)(4,1)}, pred[16,16]{1,0:T(8,128)(4,1)S(1)}, u32[]{:S(2)}) copy-start(pred[16,16]{1,0:T(8,128)(4,1)S(1)} %get-tuple-element.419) | copy-start | bytes 772
  21.0 27.4 %copy-start.4 = (pred[16,16]{1,0:T(8,128)(4,1)}, pred[16,16]{1,0:T(8,128)(4,1)S(1)}, u32[]{:S(2)}) copy-start(pred[16,16]{1,0:T(8,128)(4,1)S(1)} %get-tuple-element.424) | copy-start | bytes 772
  24.0 96.6 %all-to-all-start = ((bf16[4,2,2,16,1024]{4,3,2,1,0:T(8,128)(2,1)}), bf16[4,2,2,16,1024]{4,3,2,1,0:T(8,128)(2,1)}, u32[]{:S(2)}, u32[]{:S(2)}) async-start(bf16[4,2,2,16,1024]{4,3,2,1,0:T(8,128)(2,1)} %broadcast_select_fusion.2), calls=%async_computation | async-start | bytes 1048576 | tf_op jit(solution)/shard_map/all_to_all | solution.py:180
  93.2 27.0 %copy-start.10 = (pred[4]{0:T(512)(128)(4,1)S(1)}, pred[4]{0:T(512)(128)(4,1)}, u32[]{:S(2)}) copy-start(pred[4]{0:T(512)(128)(4,1)} %fusion.54) | copy-start | bytes 16
  93.2 27.2 %copy-start.6 = (s32[2,4]{1,0:T(2,128)S(1)}, s32[2,4]{1,0:T(2,128)}, u32[]{:S(2)}) copy-start(s32[2,4]{1,0:T(2,128)} %copy-done.5) | copy-start | bytes 100
  93.2 27.2 %copy-start.9 = (pred[4]{0:T(512)(128)(4,1)S(1)}, pred[4]{0:T(512)(128)(4,1)}, u32[]{:S(2)}) copy-start(pred[4]{0:T(512)(128)(4,1)} %copy-done.8) | copy-start | bytes 16
  123.2 1.0 copy-start.1
where the time goes:
time: 125 us; the launch traced here: 124 us
  blocking collectives  53.9 us (43%)
  matrix products  33.4 us (27%)
  local copies, waits for them, and re-layouts  17.9 us (14%)
  other arithmetic  12.7 us (10%)
  starting transfers between devices  5.05 us (4%)
    all_gather x6, blocking collectives, merged(): everything = jax.tree.map(lambda part: lax.all_gather(part, axis), x)  41.2 us
    dot_general x2, matrix products, project(): jnp.dot(mixed, w_out, preferred_element_type=jnp.float32)  26.9 us
    all_gather x2, blocking collectives, gather_rows(): return lax.all_gather(token_rows, 'tp', axis=1, tiled=True)  12.7 us
    all_to_all x1, starting transfers between devices, local(): lax.all_to_all(outgoing, 'inst', split_axis=0, concat_axis=0, tiled=True)  5.05 us
    unnamed x30, local copies, waits for them, and re-layouts  3.69 us
  transfers between devices with their start and end apart: 1, of which 0 were waited for; matrix products, arithmetic and copies ran while one was open for 40% of the time, Pallas kernels for 0%

commit v1 on v0

v1 whole, which is shorter than its diff:
```python
import functools
import math

import jax
import jax.numpy as jnp
from jax import lax
from jax.experimental import pallas as pl
from jax.experimental.pallas import tpu as pltpu
from jax.sharding import PartitionSpec as P

HEAD_SIZE = 128
LANES = 128
NEG_LARGE = -1e30
BF16 = jnp.bfloat16
F32 = jnp.float32
I32 = jnp.int32
VMEM = pltpu.VMEM
HBM = pltpu.HBM
TILE = 256
PARTS = 2
CHUNKS = 8
copy_of = pltpu.make_async_copy


def spec(space):
    return pl.BlockSpec(memory_space=space)


def in_hbm(x):
    return pltpu.with_memory_space_constraint(x, HBM)


def shape(dims, dtype=BF16):
    return jax.ShapeDtypeStruct(dims, dtype)


def run(kernel, name, micros, ins, outs, scratch, args, aliases=None, after=(), limit=8):
    count = len(ins)

    def body(*refs):
        kernel(*refs[:count], *refs[count + len(after) :])

    ins = list(ins) + [pl.ANY] * len(after)
    args = list(args) + list(after)
    return pl.pallas_call(
        body,
        out_shape=tuple(s for s, _ in outs),
        in_specs=[spec(space) for space in ins],
        out_specs=tuple(spec(space) for _, space in outs),
        scratch_shapes=scratch,
        input_output_aliases=aliases or {},
        compiler_params=pltpu.CompilerParams(vmem_limit_bytes=limit << 20),
        cost_estimate=pl.CostEstimate(
            flops=int(micros * 3e8), bytes_accessed=0, transcendentals=0
        ),
        name=name,
    )(*args)


def behind(x, token):
    return lax.optimization_barrier((x, token))[0]


def rounded_up(x, to):
    return -(-x // to) * to


class Sizes:
    def __init__(self, n, inst_count, rows_of, per_rank, kv_shape, w_shape):
        self.n = n
        self.inst_count = inst_count
        self.rows_of = rows_of
        self.per_rank = per_rank
        self.pool, _, self.extent, self.kv_width = kv_shape
        self.q_width, self.out_columns = w_shape
        self.q_heads = self.q_width // HEAD_SIZE
        self.kv_heads = self.kv_width // HEAD_SIZE
        self.group = self.q_heads // self.kv_heads
        self.step_rows = rounded_up(rows_of, 8)
        self.all_rows = 2 * self.step_rows
        self.positions = self.pool * self.extent
        self.part_groups = self.kv_heads // (2 * PARTS)
        self.part_heads = self.part_groups * self.group
        self.part_width = self.part_heads * HEAD_SIZE
        self.packed = self.part_width + LANES
        self.chunk_rows = self.q_width // CHUNKS
        self.at_offset = 2 * rows_of
        self.at_source = 4 * rows_of
        self.at_send = self.at_source + self.pool
        self.at_place = self.at_send + (inst_count - 1) * per_rank
        self.plan_rows = rounded_up(
            -(-(self.at_place + (inst_count - 1) * per_rank) // LANES), 8
        )


def w_chunk(w_hbm, k):
    rows = w_hbm.shape[0] // CHUNKS
    side = lax.rem(lax.axis_index("tp"), 2)
    half = side if k < CHUNKS // 2 else 1 - side
    start = half * (w_hbm.shape[0] // 2) + (k % (CHUNKS // 2)) * rows
    return w_hbm.at[pl.ds(pl.multiple_of(start, LANES), rows)]


def w_copies(w_hbm, chunks, refs, sems, first):
    return [copy_of(w_chunk(w_hbm, k), ref, sems.at[first + i]) for i, (k, ref) in enumerate(zip(chunks, refs))]


def prepare_kernel(z, chunks, *refs):
    w_hbm, kv_hbm, first_hbm, second_hbm, lengths_hbm, table_hbm, moves_hbm, dest_hbm = refs[:8]
    pages, first_ref, second_ref, visible_ref, plan_ref = refs[8:13]
    w_refs = refs[13 : 13 + len(chunks)]
    lengths, table, moves, dest, plan, sems = refs[13 + len(chunks) :]
    me = lax.axis_index("tp")
    inst = lax.axis_index("inst")
    small = [
        copy_of(lengths_hbm, lengths, sems.at[0]),
        copy_of(table_hbm, table, sems.at[1]),
        copy_of(moves_hbm, moves, sems.at[2]),
        copy_of(dest_hbm, dest, sems.at[3]),
    ]
    large = [
        copy_of(kv_hbm, pages.at[pl.ds(0, z.pool)], sems.at[4]),
        copy_of(first_hbm, first_ref, sems.at[5]),
        copy_of(second_hbm, second_ref, sems.at[6]),
    ] + w_copies(w_hbm, chunks, w_refs, sems, 7)
    for copy in small + large:
        copy.start()
    pages[z.pool] = jnp.zeros_like(pages[z.pool])
    for copy in small:
        copy.wait()

    grid = (z.all_rows, z.positions)
    at = lax.broadcasted_iota(I32, grid, 1)
    row = lax.broadcasted_iota(I32, grid, 0)
    step = lax.div(row, z.step_rows)
    row_of = row - step * z.step_rows
    page_of = lax.div(at, z.extent)
    offset = at - page_of * z.extent
    newest = jnp.full(grid, -1, I32)
    place = jnp.full(grid, 1 << 30, I32)
    for r in range(z.rows_of):
        here = row_of == r
        newest = jnp.where(here, lengths[inst * z.rows_of + r], newest)
        for j in range(z.per_rank):
            number = me + z.n * j
            local = table[r, number] - me * z.pool
            place = jnp.where(here & (page_of == local), number * z.extent + offset, place)
    visible_ref[...] = (place <= newest + step).astype(I32)

    for k in range(2):
        for r in range(z.rows_of):
            position = lengths[inst * z.rows_of + r] + k
            local = table[r, lax.div(position, z.extent)] - me * z.pool
            mine = (local >= 0) & (local < z.pool)
            plan[k * z.rows_of + r] = jnp.where(mine, local, z.pool + 1)
            plan[z.at_offset + k * z.rows_of + r] = lax.rem(position, z.extent)
    for p in range(z.pool):
        plan[z.at_source + p] = p
    for k in range(2 * (z.inst_count - 1) * z.per_rank):
        plan[z.at_send + k] = -1
    for i in range(moves.shape[1]):
        request = moves[0, i]
        target = moves[1, i]
        origin = lax.div(request, z.rows_of)
        shift = lax.rem(target - origin + z.inst_count, z.inst_count)

        @pl.when((origin == inst) & (shift > 0))
        def _():
            for j in range(z.per_rank):
                local = table[request - inst * z.rows_of, me + z.n * j] - me * z.pool
                plan[z.at_source + local] = z.pool
                plan[z.at_send + (shift - 1) * z.per_rank + j] = local

        @pl.when((target == inst) & (shift > 0))
        def _():
            for j in range(z.per_rank):
                plan[z.at_place + (shift - 1) * z.per_rank + j] = dest[i, me + z.n * j] - me * z.pool

    where = lax.broadcasted_iota(I32, plan_ref.shape, 0) * LANES + lax.broadcasted_iota(
        I32, plan_ref.shape, 1
    )
    packed = jnp.zeros(plan_ref.shape, I32)
    for k in range(z.at_place + (z.inst_count - 1) * z.per_rank):
        packed = jnp.where(where == k, plan[k], packed)
    plan_ref[...] = packed
    for copy in large:
        copy.wait()


def read(plan, k):
    return plan[k // LANES, k % LANES]


def attend_part(z, part, rows, pages, visible, send_ref, keep_ref, stats_ref):
    side = lax.rem(lax.axis_index("tp"), 2)
    half = z.kv_heads // 2
    lane = lax.broadcasted_iota(I32, (z.all_rows, LANES), 1)
    scale = 1.0 / math.sqrt(HEAD_SIZE)
    stats = [jnp.zeros((z.all_rows, LANES), F32) for _ in range(2)]
    for i in range(2 * z.part_groups):
        kept, k = divmod(i, z.part_groups)
        g = (side if kept else 1 - side) * half + part * z.part_groups + k
        q = jnp.concatenate(
            [
                rows[:, pl.ds(pl.multiple_of((g * z.group + h) * HEAD_SIZE, LANES), HEAD_SIZE)]
                for h in range(z.group)
            ],
            axis=0,
        )
        columns = pl.ds(pl.multiple_of(g * HEAD_SIZE, LANES), HEAD_SIZE)
        keys = pages[0 : z.pool, 0, :, columns].reshape(z.positions, HEAD_SIZE)
        values = pages[0 : z.pool, 1, :, columns].reshape(z.positions, HEAD_SIZE)
        scores = lax.dot_general(q, keys, (((1,), (1,)), ((), ())), preferred_element_type=F32)
        scores = (scores * scale).reshape(z.group, z.all_rows, z.positions)
        scores = jnp.where(visible, scores, NEG_LARGE)
        top = jnp.max(scores, axis=2, keepdims=True)
        exponent = jnp.where(visible, jnp.exp(scores - top), 0.0)
        total = jnp.sum(exponent, axis=2, keepdims=True)
        summed = jnp.dot(
            exponent.astype(BF16).reshape(z.group * z.all_rows, z.positions),
            values,
            preferred_element_type=F32,
        )
        for h in range(z.group):
            head = k * z.group + h
            piece = summed[h * z.all_rows : (h + 1) * z.all_rows]
            out_columns = slice(head * HEAD_SIZE, (head + 1) * HEAD_SIZE)
            if kept:
                keep_ref[:, out_columns] = piece
            else:
                send_ref[:, out_columns] = piece.astype(BF16)
            stats[kept] = jnp.where(lane == head, top[h], stats[kept])
            stats[kept] = jnp.where(lane == z.part_heads + head, total[h], stats[kept])
    put_stats(z, send_ref, stats[0])
    stats_ref[...] = stats[1]


def put_stats(z, ref, stats):
    used = 2 * z.part_heads
    lane = lax.broadcasted_iota(I32, stats.shape, 1)
    high = stats.astype(BF16).astype(F32)
    rest = stats - high
    middle = rest.astype(BF16).astype(F32)
    low = rest - middle
    pieces = jnp.where(
        lane < used,
        high,
        jnp.where(lane < 2 * used, pltpu.roll(middle, used, 1), pltpu.roll(low, 2 * used, 1)),
    )
    ref[:, z.part_width :] = pieces.astype(BF16)


def get_stats(z, ref):
    used = 2 * z.part_heads
    pieces = ref[:, z.part_width :].astype(F32)
    lane = lax.broadcasted_iota(I32, pieces.shape, 1)
    stats = (
        pieces
        + pltpu.roll(pieces, LANES - used, 1)
        + pltpu.roll(pieces, LANES - 2 * used, 1)
    )
    return jnp.where(lane < used, stats, 0.0)


def attend_first_kernel(z, chunks, *refs):
    m = 2 * z.n
    w_hbm, plan_vmem, visible_ref, pages_in = refs[:4]
    pieces = refs[4 : 4 + m]
    send_ref, keep_ref, stats_ref, rows, pages, kv_out = refs[4 + m : 10 + m]
    outgoing = refs[10 + m : 9 + m + z.inst_count]
    w_refs = refs[9 + m + z.inst_count : 9 + m + z.inst_count + len(chunks)]
    plan, sems = refs[9 + m + z.inst_count + len(chunks) :]
    me = lax.axis_index("tp")
    width = pieces[0].shape[1]
    plan_copy = copy_of(plan_vmem, plan, sems.at[0])
    plan_copy.start()
    w_loads = w_copies(w_hbm, chunks, w_refs, sems, 3)
    for copy in w_loads:
        copy.start()
    rows[...] = jnp.zeros_like(rows)
    for d in range(z.n):
        start = pl.multiple_of((me ^ d) * width, LANES)
        for k in range(2):
            rows[k * z.step_rows : k * z.step_rows + z.rows_of, pl.ds(start, width)] = pieces[
                2 * d + k
            ][...]
    plan_copy.wait()

    fresh = rows[:, z.q_width :].astype(F32)
    row_id = lax.broadcasted_iota(I32, (z.extent, z.kv_width), 0)
    for k in range(2):
        for r in range(z.rows_of):
            slot = read(plan, k * z.rows_of + r)
            here = row_id == read(plan, z.at_offset + k * z.rows_of + r)
            line = k * z.step_rows + r
            for kv in range(2):
                new = fresh[line : line + 1, kv * z.kv_width : (kv + 1) * z.kv_width]
                old = pages[slot, kv].astype(F32)
                pages[slot, kv] = jnp.where(here, new, old).astype(BF16)

    def sends(act):
        for s in range(z.inst_count - 1):
            for j in range(z.per_rank):
                slot = read(plan, z.at_send + s * z.per_rank + j)

                @pl.when(slot >= 0)
                def _():
                    act(copy_of(pages.at[slot], outgoing[s].at[j], sems.at[1]))

    sends(lambda copy: copy.start())
    writes = [
        copy_of(pages.at[read(plan, z.at_source + p)], kv_out.at[p], sems.at[2])
        for p in range(z.pool)
    ]
    for copy in writes:
        copy.start()
    visible = (visible_ref[...] > 0)[None]
    attend_part(z, 0, rows, pages, visible, send_ref, keep_ref, stats_ref)
    sends(lambda copy: copy.wait())
    for copy in writes + w_loads:
        copy.wait()


def attend_more_kernel(z, part, chunks, *refs):
    w_hbm, visible_ref, rows, pages, send_ref, keep_ref, stats_ref = refs[:7]
    w_refs = refs[7 : 7 + len(chunks)]
    (sems,) = refs[7 + len(chunks) :]
    w_loads = w_copies(w_hbm, chunks, w_refs, sems, 0)
    for copy in w_loads:
        copy.start()
    visible = (visible_ref[...] > 0)[None]
    attend_part(z, part, rows, pages, visible, send_ref, keep_ref, stats_ref)
    for copy in w_loads:
        copy.wait()


def joined(z, acc_ref, stats_ref, other_ref):
    mine = stats_ref[...]
    theirs = get_stats(z, other_ref)
    lane = lax.broadcasted_iota(I32, mine.shape, 1)
    top = jnp.maximum(mine, theirs)
    scale_mine = jnp.exp(mine - top)
    scale_theirs = jnp.exp(theirs - top)
    total = mine * pltpu.roll(scale_mine, z.part_heads, 1) + theirs * pltpu.roll(
        scale_theirs, z.part_heads, 1
    )
    stats = jnp.where(
        lane < z.part_heads, top, jnp.where(lane < 2 * z.part_heads, total, 0.0)
    )
    for h in range(z.part_heads):
        columns = slice(h * HEAD_SIZE, (h + 1) * HEAD_SIZE)
        piece = acc_ref[:, columns] * scale_mine[:, h : h + 1] + other_ref[:, columns].astype(
            F32
        ) * scale_theirs[:, h : h + 1]
        yield columns, piece, stats, h


def merge_kernel(z, acc_ref, stats_ref, other_ref, acc_out, stats_out, send_ref):
    for columns, piece, stats, _ in joined(z, acc_ref, stats_ref, other_ref):
        acc_out[:, columns] = piece
        send_ref[:, columns] = piece.astype(BF16)
    stats_out[...] = stats
    put_stats(z, send_ref, stats)


def finish_kernel(z, acc_ref, stats_ref, other_ref, mixed_ref):
    for columns, piece, stats, h in joined(z, acc_ref, stats_ref, other_ref):
        total = stats[:, z.part_heads + h : z.part_heads + h + 1]
        mixed_ref[:, columns] = (piece / total).astype(BF16)


def stage_kernel(chunks, w_hbm, *refs):
    loads = w_copies(w_hbm, chunks, refs[: len(chunks)], refs[-1], 0)
    for copy in loads:
        copy.start()
    for copy in loads:
        copy.wait()


def product(mixed, w_refs, columns):
    rows = w_refs[0].shape[0]
    total = None
    for i, w in enumerate(w_refs):
        part = jnp.dot(
            mixed[:, i * rows : (i + 1) * rows], w[:, columns], preferred_element_type=F32
        )
        total = part if total is None else total + part
    return total


def column_tiles(width, body):
    @pl.loop(0, width // TILE)
    def _(t):
        body(pl.ds(pl.multiple_of(t * TILE, TILE), TILE))


def project_kernel(z, used, chunks, has_acc, *refs):
    w_hbm, mixed = refs[:2]
    w_used = refs[2 : 2 + used]
    acc_in = refs[2 + used] if has_acc else None
    acc_ref = refs[2 + used + has_acc]
    w_refs = refs[3 + used + has_acc : -1]
    loads = w_copies(w_hbm, chunks, w_refs, refs[-1], 0)
    for copy in loads:
        copy.start()

    def body(columns):
        total = product(mixed, w_used, columns)
        if has_acc:
            total += acc_in[:, columns]
        acc_ref[:, columns] = total

    column_tiles(z.out_columns, body)
    for copy in loads:
        copy.wait()


def last_kernel(z, held, chunks, *refs):
    w_hbm, acc_in = refs[:2]
    mixed = refs[2 : 2 + PARTS]
    w_held = refs[2 + PARTS : 2 + PARTS + held]
    first_ref, second_ref, token, w_late, acc, sems = refs[2 + PARTS + held :]
    token[...] = jnp.zeros_like(token)
    loads = w_copies(w_hbm, chunks, [w_late.at[i] for i in range(len(chunks))], sems, 0)
    for copy in loads:
        copy.start()
    per_part = CHUNKS // (2 * PARTS)
    rows = z.chunk_rows

    def mixed_of(k):
        return mixed[k // per_part][:, (k % per_part) * rows : (k % per_part + 1) * rows]

    def early(columns):
        total = acc_in[:, columns]
        for k in range(held):
            total += jnp.dot(mixed_of(k), w_held[k][:, columns], preferred_element_type=F32)
        acc[:, columns] = total

    column_tiles(z.out_columns, early)
    for copy in loads:
        copy.wait()

    def late(columns):
        total = acc[:, columns]
        for i in range(len(chunks)):
            total += jnp.dot(
                mixed_of(held + i), w_late[i, :, columns], preferred_element_type=F32
            )
        first_ref[:, columns] = total[: z.rows_of].astype(BF16)
        second_ref[:, columns] = total[z.step_rows : z.step_rows + z.rows_of].astype(BF16)

    column_tiles(z.out_columns, late)


def place_kernel(z, *refs):
    plan_vmem = refs[0]
    arrived = refs[1 : z.inst_count]
    kv_out, plan, sems = refs[1 + z.inst_count :]
    plan_copy = copy_of(plan_vmem, plan, sems.at[0])
    plan_copy.start()
    plan_copy.wait()

    def each(act):
        for s in range(z.inst_count - 1):
            for j in range(z.per_rank):
                slot = read(plan, z.at_place + s * z.per_rank + j)

                @pl.when(slot >= 0)
                def _():
                    act(copy_of(arrived[s].at[j], kv_out.at[slot], sems.at[1]))

    each(lambda copy: copy.start())
    each(lambda copy: copy.wait())


def local(qkv_first, qkv_second, w_out, kv_cache, lengths, page_table, moves, dest_pages):
    n = lax.axis_size("tp")
    inst_count = lax.axis_size("inst")
    moves = moves.T
    rows_of, max_pages = page_table.shape
    z = Sizes(n, inst_count, rows_of, max_pages // n, kv_cache.shape, w_out.shape)
    smem = pltpu.SMEM
    dma = pltpu.SemaphoreType.DMA
    w_hbm = in_hbm(w_out)
    chunk = (shape((z.chunk_rows, z.out_columns)), VMEM)
    page = kv_cache.shape[1:]

    def swap(x, d):
        return lax.ppermute(x, "tp", [(i, i ^ d) for i in range(n)])

    stages = []
    while (1 << len(stages)) < n:
        stages.append(1 << len(stages))

    w = {}
    took = (0,)
    pages, own_first, own_second, visible, plan, *loaded = run(
        functools.partial(prepare_kernel, z, took),
        "prepare",
        2,
        [HBM] * 8,
        [
            (shape((z.pool + 2,) + page), VMEM),
            (shape(qkv_first.shape), VMEM),
            (shape(qkv_second.shape), VMEM),
            (shape((z.all_rows, z.positions), I32), VMEM),
            (shape((z.plan_rows, LANES), I32), VMEM),
        ]
        + [chunk] * len(took),
        [
            smem(lengths.shape, I32),
            smem(page_table.shape, I32),
            smem(moves.shape, I32),
            smem(dest_pages.shape, I32),
            smem((z.plan_rows * LANES,), I32),
            dma((7 + len(took),)),
        ],
        [w_hbm]
        + [
            in_hbm(x)
            for x in (kv_cache, qkv_first, qkv_second, lengths, page_table, moves, dest_pages)
        ],
    )
    w.update(zip(took, loaded))

    have = {0: (qkv_first, qkv_second)}
    for d in stages[1:] + stages[:1]:
        for e, pair in list(have.items()):
            if d == 1 and e:
                pair = tuple(behind(x, plan) for x in pair)
            have[e ^ d] = tuple(swap(x, d) for x in pair)
    have[0] = (own_first, own_second)
    pieces = [x for d in range(n) for x in have[d]]

    took = (1, 2)
    partial_out = [
        (shape((z.all_rows, z.packed)), VMEM),
        (shape((z.all_rows, z.part_width), F32), VMEM),
        (shape((z.all_rows, LANES), F32), VMEM),
    ]
    send, acc, stats = [None] * PARTS, [None] * PARTS, [None] * PARTS
    results = run(
        functools.partial(attend_first_kernel, z, took),
        "attend0",
        2,
        [HBM] + [VMEM] * (3 + 2 * n),
        partial_out
        + [
            (shape((z.all_rows, z.q_width + 2 * z.kv_width)), VMEM),
            (shape(pages.shape), VMEM),
            (shape(kv_cache.shape), HBM),
        ]
        + [(shape((z.per_rank,) + page), VMEM)] * (inst_count - 1)
        + [chunk] * len(took),
        [smem((z.plan_rows, LANES), I32), dma((3 + len(took),))],
        [w_hbm, plan, visible, pages, *pieces],
        aliases={3: 4},
    )
    send[0], acc[0], stats[0], rows, pages, kv_mid = results[:6]
    outgoing = results[6 : 5 + inst_count]
    w.update(zip(took, results[5 + inst_count :]))

    theirs = [None] * PARTS
    theirs[0] = swap(send[0], 1)
    took = (3,)
    for part in range(1, PARTS):
        send[part], acc[part], stats[part], *loaded = run(
            functools.partial(attend_more_kernel, z, part, took),
            f"attend{part}",
            1.5,
            [HBM] + [VMEM] * 3,
            partial_out + [chunk] * len(took),
            [dma((len(took),))],
            [w_hbm, visible, rows, pages],
        )
        w.update(zip(took, loaded))
        theirs[part] = swap(send[part], 1)

    for d in stages[1:]:
        for part in range(PARTS):
            acc[part], stats[part], send[part] = run(
                functools.partial(merge_kernel, z),
                f"merge{d}_{part}",
                0.2,
                [VMEM] * 3,
                [partial_out[1], partial_out[2], partial_out[0]],
                [],
                [acc[part], stats[part], theirs[part]],
            )
            theirs[part] = swap(send[part], d)

    outgoing = [behind(x, stats[PARTS - 1]) for x in outgoing]
    arrived = [
        lax.ppermute(
            outgoing[s - 1], "inst", [(i, (i + s) % inst_count) for i in range(inst_count)]
        )
        for s in range(1, inst_count)
    ]
    took = (4,)
    w.update(
        zip(
            took,
            run(
                functools.partial(stage_kernel, took),
                "stage",
                1.5,
                [HBM],
                [chunk] * len(took),
                [dma((len(took),))],
                [w_hbm],
                after=[stats[PARTS - 1]],
            ),
        )
    )

    total = None
    mixed, others = [], []
    per_part = CHUNKS // (2 * PARTS)
    for part in range(PARTS):
        (ready,) = run(
            functools.partial(finish_kernel, z),
            f"finish{part}",
            0.3,
            [VMEM] * 3,
            [(shape((z.all_rows, z.part_width)), VMEM)],
            [],
            [acc[part], stats[part], theirs[part]],
            after=[] if total is None else [total],
        )
        others.append(swap(ready, 1))
        took = (5 + part,)
        weights = [w[part * per_part + k] for k in range(per_part)]
        before = [] if total is None else [total]
        total, *loaded = run(
            functools.partial(project_kernel, z, per_part, took, len(before)),
            f"project{part}",
            1.6,
            [HBM] + [VMEM] * (1 + per_part + len(before)),
            [(shape((z.all_rows, z.out_columns), F32), VMEM)] + [chunk] * len(took),
            [dma((len(took),))],
            [w_hbm, ready, *weights, *before],
        )
        w.update(zip(took, loaded))

    held = [w[k] for k in range(CHUNKS // 2, CHUNKS) if k in w]
    late = tuple(range(CHUNKS // 2 + len(held), CHUNKS))
    out_first, out_second, token = run(
        functools.partial(last_kernel, z, len(held), late),
        "last",
        3,
        [HBM] + [VMEM] * (1 + PARTS + len(held)),
        [(shape((rows_of, z.out_columns)), VMEM)] * 2 + [(shape((8, LANES), I32), VMEM)],
        [
            pltpu.VMEM((max(len(late), 1), z.chunk_rows, z.out_columns), BF16),
            pltpu.VMEM((z.all_rows, z.out_columns), F32),
            dma((max(len(late), 1),)),
        ],
        [w_hbm, total, *others, *held],
    )
    (kv_out,) = run(
        functools.partial(place_kernel, z),
        "place",
        1,
        [VMEM] * inst_count + [HBM],
        [(shape(kv_cache.shape), HBM)],
        [smem((z.plan_rows, LANES), I32), dma((2,))],
        [plan, *arrived, kv_mid],
        aliases={inst_count: 0},
        after=[token],
    )
    return out_first, out_second, kv_out


def solution(mesh):
    placed = (
        P(("groups", "inst"), "tp"),
        P(("groups", "inst"), "tp"),
        P(None, "tp"),
        P(("groups", "inst", "tp"), None, None, None),
        P("groups"),
        P(("groups", "inst"), None),
        P("groups", None),
        P("groups", None),
    )
    return jax.shard_map(
        local,
        mesh=mesh,
        in_specs=placed,
        out_specs=(
            P(("groups", "inst"), "tp"),
            P(("groups", "inst"), "tp"),
            P(("groups", "inst", "tp"), None, None, None),
        ),
        check_vma=False,
    )
```

time: 125 us -> 38.3 us (0.31)
  blocking collectives: 53.9 us -> 0 us
  matrix products: 33.4 us -> 0 us
  Pallas kernels: 0 us -> 22.3 us
  local copies, waits for them, and re-layouts: 17.9 us -> 0 us
  other arithmetic: 12.7 us -> 0 us
  starting transfers between devices: 5.05 us -> 13 us
  waiting for transfers between devices: 0.01 us -> 1.97 us
    all_gather x8 -> x0, blocking collectives: 53.9 us -> none  [the longest x6 41.2 us: merged(): everything = jax.tree.map(lambda part: lax.all_gather(part, axis), x)]
    dot_general x14 -> x0, matrix products: 33.4 us -> none  [the longest x2 26.9 us: project(): jnp.dot(mixed, w_out, preferred_element_type=jnp.float32)]
    pallas_call x0 -> x12, Pallas kernels: none -> 22.3 us  [run(): pl.pallas_call(body, out_shape=tuple((s for s, _ in outs)), in_specs=[spe...]
    ppermute x0 -> x15, starting transfers between devices: none -> 13 us  [the longest x12 7.5 us: swap(): return lax.ppermute(x, 'tp', [(i, i ^ d) for i in range(n)])]
    all_to_all x1 -> x0, starting transfers between devices: 5.05 us -> none  [local(): lax.all_to_all(outgoing, 'inst', split_axis=0, concat_axis=0, tiled=True)]
    gather x7 -> x0, local copies, waits for them, and re-layouts: 4.35 us -> none  [the longest x3 1.89 us: local(): page_table[send_rows][:, rank_cols] - tp_rank * shared_pages]
    select_n x14 -> x0, other arithmetic: 3.82 us -> none  [the longest x1 1.47 us: write_tokens(): return jnp.where(page_hit[:, None, :, None], placed, paged_memory)]
    unnamed x30 -> x0, local copies, waits for them, and re-layouts: 3.69 us -> none
  transfers between devices with their start and end apart: 1 -> 15, of which waited for: 0 -> 3; matrix products, arithmetic and copies ran while one was open for 40% -> 0% of each run, Pallas kernels for 0% -> 46%
where the time goes in v1:
time: 38.3 us; the launch traced here: 38.1 us
  Pallas kernels  22.3 us (58%)
  starting transfers between devices  13 us (34%)
  waiting for transfers between devices  1.97 us (5%)
  between operations  0.78 us (2%)
    pallas_call x12, Pallas kernels, run(): pl.pallas_call(body, out_shape=tuple((s for s, _ in outs)), in_specs=[spe...  22.3 us
    ppermute x12, starting transfers between devices, swap(): return lax.ppermute(x, 'tp', [(i, i ^ d) for i in range(n)])  7.5 us
    ppermute x3, starting transfers between devices, local(): lax.ppermute(outgoing[s - 1], 'inst', [(i, (i + s) % inst_count) for i in...  5.51 us
    ppermute x12, waiting for transfers between devices, swap(): return lax.ppermute(x, 'tp', [(i, i ^ d) for i in range(n)])  1.96 us
  transfers between devices with their start and end apart: 15, of which 3 were waited for; matrix products, arithmetic and copies ran while one was open for 0% of the time, Pallas kernels for 46%

profile of v1, /device:TPU:0, one launch (start us, length us, event | category | flops | bytes accessed | tf_op | source)
XLA Modules:
  0.0 38.1 jit_solution(15682032381623045259)
XLA Ops:
  0.6 3.1 %collective-permute-start.2 = (bf16[6,2560]{1,0:T(8,128)(2,1)}, bf16[6,2560]{1,0:T(8,128)(2,1)S(1)}, u32[]{:S(2)}, u32[]{:S(2)}) collective-permute-start(bf16[6,2560]{1,0:T(8,128)(2,1)} %refs_2_.1), channel_id=1, source_target_pairs={{0,2},{1,3},{2,0},{3,1},{4,6},{5,7},{6,4},{7,5},{8,10},{9,11},{10,... | collective-permute-start | bytes 92168 | tf_op jit(solution)/shard_map/ppermute | solution.py:489
  3.7 0.0 collective-permute-start
  3.7 0.2 collective-permute-start.3
  3.9 0.4 collective-permute-start.1
  4.2 2.6 %prepare.1 = (bf16[18,2,16,1024]{3,2,1,0:T(8,128)(2,1)S(1)}, bf16[6,2560]{1,0:T(8,128)(2,1)S(1)}, bf16[6,2560]{1,0:T(8,128)(2,1)S(1)}, s32[16,256]{1,0:T(8,128)S...) custom-call(bf16[8192,2048]{1,0:T(8,128)(2,1)} %refs_0_.13, bf16[16,2,16,1024]{3,2,1,0:T(8,128)(2,1)} %refs_1_.1, ...), custom_call_target="tpu_custom_call" | custom-call | flops 600000000 | tf_op jit(solution)/shard_map/prepare/pallas_call | solution.py:45
  6.8 1.1 %collective-permute-done.3.refs_9_ = bf16[6,2560]{1,0:T(8,128)(2,1)S(1)} collective-permute-done((bf16[6,2560]{1,0:T(8,128)(2,1)}, bf16[6,2560]{1,0:T(8,128)(2,1)S(1)}, u32[]{:S(2)}, u32[]{:S(2)}) %collective-permute-start.3) | collective-permute-done | bytes 30752 | tf_op jit(solution)/shard_map/ppermute | solution.py:489
  7.9 0.0 collective-permute-done.2.refs_8_
  7.9 0.0 collective-permute-start.4
  7.9 0.5 %collective-permute-start.5 = (bf16[6,2560]{1,0:T(8,128)(2,1)S(1)}, bf16[6,2560]{1,0:T(8,128)(2,1)S(1)}, u32[]{:S(2)}, u32[]{:S(2)}) collective-permute-start(bf16[6,2560]{1,0:T(8,128)(2,1)S(1)} %collective-permute-done.3.refs_9_), channel_id=1, source_target_pairs={{0,1},{1,0},{2,3},{3,2},{4,5},{5,4},{6,7},{7,6},{8,9},{9,8},{10,11... | collective-permute-start | bytes 92168 | tf_op jit(solution)/shard_map/ppermute | solution.py:489
  8.4 0.0 collective-permute-done.refs_6_
  8.4 0.0 collective-permute-done.1.refs_7_
  8.4 0.7 %collective-permute-done.4.refs_10_ = bf16[6,2560]{1,0:T(8,128)(2,1)S(1)} collective-permute-done((bf16[6,2560]{1,0:T(8,128)(2,1)S(1)}, bf16[6,2560]{1,0:T(8,128)(2,1)S(1)}, u32[]{:S(2)}, u32[]{:S(2)}) %collective-permute-start.4) | collective-permute-done | bytes 30752 | tf_op jit(solution)/shard_map/ppermute | solution.py:489
  9.1 0.2 collective-permute-done.5.refs_11_
  9.3 3.9 %attend0.1 = (bf16[16,2176]{1,0:T(8,128)(2,1)S(1)}, f32[16,2048]{1,0:T(8,128)S(1)}, f32[16,128]{1,0:T(8,128)S(1)}, bf16[16,10240]{1,0:T(8,128)(2,1)S(1)}, bf16[1...) custom-call(bf16[8192,2048]{1,0:T(8,128)(2,1)} %refs_0_.13, ...), custom_call_target="tpu_custom_call", output_to_operand_aliasing={{4}: (3, {})} | custom-call | flops 600000000 | tf_op jit(solution)/shard_map/attend0/pallas_call | solution.py:45
  13.2 0.4 %collective-permute-start.8 = (bf16[16,2176]{1,0:T(8,128)(2,1)S(1)}, bf16[16,2176]{1,0:T(8,128)(2,1)S(1)}, u32[]{:S(2)}, u32[]{:S(2)}) collective-permute-start(bf16[16,2176]{1,0:T(8,128)(2,1)S(1)} %get-tuple-element.59), channel_id=1, source_target_pairs={{0,1},{1,0},{2,3},{3,2},{4,5},{5,4},{6,7},{7,6},{8,9},{9,8},{10,11... | collective-permute-start | bytes 208904 | tf_op jit(solution)/shard_map/ppermute | solution.py:489
  13.6 2.5 %attend1.1 = (bf16[16,2176]{1,0:T(8,128)(2,1)S(1)}, f32[16,2048]{1,0:T(8,128)S(1)}, f32[16,128]{1,0:T(8,128)S(1)}, bf16[1024,2048]{1,0:T(8,128)(2,1)S(1)}) custom-call(bf16[8192,2048]{1,0:T(8,128)(2,1)} %refs_0_.13, s32[16,256]{1,0:T(8,128)S(1)} %get-tuple-element.42.refs_2_.refs_1_, bf16[16,10240]{1,0:T(8,128)(2,1)S(1)} %get-tuple-element.49.refs_2_, ...), custom_call_target="tpu_custom_call" | custom-call | flops 450000000 | tf_op jit(solution)/shard_map/attend1/pallas_call | solution.py:45
  16.2 0.2 collective-permute-start.6
  16.4 0.0 collective-permute-done.8.refs_2_
  16.4 0.2 merge2_0.1
  16.7 0.9 %collective-permute-start.9 = (bf16[16,2176]{1,0:T(8,128)(2,1)S(1)}, bf16[16,2176]{1,0:T(8,128)(2,1)S(1)}, u32[]{:S(2)}, u32[]{:S(2)}) collective-permute-start(bf16[16,2176]{1,0:T(8,128)(2,1)S(1)} %get-tuple-element.62), channel_id=1, source_target_pairs={{0,2},{1,3},{2,0},{3,1},{4,6},{5,7},{6,4},{7,5},{8,10},{9,11},{10,... | collective-permute-start | bytes 208904 | tf_op jit(solution)/shard_map/ppermute | solution.py:489
  17.6 0.0 collective-permute-done.6.refs_2_
  17.6 0.2 merge2_1.1
  17.9 1.2 %collective-permute-start.7 = (bf16[16,2176]{1,0:T(8,128)(2,1)S(1)}, bf16[16,2176]{1,0:T(8,128)(2,1)S(1)}, u32[]{:S(2)}, u32[]{:S(2)}) collective-permute-start(bf16[16,2176]{1,0:T(8,128)(2,1)S(1)} %get-tuple-element.56), channel_id=1, source_target_pairs={{0,2},{1,3},{2,0},{3,1},{4,6},{5,7},{6,4},{7,5},{8,10},{9,11},{10,... | collective-permute-start | bytes 208904 | tf_op jit(solution)/shard_map/ppermute | solution.py:489
  19.1 1.6 %collective-permute-start.12 = (bf16[2,2,16,1024]{3,2,1,0:T(8,128)(2,1)S(1)}, bf16[2,2,16,1024]{3,2,1,0:T(8,128)(2,1)S(1)}, u32[]{:S(2)}, u32[]{:S(2)}) collective-permute-start(bf16[2,2,16,1024]{3,2,1,0:T(8,128)(2,1)S(1)} %get-tuple-element.74), channel_id=1, source_target_pairs={{0,4},{4,8},{8,12},{12,0},{1,5},{5,9},{9,13},{13,1},{2,6},{6,10},{... | collective-permute-start | bytes 393224 | tf_op jit(solution)/shard_map/ppermute | solution.py:594
  20.7 2.6 %collective-permute-start.13 = (bf16[2,2,16,1024]{3,2,1,0:T(8,128)(2,1)S(1)}, bf16[2,2,16,1024]{3,2,1,0:T(8,128)(2,1)S(1)}, u32[]{:S(2)}, u32[]{:S(2)}) collective-permute-start(bf16[2,2,16,1024]{3,2,1,0:T(8,128)(2,1)S(1)} %get-tuple-element.76), channel_id=1, source_target_pairs={{0,8},{4,12},{8,0},{12,4},{1,9},{5,13},{9,1},{13,5},{2,10},{6,14},... | collective-permute-start | bytes 393224 | tf_op jit(solution)/shard_map/ppermute | solution.py:594
  23.2 1.3 %collective-permute-start.14 = (bf16[2,2,16,1024]{3,2,1,0:T(8,128)(2,1)S(1)}, bf16[2,2,16,1024]{3,2,1,0:T(8,128)(2,1)S(1)}, u32[]{:S(2)}, u32[]{:S(2)}) collective-permute-start(bf16[2,2,16,1024]{3,2,1,0:T(8,128)(2,1)S(1)} %get-tuple-element.78), channel_id=1, source_target_pairs={{0,12},{4,0},{8,4},{12,8},{1,13},{5,1},{9,5},{13,9},{2,14},{6,2},{... | collective-permute-start | bytes 393224 | tf_op jit(solution)/shard_map/ppermute | solution.py:594
  24.6 0.0 collective-permute-done.9.refs_2_
  24.6 0.3 finish0.1.refs_1_
  24.9 0.1 collective-permute-start.10
  25.0 2.2 %project0.1 = (f32[16,2048]{1,0:T(8,128)S(1)}, bf16[1024,2048]{1,0:T(8,128)(2,1)S(1)}) custom-call(bf16[8192,2048]{1,0:T(8,128)(2,1)} %refs_0_.13, bf16[16,2048]{1,0:T(8,128)(2,1)S(1)} %finish0.1.refs_1_, bf16[1024,2048]{1,0:T(8,128)(2,1)S(1)} %get-tuple-element.63.refs_2_, bf16[1024,2048]{1,0:T(8,128)(2,1)S(1)} %get-tuple-element.64.refs_3_), custom_call_target="tpu_custom_call" | custom-call | flops 480000000 | tf_op jit(solution)/shard_map/project0/pallas_call | solution.py:45
  27.2 0.0 collective-permute-done.7.refs_2_
  27.2 0.3 finish1.1.refs_1_
  27.5 0.5 %collective-permute-start.11 = (bf16[16,2048]{1,0:T(8,128)(2,1)S(1)}, bf16[16,2048]{1,0:T(8,128)(2,1)S(1)}, u32[]{:S(2)}, u32[]{:S(2)}) collective-permute-start(bf16[16,2048]{1,0:T(8,128)(2,1)S(1)} %finish1.1.refs_1_), channel_id=1, source_target_pairs={{0,1},{1,0},{2,3},{3,2},{4,5},{5,4},{6,7},{7,6},{8,9},{9,8},{10,11... | collective-permute-start | bytes 196616 | tf_op jit(solution)/shard_map/ppermute | solution.py:489
  28.1 2.2 %stage.1.refs_4_ = bf16[1024,2048]{1,0:T(8,128)(2,1)S(1)} custom-call(bf16[8192,2048]{1,0:T(8,128)(2,1)} %refs_0_.13, f32[16,128]{1,0:T(8,128)S(1)} %get-tuple-element.55.refs_1_), custom_call_target="tpu_custom_call" | custom-call | flops 450000000 | tf_op jit(solution)/shard_map/stage/pallas_call | solution.py:45
  30.3 2.2 %project1.1 = (f32[16,2048]{1,0:T(8,128)S(1)}, bf16[1024,2048]{1,0:T(8,128)(2,1)S(1)}) custom-call(bf16[8192,2048]{1,0:T(8,128)(2,1)} %refs_0_.13, bf16[16,2048]{1,0:T(8,128)(2,1)S(1)} %finish1.1.refs_1_, bf16[1024,2048]{1,0:T(8,128)(2,1)S(1)} %get-tuple-element.66.refs_2_, bf16[1024,2048]{1,0:T(8,128)(2,1)S(1)} %get-tuple-element.67.refs_3_, ...), custom_call_target="tpu_custom_call" | custom-call | flops 480000000 | tf_op jit(solution)/shard_map/project1/pallas_call | solution.py:45
  32.5 0.0 collective-permute-done.10.refs_2_
  32.5 0.0 collective-permute-done.11.refs_3_
  32.5 4.8 %last.1 = (bf16[6,2048]{1,0:T(8,128)(2,1)}, bf16[6,2048]{1,0:T(8,128)(2,1)}, s32[8,128]{1,0:T(8,128)S(1)}) custom-call(bf16[8192,2048]{1,0:T(8,128)(2,1)} %refs_0_.13, f32[16,2048]{1,0:T(8,128)S(1)} %get-tuple-element.68.refs_1_, bf16[16,2048]{1,0:T(8,128)(2,1)S(1)} %collective-permute-done.10.refs_2_, bf16[16,2048]{1,0:T(8,128)(2,1)S(1)} %collective-permute-done.11.refs_3_, ...), custom_call_target="tpu_custom_call" | custom-call | flops 900000000 | tf_op jit(solution)/shard_map/last/pallas_call | solution.py:45
  37.4 0.0 collective-permute-done.12.refs_1_
  37.4 0.0 collective-permute-done.13.refs_2_
  37.4 0.0 collective-permute-done.14.refs_3_
  37.4 0.7 %place.1 = bf16[16,2,16,1024]{3,2,1,0:T(8,128)(2,1)} custom-call(s32[8,128]{1,0:T(8,128)S(1)} %get-tuple-element.43.refs_1_.refs_0_, bf16[2,2,16,1024]{3,2,1,0:T(8,128)(2,1)S(1)} %collective-permute-done.12.refs_1_, bf16[2,2,16,1024]{3,2,1,0:T(8,128)(2,1)S(1)} %collective-permute-done.13.refs_2_, ...), custom_call_target="tpu_custom_call", output_to_operand_aliasing={{}: (4, {})} | custom-call | flops 300000000 | tf_op jit(solution)/shard_map/place/pallas_call | solution.py:45
Async XLA Ops:
  0.6 7.3 %collective-permute-start.2 = (bf16[6,2560]{1,0:T(8,128)(2,1)}, bf16[6,2560]{1,0:T(8,128)(2,1)S(1)}, u32[]{:S(2)}, u32[]{:S(2)}) collective-permute-start(bf16[6,2560]{1,0:T(8,128)(2,1)} %refs_2_.1), channel_id=1, source_target_pairs={{0,2},{1,3},{2,0},{3,1},{4,6},{5,7},{6,4},{7,5},{8,10},{9,11},{10,... | collective-permute-start | bytes 92168 | tf_op jit(solution)/shard_map/ppermute | solution.py:489
  3.7 4.7 %collective-permute-start = (bf16[6,2560]{1,0:T(8,128)(2,1)}, bf16[6,2560]{1,0:T(8,128)(2,1)S(1)}, u32[]{:S(2)}, u32[]{:S(2)}) collective-permute-start(bf16[6,2560]{1,0:T(8,128)(2,1)} %refs_2_.1), channel_id=1, source_target_pairs={{0,1},{1,0},{2,3},{3,2},{4,5},{5,4},{6,7},{7,6},{8,9},{9,8},{10,11... | collective-permute-start | bytes 92168 | tf_op jit(solution)/shard_map/ppermute | solution.py:489
  3.7 4.2 %collective-permute-start.3 = (bf16[6,2560]{1,0:T(8,128)(2,1)}, bf16[6,2560]{1,0:T(8,128)(2,1)S(1)}, u32[]{:S(2)}, u32[]{:S(2)}) collective-permute-start(bf16[6,2560]{1,0:T(8,128)(2,1)} %refs_3_.1), channel_id=1, source_target_pairs={{0,2},{1,3},{2,0},{3,1},{4,6},{5,7},{6,4},{7,5},{8,10},{9,11},{10,... | collective-permute-start | bytes 92168 | tf_op jit(solution)/shard_map/ppermute | solution.py:489
  3.9 4.6 %collective-permute-start.1 = (bf16[6,2560]{1,0:T(8,128)(2,1)}, bf16[6,2560]{1,0:T(8,128)(2,1)S(1)}, u32[]{:S(2)}, u32[]{:S(2)}) collective-permute-start(bf16[6,2560]{1,0:T(8,128)(2,1)} %refs_3_.1), channel_id=1, source_target_pairs={{0,1},{1,0},{2,3},{3,2},{4,5},{5,4},{6,7},{7,6},{8,9},{9,8},{10,11... | collective-permute-start | bytes 92168 | tf_op jit(solution)/shard_map/ppermute | solution.py:489
  7.9 1.2 %collective-permute-start.4 = (bf16[6,2560]{1,0:T(8,128)(2,1)S(1)}, bf16[6,2560]{1,0:T(8,128)(2,1)S(1)}, u32[]{:S(2)}, u32[]{:S(2)}) collective-permute-start(bf16[6,2560]{1,0:T(8,128)(2,1)S(1)} %collective-permute-done.2.refs_8_), channel_id=1, source_target_pairs={{0,1},{1,0},{2,3},{3,2},{4,5},{5,4},{6,7},{7,6},{8,9},{9,8},{10,11... | collective-permute-start | bytes 92168 | tf_op jit(solution)/shard_map/ppermute | solution.py:489
  7.9 1.4 %collective-permute-start.5 = (bf16[6,2560]{1,0:T(8,128)(2,1)S(1)}, bf16[6,2560]{1,0:T(8,128)(2,1)S(1)}, u32[]{:S(2)}, u32[]{:S(2)}) collective-permute-start(bf16[6,2560]{1,0:T(8,128)(2,1)S(1)} %collective-permute-done.3.refs_9_), channel_id=1, source_target_pairs={{0,1},{1,0},{2,3},{3,2},{4,5},{5,4},{6,7},{7,6},{8,9},{9,8},{10,11... | collective-permute-start | bytes 92168 | tf_op jit(solution)/shard_map/ppermute | solution.py:489
  13.2 3.2 %collective-permute-start.8 = (bf16[16,2176]{1,0:T(8,128)(2,1)S(1)}, bf16[16,2176]{1,0:T(8,128)(2,1)S(1)}, u32[]{:S(2)}, u32[]{:S(2)}) collective-permute-start(bf16[16,2176]{1,0:T(8,128)(2,1)S(1)} %get-tuple-element.59), channel_id=1, source_target_pairs={{0,1},{1,0},{2,3},{3,2},{4,5},{5,4},{6,7},{7,6},{8,9},{9,8},{10,11... | collective-permute-start | bytes 208904 | tf_op jit(solution)/shard_map/ppermute | solution.py:489
  16.2 1.4 %collective-permute-start.6 = (bf16[16,2176]{1,0:T(8,128)(2,1)S(1)}, bf16[16,2176]{1,0:T(8,128)(2,1)S(1)}, u32[]{:S(2)}, u32[]{:S(2)}) collective-permute-start(bf16[16,2176]{1,0:T(8,128)(2,1)S(1)} %get-tuple-element.53), channel_id=1, source_target_pairs={{0,1},{1,0},{2,3},{3,2},{4,5},{5,4},{6,7},{7,6},{8,9},{9,8},{10,11... | collective-permute-start | bytes 208904 | tf_op jit(solution)/shard_map/ppermute | solution.py:489
  16.7 7.9 %collective-permute-start.9 = (bf16[16,2176]{1,0:T(8,128)(2,1)S(1)}, bf16[16,2176]{1,0:T(8,128)(2,1)S(1)}, u32[]{:S(2)}, u32[]{:S(2)}) collective-permute-start(bf16[16,2176]{1,0:T(8,128)(2,1)S(1)} %get-tuple-element.62), channel_id=1, source_target_pairs={{0,2},{1,3},{2,0},{3,1},{4,6},{5,7},{6,4},{7,5},{8,10},{9,11},{10,... | collective-permute-start | bytes 208904 | tf_op jit(solution)/shard_map/ppermute | solution.py:489
  17.9 9.4 %collective-permute-start.7 = (bf16[16,2176]{1,0:T(8,128)(2,1)S(1)}, bf16[16,2176]{1,0:T(8,128)(2,1)S(1)}, u32[]{:S(2)}, u32[]{:S(2)}) collective-permute-start(bf16[16,2176]{1,0:T(8,128)(2,1)S(1)} %get-tuple-element.56), channel_id=1, source_target_pairs={{0,2},{1,3},{2,0},{3,1},{4,6},{5,7},{6,4},{7,5},{8,10},{9,11},{10,... | collective-permute-start | bytes 208904 | tf_op jit(solution)/shard_map/ppermute | solution.py:489
  19.1 18.3 %collective-permute-start.12 = (bf16[2,2,16,1024]{3,2,1,0:T(8,128)(2,1)S(1)}, bf16[2,2,16,1024]{3,2,1,0:T(8,128)(2,1)S(1)}, u32[]{:S(2)}, u32[]{:S(2)}) collective-permute-start(bf16[2,2,16,1024]{3,2,1,0:T(8,128)(2,1)S(1)} %get-tuple-element.74), channel_id=1, source_target_pairs={{0,4},{4,8},{8,12},{12,0},{1,5},{5,9},{9,13},{13,1},{2,6},{6,10},{... | collective-permute-start | bytes 393224 | tf_op jit(solution)/shard_map/ppermute | solution.py:594
  20.7 16.7 %collective-permute-start.13 = (bf16[2,2,16,1024]{3,2,1,0:T(8,128)(2,1)S(1)}, bf16[2,2,16,1024]{3,2,1,0:T(8,128)(2,1)S(1)}, u32[]{:S(2)}, u32[]{:S(2)}) collective-permute-start(bf16[2,2,16,1024]{3,2,1,0:T(8,128)(2,1)S(1)} %get-tuple-element.76), channel_id=1, source_target_pairs={{0,8},{4,12},{8,0},{12,4},{1,9},{5,13},{9,1},{13,5},{2,10},{6,14},... | collective-permute-start | bytes 393224 | tf_op jit(solution)/shard_map/ppermute | solution.py:594
  23.2 14.1 %collective-permute-start.14 = (bf16[2,2,16,1024]{3,2,1,0:T(8,128)(2,1)S(1)}, bf16[2,2,16,1024]{3,2,1,0:T(8,128)(2,1)S(1)}, u32[]{:S(2)}, u32[]{:S(2)}) collective-permute-start(bf16[2,2,16,1024]{3,2,1,0:T(8,128)(2,1)S(1)} %get-tuple-element.78), channel_id=1, source_target_pairs={{0,12},{4,0},{8,4},{12,8},{1,13},{5,1},{9,5},{13,9},{2,14},{6,2},{... | collective-permute-start | bytes 393224 | tf_op jit(solution)/shard_map/ppermute | solution.py:594
  24.9 7.6 %collective-permute-start.10 = (bf16[16,2048]{1,0:T(8,128)(2,1)S(1)}, bf16[16,2048]{1,0:T(8,128)(2,1)S(1)}, u32[]{:S(2)}, u32[]{:S(2)}) collective-permute-start(bf16[16,2048]{1,0:T(8,128)(2,1)S(1)} %finish0.1.refs_1_), channel_id=1, source_target_pairs={{0,1},{1,0},{2,3},{3,2},{4,5},{5,4},{6,7},{7,6},{8,9},{9,8},{10,11... | collective-permute-start | bytes 196616 | tf_op jit(solution)/shard_map/ppermute | solution.py:489
  27.5 5.0 %collective-permute-start.11 = (bf16[16,2048]{1,0:T(8,128)(2,1)S(1)}, bf16[16,2048]{1,0:T(8,128)(2,1)S(1)}, u32[]{:S(2)}, u32[]{:S(2)}) collective-permute-start(bf16[16,2048]{1,0:T(8,128)(2,1)S(1)} %finish1.1.refs_1_), channel_id=1, source_target_pairs={{0,1},{1,0},{2,3},{3,2},{4,5},{5,4},{6,7},{7,6},{8,9},{9,8},{10,11... | collective-permute-start | bytes 196616 | tf_op jit(solution)/shard_map/ppermute | solution.py:489

commit v2 on v1

v2 whole, which is shorter than its diff:
```python
import functools
import math

import jax
import jax.numpy as jnp
from jax import lax
from jax.experimental import pallas as pl
from jax.experimental.pallas import tpu as pltpu
from jax.sharding import PartitionSpec as P

HEAD_SIZE = 128
LANES = 128
NEG_LARGE = -1e30
BF16 = jnp.bfloat16
F32 = jnp.float32
I32 = jnp.int32
VMEM = pltpu.VMEM
HBM = pltpu.HBM
TILE = 256
PARTS = 1
CHUNKS = 8
FLOPS = 3e8
BYTES = 0
copy_of = pltpu.make_async_copy


def spec(space):
    return pl.BlockSpec(memory_space=space)


def in_hbm(x):
    return pltpu.with_memory_space_constraint(x, HBM)


def shape(dims, dtype=BF16):
    return jax.ShapeDtypeStruct(dims, dtype)


def run(kernel, micros, ins, outs, scratch, args, aliases=None, after=(), limit=8):
    count = len(ins)

    def body(*refs):
        kernel(*refs[:count], *refs[count + len(after) :])

    ins = list(ins) + [pl.ANY] * len(after)
    args = list(args) + list(after)
    return pl.pallas_call(
        body,
        out_shape=tuple(s for s, _ in outs),
        in_specs=[spec(space) for space in ins],
        out_specs=tuple(spec(space) for _, space in outs),
        scratch_shapes=scratch,
        input_output_aliases=aliases or {},
        compiler_params=pltpu.CompilerParams(vmem_limit_bytes=limit << 20),
        cost_estimate=pl.CostEstimate(
            flops=int(micros * FLOPS), bytes_accessed=int(micros * BYTES), transcendentals=0
        ),
    )(*args)


def behind(x, token):
    return lax.optimization_barrier((x, token))[0]


def rounded_up(x, to):
    return -(-x // to) * to


class Sizes:
    def __init__(self, n, inst_count, rows_of, per_rank, kv_shape, w_shape):
        self.n = n
        self.inst_count = inst_count
        self.rows_of = rows_of
        self.per_rank = per_rank
        self.pool, _, self.extent, self.kv_width = kv_shape
        self.q_width, self.out_columns = w_shape
        self.q_heads = self.q_width // HEAD_SIZE
        self.kv_heads = self.kv_width // HEAD_SIZE
        self.group = self.q_heads // self.kv_heads
        self.step_rows = rounded_up(rows_of, 8)
        self.all_rows = 2 * self.step_rows
        self.positions = self.pool * self.extent
        self.part_groups = self.kv_heads // (2 * PARTS)
        self.part_heads = self.part_groups * self.group
        self.part_width = self.part_heads * HEAD_SIZE
        self.per_tile = LANES // (2 * self.part_heads)
        self.packed = self.part_width + LANES * -(-3 // self.per_tile)
        self.chunk_rows = self.q_width // CHUNKS
        self.early = 2
        while self.early * (self.q_width + 2 * self.kv_width) < n * 2 * self.kv_width:
            self.early *= 2
        self.at_offset = 2 * rows_of
        self.at_source = 4 * rows_of
        self.at_place = self.at_source + self.pool
        self.plan_rows = rounded_up(
            -(-(self.at_place + (inst_count - 1) * per_rank) // LANES), 8
        )


def w_copies(w_hbm, chunks, refs, sems, first=0):
    rows = w_hbm.shape[0] // CHUNKS
    side = lax.rem(lax.axis_index("tp"), 2)
    copies = []
    for i, k in enumerate(chunks):
        half = side if k < CHUNKS // 2 else 1 - side
        start = half * (w_hbm.shape[0] // 2) + (k % (CHUNKS // 2)) * rows
        source = w_hbm.at[pl.ds(pl.multiple_of(start, LANES), rows)]
        copies.append(copy_of(source, refs[i], sems.at[first + i]))
    return copies


def prepare_kernel(z, chunks, *refs):
    m = 2 * z.early
    w_hbm, kv_hbm, lengths_hbm, table_hbm, moves_hbm, dest_hbm, first_hbm, second_hbm = refs[:8]
    pieces = (None, None) + refs[8 : 6 + m]
    pages, rows, visible_ref, plan_ref = refs[6 + m : 10 + m]
    outgoing = refs[10 + m : 9 + m + z.inst_count]
    w_refs = refs[9 + m + z.inst_count : 9 + m + z.inst_count + len(chunks)]
    first, second, lengths, table, moves, dest, plan, sems = refs[9 + m + z.inst_count + len(chunks) :]
    me = lax.axis_index("tp")
    inst = lax.axis_index("inst")
    small = [
        copy_of(table_hbm, table, sems.at[1]),
        copy_of(moves_hbm, moves, sems.at[2]),
        copy_of(lengths_hbm, lengths, sems.at[0]),
        copy_of(dest_hbm, dest, sems.at[3]),
    ]
    own = [copy_of(first_hbm, first, sems.at[5]), copy_of(second_hbm, second, sems.at[6])]
    kv_copy = copy_of(kv_hbm, pages.at[pl.ds(0, z.pool)], sems.at[4])
    for copy in small + own + [kv_copy]:
        copy.start()
    pages[z.pool] = jnp.zeros_like(pages[z.pool])
    rows[...] = jnp.zeros_like(rows)
    for copy in small:
        copy.wait()

    def sends(i, act):
        request = moves[0, i]
        origin = lax.div(request, z.rows_of)
        slot = lax.bitwise_xor(moves[1, i], origin)
        row = request - inst * z.rows_of
        for s in range(1, z.inst_count):

            @pl.when((origin == inst) & (slot == s))
            def _():
                for j in range(z.per_rank):
                    local = table[row, me + z.n * j] - me * z.pool
                    act(copy_of(kv_hbm.at[local], outgoing[s - 1].at[j], sems.at[7]))

    for i in range(moves.shape[1]):
        sends(i, lambda copy: copy.start())
    w_loads = w_copies(w_hbm, chunks, w_refs, sems, 8)
    for copy in w_loads:
        copy.start()

    grid = (z.all_rows, z.positions)
    at = lax.broadcasted_iota(I32, grid, 1)
    row = lax.broadcasted_iota(I32, grid, 0)
    step = lax.div(row, z.step_rows)
    row_of = row - step * z.step_rows
    page_of = lax.div(at, z.extent)
    offset = at - page_of * z.extent
    newest = jnp.full(grid, -1, I32)
    place = jnp.full(grid, 1 << 30, I32)
    for r in range(z.rows_of):
        here = row_of == r
        newest = jnp.where(here, lengths[inst * z.rows_of + r], newest)
        for j in range(z.per_rank):
            number = me + z.n * j
            local = table[r, number] - me * z.pool
            place = jnp.where(here & (page_of == local), number * z.extent + offset, place)
    visible_ref[...] = (place <= newest + step).astype(I32)

    for k in range(2):
        for r in range(z.rows_of):
            position = lengths[inst * z.rows_of + r] + k
            local = table[r, lax.div(position, z.extent)] - me * z.pool
            mine = (local >= 0) & (local < z.pool)
            plan[k * z.rows_of + r] = jnp.where(mine, local, z.pool + 1)
            plan[z.at_offset + k * z.rows_of + r] = lax.rem(position, z.extent)
    for p in range(z.pool):
        plan[z.at_source + p] = p
    for k in range((z.inst_count - 1) * z.per_rank):
        plan[z.at_place + k] = -1
    for i in range(moves.shape[1]):
        request = moves[0, i]
        target = moves[1, i]
        origin = lax.div(request, z.rows_of)
        slot = lax.bitwise_xor(target, origin)

        @pl.when((origin == inst) & (slot > 0))
        def _():
            for j in range(z.per_rank):
                local = table[request - inst * z.rows_of, me + z.n * j] - me * z.pool
                plan[z.at_source + local] = z.pool

        @pl.when((target == inst) & (slot > 0))
        def _():
            for j in range(z.per_rank):
                plan[z.at_place + (slot - 1) * z.per_rank + j] = dest[i, me + z.n * j] - me * z.pool

    where = lax.broadcasted_iota(I32, plan_ref.shape, 0) * LANES + lax.broadcasted_iota(
        I32, plan_ref.shape, 1
    )
    packed = jnp.zeros(plan_ref.shape, I32)
    for k in range(z.at_place + (z.inst_count - 1) * z.per_rank):
        packed = jnp.where(where == k, plan[k], packed)
    plan_ref[...] = packed

    for copy in own:
        copy.wait()
    put_pieces(z, rows, range(z.early), (first, second) + pieces[2:])
    fresh = rows[:, z.q_width :].astype(F32)
    line_id = lax.broadcasted_iota(I32, fresh.shape, 0)
    row_id = lax.broadcasted_iota(I32, (z.extent, z.kv_width), 0)
    for i in range(moves.shape[1]):
        sends(i, lambda copy: copy.wait())
    for i in range(moves.shape[1]):
        request = moves[0, i]
        origin = lax.div(request, z.rows_of)
        slot = lax.bitwise_xor(moves[1, i], origin)
        r = request - inst * z.rows_of
        for s in range(1, z.inst_count):

            @pl.when((origin == inst) & (slot == s) & (me >= z.n - 2))
            def _():
                for k in range(2):
                    position = lengths[request] + k
                    number = lax.div(position, z.extent)
                    chosen = line_id == k * z.step_rows + r
                    new = jnp.sum(jnp.where(chosen, fresh, 0.0), axis=0, keepdims=True)
                    target = jnp.where(
                        number == me + z.n * (z.per_rank - 1), lax.rem(position, z.extent), -1
                    )
                    for kv in range(2):
                        old = outgoing[s - 1][z.per_rank - 1, kv].astype(F32)
                        outgoing[s - 1][z.per_rank - 1, kv] = jnp.where(
                            row_id == target, new[:, kv * z.kv_width : (kv + 1) * z.kv_width], old
                        ).astype(BF16)

    for copy in [kv_copy] + w_loads:
        copy.wait()


def put_pieces(z, rows, which, pieces):
    me = lax.axis_index("tp")
    width = pieces[0].shape[1]
    for i, d in enumerate(which):
        start = pl.multiple_of((me ^ d) * width, LANES)
        for k in range(2):
            rows[k * z.step_rows : k * z.step_rows + z.rows_of, pl.ds(start, width)] = pieces[
                2 * i + k
            ][...]


def read(plan, k):
    return plan[k // LANES, k % LANES]


def attend_part(z, part, rows, pages, visible, send_ref, keep_ref, stats_ref):
    side = lax.rem(lax.axis_index("tp"), 2)
    half = z.kv_heads // 2
    lane = lax.broadcasted_iota(I32, (z.all_rows, LANES), 1)
    scale = 1.0 / math.sqrt(HEAD_SIZE)
    stats = [jnp.zeros((z.all_rows, LANES), F32) for _ in range(2)]
    for i in range(2 * z.part_groups):
        kept, k = divmod(i, z.part_groups)
        g = (side if kept else 1 - side) * half + part * z.part_groups + k
        q = jnp.concatenate(
            [
                rows[:, pl.ds(pl.multiple_of((g * z.group + h) * HEAD_SIZE, LANES), HEAD_SIZE)]
                for h in range(z.group)
            ],
            axis=0,
        )
        columns = pl.ds(pl.multiple_of(g * HEAD_SIZE, LANES), HEAD_SIZE)
        keys = pages[0 : z.pool, 0, :, columns].reshape(z.positions, HEAD_SIZE)
        values = pages[0 : z.pool, 1, :, columns].reshape(z.positions, HEAD_SIZE)
        scores = lax.dot_general(q, keys, (((1,), (1,)), ((), ())), preferred_element_type=F32)
        scores = (scores * scale).reshape(z.group, z.all_rows, z.positions)
        scores = jnp.where(visible, scores, NEG_LARGE)
        top = jnp.max(scores, axis=2, keepdims=True)
        exponent = jnp.where(visible, jnp.exp(scores - top), 0.0)
        total = jnp.sum(exponent, axis=2, keepdims=True)
        summed = jnp.dot(
            exponent.astype(BF16).reshape(z.group * z.all_rows, z.positions),
            values,
            preferred_element_type=F32,
        )
        for h in range(z.group):
            head = k * z.group + h
            piece = summed[h * z.all_rows : (h + 1) * z.all_rows]
            out_columns = slice(head * HEAD_SIZE, (head + 1) * HEAD_SIZE)
            if kept:
                keep_ref[:, out_columns] = piece
            else:
                send_ref[:, out_columns] = piece.astype(BF16)
            stats[kept] = jnp.where(lane == head, top[h], stats[kept])
            stats[kept] = jnp.where(lane == z.part_heads + head, total[h], stats[kept])
    put_stats(z, send_ref, stats[0])
    stats_ref[...] = stats[1]


def put_stats(z, ref, stats):
    used = 2 * z.part_heads
    lane = lax.broadcasted_iota(I32, stats.shape, 1)
    rest = stats
    tiles = {}
    for k in range(3):
        term = rest.astype(BF16).astype(F32)
        rest = rest - term
        tile, at = divmod(k, z.per_tile)
        if at:
            term = jnp.where(lane < at * used, tiles[tile], pltpu.roll(term, at * used, 1))
        tiles[tile] = term
    for tile, value in tiles.items():
        start = z.part_width + tile * LANES
        ref[:, start : start + LANES] = value.astype(BF16)


def get_stats(z, ref):
    used = 2 * z.part_heads
    stats = 0.0
    for k in range(3):
        tile, at = divmod(k, z.per_tile)
        start = z.part_width + tile * LANES
        term = ref[:, start : start + LANES].astype(F32)
        stats += pltpu.roll(term, LANES - at * used, 1) if at else term
    lane = lax.broadcasted_iota(I32, stats.shape, 1)
    return jnp.where(lane < used, stats, 0.0)


def attend_kernel(z, chunks, *refs):
    m = 2 * (z.n - z.early)
    w_hbm, plan_vmem, visible_ref, _, _ = refs[:5]
    pieces = refs[5 : 5 + m]
    send_ref, keep_ref, stats_ref, rows, pages, kv_out = refs[5 + m : 11 + m]
    w_refs = refs[11 + m : 11 + m + len(chunks)]
    plan, sems = refs[11 + m + len(chunks) :]
    w_loads = w_copies(w_hbm, chunks, w_refs, sems, 2)
    for copy in w_loads:
        copy.start()
    plan_copy = copy_of(plan_vmem, plan, sems.at[0])
    plan_copy.start()
    put_pieces(z, rows, range(z.early, z.n), pieces)
    plan_copy.wait()

    fresh = rows[:, z.q_width :].astype(F32)
    row_id = lax.broadcasted_iota(I32, (z.extent, z.kv_width), 0)
    for k in range(2):
        for r in range(z.rows_of):
            slot = read(plan, k * z.rows_of + r)
            here = row_id == read(plan, z.at_offset + k * z.rows_of + r)
            line = k * z.step_rows + r
            for kv in range(2):
                new = fresh[line : line + 1, kv * z.kv_width : (kv + 1) * z.kv_width]
                old = pages[slot, kv].astype(F32)
                pages[slot, kv] = jnp.where(here, new, old).astype(BF16)

    writes = [
        copy_of(pages.at[read(plan, z.at_source + p)], kv_out.at[p], sems.at[1])
        for p in range(z.pool)
    ]
    for copy in writes:
        copy.start()
    visible = (visible_ref[...] > 0)[None]
    attend_part(z, 0, rows, pages, visible, send_ref, keep_ref, stats_ref)
    for copy in writes + w_loads:
        copy.wait()


def joined(z, acc_ref, stats_ref, other_ref):
    mine = stats_ref[...]
    theirs = get_stats(z, other_ref)
    lane = lax.broadcasted_iota(I32, mine.shape, 1)
    top = jnp.maximum(mine, theirs)
    scale_mine = jnp.exp(mine - top)
    scale_theirs = jnp.exp(theirs - top)
    total = mine * pltpu.roll(scale_mine, z.part_heads, 1) + theirs * pltpu.roll(
        scale_theirs, z.part_heads, 1
    )
    stats = jnp.where(
        lane < z.part_heads, top, jnp.where(lane < 2 * z.part_heads, total, 0.0)
    )
    for h in range(z.part_heads):
        columns = slice(h * HEAD_SIZE, (h + 1) * HEAD_SIZE)
        piece = acc_ref[:, columns] * scale_mine[:, h : h + 1] + other_ref[:, columns].astype(
            F32
        ) * scale_theirs[:, h : h + 1]
        yield columns, piece, stats, h


def merge_kernel(z, acc_ref, stats_ref, other_ref, acc_out, stats_out, send_ref):
    for columns, piece, stats, _ in joined(z, acc_ref, stats_ref, other_ref):
        acc_out[:, columns] = piece
        send_ref[:, columns] = piece.astype(BF16)
    stats_out[...] = stats
    put_stats(z, send_ref, stats)


def finish_kernel(z, acc_ref, stats_ref, other_ref, mixed_ref):
    for columns, piece, stats, h in joined(z, acc_ref, stats_ref, other_ref):
        total = stats[:, z.part_heads + h : z.part_heads + h + 1]
        mixed_ref[:, columns] = (piece / total).astype(BF16)


def stage_kernel(chunks, w_hbm, *refs):
    loads = w_copies(w_hbm, chunks, refs, refs[-1])
    for copy in loads:
        copy.start()
    for copy in loads:
        copy.wait()


def column_tiles(width, body):
    @pl.loop(0, width // TILE)
    def _(t):
        body(pl.ds(pl.multiple_of(t * TILE, TILE), TILE))


def product(z, mixed, weights, columns, first=0):
    total = None
    for i, w in enumerate(weights):
        begin = (first + i) * z.chunk_rows
        term = jnp.dot(
            mixed[:, begin : begin + z.chunk_rows], w[:, columns], preferred_element_type=F32
        )
        total = term if total is None else total + term
    return total


def project_kernel(z, chunks, *refs):
    half = CHUNKS // 2
    w_hbm, mixed = refs[:2]
    weights = refs[2 : 2 + half]
    acc_ref = refs[2 + half]
    loads = w_copies(w_hbm, chunks, refs[3 + half :], refs[-1])
    for copy in loads:
        copy.start()

    def body(columns):
        acc_ref[:, columns] = product(z, mixed, weights, columns)

    column_tiles(z.out_columns, body)
    for copy in loads:
        copy.wait()


def last_kernel(z, held, chunks, *refs):
    w_hbm, acc_in, mixed, plan_vmem = refs[:4]
    weights = refs[4 : 4 + held]
    arrived = refs[4 + held : 3 + held + z.inst_count]
    first_ref, second_ref, kv_out, late, acc, plan, sems = refs[4 + held + z.inst_count :]
    plan_copy = copy_of(plan_vmem, plan, sems.at[0])
    plan_copy.start()
    late_refs = [late.at[i] for i in range(len(chunks))]
    loads = w_copies(w_hbm, chunks, late_refs, sems, 2)
    for copy in loads:
        copy.start()
    plan_copy.wait()

    def placed(act):
        for s in range(z.inst_count - 1):
            for j in range(z.per_rank):
                slot = read(plan, z.at_place + s * z.per_rank + j)

                @pl.when(slot >= 0)
                def _():
                    act(copy_of(arrived[s].at[j], kv_out.at[slot], sems.at[1]))

    placed(lambda copy: copy.start())

    def early(columns):
        acc[:, columns] = acc_in[:, columns] + product(z, mixed, weights, columns)

    column_tiles(z.out_columns, early)
    for i, copy in enumerate(loads):
        copy.wait()

        def body(columns):
            total = acc[:, columns] + product(z, mixed, [late_refs[i]], columns, held + i)
            if i < len(loads) - 1:
                acc[:, columns] = total
            else:
                first_ref[:, columns] = total[: z.rows_of].astype(BF16)
                second_ref[:, columns] = total[z.step_rows : z.step_rows + z.rows_of].astype(BF16)

        column_tiles(z.out_columns, body)
    placed(lambda copy: copy.wait())


def steps(qkv_first, qkv_second, w_out, kv_cache, lengths, page_table, moves, dest_pages):
    n = lax.axis_size("tp")
    inst_count = lax.axis_size("inst")
    moves = moves.T
    rows_of, max_pages = page_table.shape
    z = Sizes(n, inst_count, rows_of, max_pages // n, kv_cache.shape, w_out.shape)
    smem = pltpu.SMEM
    dma = pltpu.SemaphoreType.DMA
    page = kv_cache.shape[1:]

    def swap(x, d):
        return lax.ppermute(x, "tp", [(i, i ^ d) for i in range(n)])

    stages = []
    while (1 << len(stages)) < n:
        stages.append(1 << len(stages))

    w_hbm = in_hbm(w_out)
    chunk = (shape((z.chunk_rows, z.out_columns)), VMEM)
    have = {0: (qkv_first, qkv_second)}
    for d in range(1, z.early):
        have[d] = tuple(swap(x, d) for x in have[0])
    far = [d for d in stages if d >= z.early]
    for d in far:
        have[d] = tuple(swap(x, d) for x in have[0])
    pages, rows, visible, plan, *more = run(
        functools.partial(prepare_kernel, z, (0,)),
        2,
        [HBM] * 8 + [VMEM] * (2 * z.early - 2),
        [
            (shape((z.pool + 2,) + page), VMEM),
            (shape((z.all_rows, z.q_width + 2 * z.kv_width)), VMEM),
            (shape((z.all_rows, z.positions), I32), VMEM),
            (shape((z.plan_rows, LANES), I32), VMEM),
        ]
        + [(shape((z.per_rank,) + page), VMEM)] * (inst_count - 1)
        + [chunk],
        [
            pltpu.VMEM(qkv_first.shape, BF16),
            pltpu.VMEM(qkv_second.shape, BF16),
            smem(lengths.shape, I32),
            smem(page_table.shape, I32),
            smem(moves.shape, I32),
            smem(dest_pages.shape, I32),
            smem((z.plan_rows * LANES,), I32),
            dma((9,)),
        ],
        [w_hbm]
        + [
            in_hbm(x)
            for x in (kv_cache, lengths, page_table, moves, dest_pages, qkv_first, qkv_second)
        ]
        + [x for d in range(1, z.early) for x in have[d]],
    )
    outgoing, weights = more[:-1], more[-1:]
    for d in far:
        for e in range(1, d):
            have[d ^ e] = tuple(swap(behind(x, plan), e) for x in have[d])
    arrived = []
    for s in range(1, inst_count):
        arrived.append(
            lax.ppermute(outgoing[s - 1], "inst", [(i, i ^ s) for i in range(inst_count)])
        )

    send, acc, stats, _, _, kv_mid, *loaded = run(
        functools.partial(attend_kernel, z, (1,)),
        2,
        [HBM] + [VMEM] * (4 + 2 * (n - z.early)),
        [
            (shape((z.all_rows, z.packed)), VMEM),
            (shape((z.all_rows, z.part_width), F32), VMEM),
            (shape((z.all_rows, LANES), F32), VMEM),
            (shape(rows.shape), VMEM),
            (shape(pages.shape), VMEM),
            (shape(kv_cache.shape), HBM),
            chunk,
        ],
        [smem((z.plan_rows, LANES), I32), dma((3,))],
        [w_hbm, plan, visible, pages, rows] + [x for d in range(z.early, n) for x in have[d]],
        aliases={3: 4, 4: 3},
    )
    weights += loaded
    for d in stages[:-1]:
        acc, stats, send = run(
            functools.partial(merge_kernel, z),
            0.2,
            [VMEM] * 3,
            [
                (shape((z.all_rows, z.part_width), F32), VMEM),
                (shape((z.all_rows, LANES), F32), VMEM),
                (shape((z.all_rows, z.packed)), VMEM),
            ],
            [],
            [acc, stats, swap(send, d)],
        )
    theirs = swap(send, stages[-1])
    weights += run(
        functools.partial(stage_kernel, (2, 3)),
        3,
        [HBM],
        [chunk] * 2,
        [dma((2,))],
        [w_hbm],
        after=[stats],
    )
    (mixed,) = run(
        functools.partial(finish_kernel, z),
        0.3,
        [VMEM] * 3,
        [(shape((z.all_rows, z.part_width)), VMEM)],
        [],
        [acc, stats, theirs],
        after=weights[-1:],
    )
    other = swap(mixed, 1)
    total, *held = run(
        functools.partial(project_kernel, z, (4, 5)),
        3.4,
        [HBM] + [VMEM] * (1 + CHUNKS // 2),
        [(shape((z.all_rows, z.out_columns), F32), VMEM)] + [chunk] * 2,
        [dma((2,))],
        [w_hbm, mixed, *weights],
    )
    return tuple(
        run(
            functools.partial(last_kernel, z, 2, (6, 7)),
            3.4,
            [HBM] + [VMEM] * (4 + inst_count) + [HBM],
            [(shape((rows_of, z.out_columns)), VMEM)] * 2 + [(shape(kv_cache.shape), HBM)],
            [
                pltpu.VMEM((2, z.chunk_rows, z.out_columns), BF16),
                pltpu.VMEM((z.all_rows, z.out_columns), F32),
                smem((z.plan_rows, LANES), I32),
                dma((4,)),
            ],
            [w_hbm, total, other, plan, *held, *arrived, kv_mid],
            aliases={5 + inst_count: 2},
            limit=12,
        )
    )


def solution(mesh):
    placed = (
        P(("groups", "inst"), "tp"),
        P(("groups", "inst"), "tp"),
        P(None, "tp"),
        P(("groups", "inst", "tp"), None, None, None),
        P("groups"),
        P(("groups", "inst"), None),
        P("groups", None),
        P("groups", None),
    )
    return jax.shard_map(
        steps,
        mesh=mesh,
        in_specs=placed,
        out_specs=(
            P(("groups", "inst"), "tp"),
            P(("groups", "inst"), "tp"),
            P(("groups", "inst", "tp"), None, None, None),
        ),
        check_vma=False,
    )
```

time: 38.3 us -> 36.4 us (0.950)
  waiting for transfers between devices: 1.97 us -> 5.27 us
  starting transfers between devices: 13 us -> 10.2 us
  Pallas kernels: 22.3 us -> 20 us
    ppermute x3, waiting for transfers between devices: 0.01 us -> 2.47 us  [steps(): lax.ppermute(outgoing[s - 1], 'inst', [(i, i ^ s) for i in range(inst_cou...]
    pallas_call x12 -> x7, Pallas kernels: 22.3 us -> 20 us  [run(): pl.pallas_call(body, out_shape=tuple((s for s, _ in outs)), in_specs=[spe...]
    ppermute x12 -> x9, starting transfers between devices: 7.5 us -> 5.84 us  [swap(): return lax.ppermute(x, 'tp', [(i, i ^ d) for i in range(n)])]
    ppermute x3, starting transfers between devices: 5.51 us -> 4.39 us  [steps(): lax.ppermute(outgoing[s - 1], 'inst', [(i, i ^ s) for i in range(inst_cou...]
    ppermute x12 -> x9, waiting for transfers between devices: 1.96 us -> 2.79 us  [swap(): return lax.ppermute(x, 'tp', [(i, i ^ d) for i in range(n)])]
  transfers between devices with their start and end apart: 15 -> 12, of which waited for: 3 -> 5; matrix products, arithmetic and copies ran while one was open for 0% -> 0% of each run, Pallas kernels for 46% -> 30%
where the time goes in v2:
time: 36.4 us; the launch traced here: 36.2 us
  Pallas kernels  20 us (55%)
  starting transfers between devices  10.2 us (28%)
  waiting for transfers between devices  5.27 us (14%)
  between operations  0.71 us (2%)
    pallas_call x7, Pallas kernels, run(): pl.pallas_call(body, out_shape=tuple((s for s, _ in outs)), in_specs=[spe...  20 us
    ppermute x9, starting transfers between devices, swap(): return lax.ppermute(x, 'tp', [(i, i ^ d) for i in range(n)])  5.84 us
    ppermute x3, starting transfers between devices, steps(): lax.ppermute(outgoing[s - 1], 'inst', [(i, i ^ s) for i in range(inst_cou...  4.39 us
    ppermute x9, waiting for transfers between devices, swap(): return lax.ppermute(x, 'tp', [(i, i ^ d) for i in range(n)])  2.79 us
    ppermute x3, waiting for transfers between devices, steps(): lax.ppermute(outgoing[s - 1], 'inst', [(i, i ^ s) for i in range(inst_cou...  2.47 us
  transfers between devices with their start and end apart: 12, of which 5 were waited for; matrix products, arithmetic and copies ran while one was open for 0% of the time, Pallas kernels for 30%

profile of v2, /device:TPU:0, one launch (start us, length us, event | category | flops | bytes accessed | tf_op | source)
XLA Modules:
  0.0 36.2 jit_solution(9937082478149425700)
XLA Ops:
  0.6 0.6 %collective-permute-start = (bf16[6,2560]{1,0:T(8,128)(2,1)}, bf16[6,2560]{1,0:T(8,128)(2,1)S(1)}, u32[]{:S(2)}, u32[]{:S(2)}) collective-permute-start(bf16[6,2560]{1,0:T(8,128)(2,1)} %refs_6_.1), channel_id=1, source_target_pairs={{0,1},{1,0},{2,3},{3,2},{4,5},{5,4},{6,7},{7,6},{8,9},{9,8},{10,11... | collective-permute-start | bytes 92168 | tf_op jit(solution)/shard_map/ppermute | solution.py:503
  1.2 0.1 collective-permute-start.1
  1.3 2.9 %collective-permute-start.2 = (bf16[6,2560]{1,0:T(8,128)(2,1)}, bf16[6,2560]{1,0:T(8,128)(2,1)S(1)}, u32[]{:S(2)}, u32[]{:S(2)}) collective-permute-start(bf16[6,2560]{1,0:T(8,128)(2,1)} %refs_6_.1), channel_id=1, source_target_pairs={{0,2},{1,3},{2,0},{3,1},{4,6},{5,7},{6,4},{7,5},{8,10},{9,11},{10,... | collective-permute-start | bytes 92168 | tf_op jit(solution)/shard_map/ppermute | solution.py:503
  4.2 0.0 collective-permute-start.3
  4.2 0.0 collective-permute-done.refs_8_
  4.2 0.0 collective-permute-done.1.refs_9_
  4.2 3.3 %shard_map.103 = (bf16[18,2,16,1024]{3,2,1,0:T(8,128)(2,1)S(1)}, bf16[16,10240]{1,0:T(8,128)(2,1)S(1)}, s32[16,256]{1,0:T(8,128)S(1)}, s32[8,128]{1,0:T(8,128)S(...) custom-call(bf16[8192,2048]{1,0:T(8,128)(2,1)} %refs_0_.9, ...), custom_call_target="tpu_custom_call" | custom-call | flops 600000000 | tf_op jit(solution)/shard_map/pallas_call | solution.py:47
  7.5 0.9 %collective-permute-done.3.refs_6_ = bf16[6,2560]{1,0:T(8,128)(2,1)S(1)} collective-permute-done((bf16[6,2560]{1,0:T(8,128)(2,1)}, bf16[6,2560]{1,0:T(8,128)(2,1)S(1)}, u32[]{:S(2)}, u32[]{:S(2)}) %collective-permute-start.3) | collective-permute-done | bytes 30752 | tf_op jit(solution)/shard_map/ppermute | solution.py:503
  8.4 0.0 collective-permute-done.2.refs_5_
  8.4 0.0 collective-permute-start.4
  8.4 0.5 %collective-permute-start.5 = (bf16[6,2560]{1,0:T(8,128)(2,1)S(1)}, bf16[6,2560]{1,0:T(8,128)(2,1)S(1)}, u32[]{:S(2)}, u32[]{:S(2)}) collective-permute-start(bf16[6,2560]{1,0:T(8,128)(2,1)S(1)} %collective-permute-done.3.refs_6_), channel_id=1, source_target_pairs={{0,1},{1,0},{2,3},{3,2},{4,5},{5,4},{6,7},{7,6},{8,9},{9,8},{10,11... | collective-permute-start | bytes 92168 | tf_op jit(solution)/shard_map/ppermute | solution.py:503
  8.9 0.7 %collective-permute-done.4.refs_7_ = bf16[6,2560]{1,0:T(8,128)(2,1)S(1)} collective-permute-done((bf16[6,2560]{1,0:T(8,128)(2,1)S(1)}, bf16[6,2560]{1,0:T(8,128)(2,1)S(1)}, u32[]{:S(2)}, u32[]{:S(2)}) %collective-permute-start.4) | collective-permute-done | bytes 30752 | tf_op jit(solution)/shard_map/ppermute | solution.py:503
  9.6 0.2 collective-permute-done.5.refs_8_
  9.8 2.5 %shard_map.104 = (bf16[16,4352]{1,0:T(8,128)(2,1)S(1)}, f32[16,4096]{1,0:T(8,128)S(1)}, f32[16,128]{1,0:T(8,128)S(1)}, bf16[16,10240]{1,0:T(8,128)(2,1)S(1)}, bf...) custom-call(bf16[8192,2048]{1,0:T(8,128)(2,1)} %refs_0_.9, ...), custom_call_target="tpu_custom_call", output_to_operand_aliasing={{4}: (3, {}), {3}: (4, {})} | custom-call | flops 600000000 | tf_op jit(solution)/shard_map/pallas_call | solution.py:47
  12.3 0.4 %collective-permute-start.6 = (bf16[16,4352]{1,0:T(8,128)(2,1)S(1)}, bf16[16,4352]{1,0:T(8,128)(2,1)S(1)}, u32[]{:S(2)}, u32[]{:S(2)}) collective-permute-start(bf16[16,4352]{1,0:T(8,128)(2,1)S(1)} %get-tuple-element.34), channel_id=1, source_target_pairs={{0,1},{1,0},{2,3},{3,2},{4,5},{5,4},{6,7},{7,6},{8,9},{9,8},{10,11... | collective-permute-start | bytes 417800 | tf_op jit(solution)/shard_map/ppermute | solution.py:503
  12.7 1.0 %collective-permute-done.6.refs_2_ = bf16[16,4352]{1,0:T(8,128)(2,1)S(1)} collective-permute-done((bf16[16,4352]{1,0:T(8,128)(2,1)S(1)}, bf16[16,4352]{1,0:T(8,128)(2,1)S(1)}, u32[]{:S(2)}, u32[]{:S(2)}) %collective-permute-start.6) | collective-permute-done | bytes 139296 | tf_op jit(solution)/shard_map/ppermute | solution.py:503
  13.7 0.3 shard_map.105
  14.1 1.3 %collective-permute-start.7 = (bf16[16,4352]{1,0:T(8,128)(2,1)S(1)}, bf16[16,4352]{1,0:T(8,128)(2,1)S(1)}, u32[]{:S(2)}, u32[]{:S(2)}) collective-permute-start(bf16[16,4352]{1,0:T(8,128)(2,1)S(1)} %get-tuple-element.37), channel_id=1, source_target_pairs={{0,2},{1,3},{2,0},{3,1},{4,6},{5,7},{6,4},{7,5},{8,10},{9,11},{10,... | collective-permute-start | bytes 417800 | tf_op jit(solution)/shard_map/ppermute | solution.py:503
  15.3 1.5 %collective-permute-start.9 = (bf16[2,2,16,1024]{3,2,1,0:T(8,128)(2,1)S(1)}, bf16[2,2,16,1024]{3,2,1,0:T(8,128)(2,1)S(1)}, u32[]{:S(2)}, u32[]{:S(2)}) collective-permute-start(bf16[2,2,16,1024]{3,2,1,0:T(8,128)(2,1)S(1)} %get-tuple-element.45), channel_id=1, source_target_pairs={{0,4},{4,0},{8,12},{12,8},{1,5},{5,1},{9,13},{13,9},{2,6},{6,2},{1... | collective-permute-start | bytes 393224 | tf_op jit(solution)/shard_map/ppermute | solution.py:553
  16.9 2.6 %collective-permute-start.10 = (bf16[2,2,16,1024]{3,2,1,0:T(8,128)(2,1)S(1)}, bf16[2,2,16,1024]{3,2,1,0:T(8,128)(2,1)S(1)}, u32[]{:S(2)}, u32[]{:S(2)}) collective-permute-start(bf16[2,2,16,1024]{3,2,1,0:T(8,128)(2,1)S(1)} %get-tuple-element.46), channel_id=1, source_target_pairs={{0,8},{4,12},{8,0},{12,4},{1,9},{5,13},{9,1},{13,5},{2,10},{6,14},... | collective-permute-start | bytes 393224 | tf_op jit(solution)/shard_map/ppermute | solution.py:553
  19.5 0.2 collective-permute-start.11
  19.7 3.5 %shard_map.106 = (bf16[1024,2048]{1,0:T(8,128)(2,1)S(1)}, bf16[1024,2048]{1,0:T(8,128)(2,1)S(1)}) custom-call(bf16[8192,2048]{1,0:T(8,128)(2,1)} %refs_0_.9, f32[16,128]{1,0:T(8,128)S(1)} %get-tuple-element.36.refs_1_), custom_call_target="tpu_custom_call" | custom-call | flops 900000000 | tf_op jit(solution)/shard_map/pallas_call | solution.py:47
  23.2 0.0 collective-permute-done.7.refs_2_
  23.2 0.5 %shard_map.107.refs_1_ = bf16[16,4096]{1,0:T(8,128)(2,1)S(1)} custom-call(f32[16,4096]{1,0:T(8,128)S(1)} %get-tuple-element.35.refs_0_, f32[16,128]{1,0:T(8,128)S(1)} %get-tuple-element.36.refs_1_, bf16[16,4352]{1,0:T(8,128)(2,1)S(1)} %collective-permute-done.7.refs_2_, bf16[1024,2048]{1,0:T(8,128)(2,1)S(1)} %get-tuple-element.38.refs_3_.refs_5_), custom_call_target="tpu_custom_call" | custom-call | flops 90000000 | tf_op jit(solution)/shard_map/pallas_call | solution.py:47
  23.7 0.1 collective-permute-start.8
  23.8 3.5 %shard_map.108 = (f32[16,2048]{1,0:T(8,128)S(1)}, bf16[1024,2048]{1,0:T(8,128)(2,1)S(1)}, bf16[1024,2048]{1,0:T(8,128)(2,1)S(1)}) custom-call(bf16[8192,2048]{1,0:T(8,128)(2,1)} %refs_0_.9, bf16[16,4096]{1,0:T(8,128)(2,1)S(1)} %shard_map.107.refs_1_, bf16[1024,2048]{1,0:T(8,128)(2,1)S(1)} %get-tuple-element.39.refs_2_, ...), custom_call_target="tpu_custom_call" | custom-call | flops 1020000000 | tf_op jit(solution)/shard_map/pallas_call | solution.py:47
  27.3 0.0 collective-permute-done.9.refs_6_
  27.3 2.5 %collective-permute-done.10.refs_7_ = bf16[2,2,16,1024]{3,2,1,0:T(8,128)(2,1)S(1)} collective-permute-done((bf16[2,2,16,1024]{3,2,1,0:T(8,128)(2,1)S(1)}, bf16[2,2,16,1024]{3,2,1,0:T(8,128)(2,1)S(1)}, u32[]{:S(2)}, u32[]{:S(2)}) %collective-permute-start.10) | collective-permute-done | bytes 131104 | tf_op jit(solution)/shard_map/ppermute | solution.py:553
  29.8 0.0 collective-permute-done.11.refs_8_
  29.8 0.0 collective-permute-done.8.refs_2_
  29.8 6.5 %shard_map.109 = (bf16[6,2048]{1,0:T(8,128)(2,1)}, bf16[6,2048]{1,0:T(8,128)(2,1)}, bf16[16,2,16,1024]{3,2,1,0:T(8,128)(2,1)}) custom-call(bf16[8192,2048]{1,0:T(8,128)(2,1)} %refs_0_.9, f32[16,2048]{1,0:T(8,128)S(1)} %get-tuple-element.42.refs_1_, bf16[16,4096]{1,0:T(8,128)(2,1)S(1)} %collective-permute-done.8.refs_2_, ...), custom_call_target="tpu_custom_call", output_to_operand_aliasing={{2}: (9, {})} | custom-call | flops 1020000000 | tf_op jit(solution)/shard_map/pallas_call | solution.py:47
Async XLA Ops:
  0.6 3.6 %collective-permute-start = (bf16[6,2560]{1,0:T(8,128)(2,1)}, bf16[6,2560]{1,0:T(8,128)(2,1)S(1)}, u32[]{:S(2)}, u32[]{:S(2)}) collective-permute-start(bf16[6,2560]{1,0:T(8,128)(2,1)} %refs_6_.1), channel_id=1, source_target_pairs={{0,1},{1,0},{2,3},{3,2},{4,5},{5,4},{6,7},{7,6},{8,9},{9,8},{10,11... | collective-permute-start | bytes 92168 | tf_op jit(solution)/shard_map/ppermute | solution.py:503
  1.2 3.0 %collective-permute-start.1 = (bf16[6,2560]{1,0:T(8,128)(2,1)}, bf16[6,2560]{1,0:T(8,128)(2,1)S(1)}, u32[]{:S(2)}, u32[]{:S(2)}) collective-permute-start(bf16[6,2560]{1,0:T(8,128)(2,1)} %refs_7_.1), channel_id=1, source_target_pairs={{0,1},{1,0},{2,3},{3,2},{4,5},{5,4},{6,7},{7,6},{8,9},{9,8},{10,11... | collective-permute-start | bytes 92168 | tf_op jit(solution)/shard_map/ppermute | solution.py:503
  1.3 7.2 %collective-permute-start.2 = (bf16[6,2560]{1,0:T(8,128)(2,1)}, bf16[6,2560]{1,0:T(8,128)(2,1)S(1)}, u32[]{:S(2)}, u32[]{:S(2)}) collective-permute-start(bf16[6,2560]{1,0:T(8,128)(2,1)} %refs_6_.1), channel_id=1, source_target_pairs={{0,2},{1,3},{2,0},{3,1},{4,6},{5,7},{6,4},{7,5},{8,10},{9,11},{10,... | collective-permute-start | bytes 92168 | tf_op jit(solution)/shard_map/ppermute | solution.py:503
  4.2 4.2 %collective-permute-start.3 = (bf16[6,2560]{1,0:T(8,128)(2,1)}, bf16[6,2560]{1,0:T(8,128)(2,1)S(1)}, u32[]{:S(2)}, u32[]{:S(2)}) collective-permute-start(bf16[6,2560]{1,0:T(8,128)(2,1)} %refs_7_.1), channel_id=1, source_target_pairs={{0,2},{1,3},{2,0},{3,1},{4,6},{5,7},{6,4},{7,5},{8,10},{9,11},{10,... | collective-permute-start | bytes 92168 | tf_op jit(solution)/shard_map/ppermute | solution.py:503
  8.4 1.2 %collective-permute-start.4 = (bf16[6,2560]{1,0:T(8,128)(2,1)S(1)}, bf16[6,2560]{1,0:T(8,128)(2,1)S(1)}, u32[]{:S(2)}, u32[]{:S(2)}) collective-permute-start(bf16[6,2560]{1,0:T(8,128)(2,1)S(1)} %collective-permute-done.2.refs_5_), channel_id=1, source_target_pairs={{0,1},{1,0},{2,3},{3,2},{4,5},{5,4},{6,7},{7,6},{8,9},{9,8},{10,11... | collective-permute-start | bytes 92168 | tf_op jit(solution)/shard_map/ppermute | solution.py:503
  8.4 1.4 %collective-permute-start.5 = (bf16[6,2560]{1,0:T(8,128)(2,1)S(1)}, bf16[6,2560]{1,0:T(8,128)(2,1)S(1)}, u32[]{:S(2)}, u32[]{:S(2)}) collective-permute-start(bf16[6,2560]{1,0:T(8,128)(2,1)S(1)} %collective-permute-done.3.refs_6_), channel_id=1, source_target_pairs={{0,1},{1,0},{2,3},{3,2},{4,5},{5,4},{6,7},{7,6},{8,9},{9,8},{10,11... | collective-permute-start | bytes 92168 | tf_op jit(solution)/shard_map/ppermute | solution.py:503
  12.3 1.4 %collective-permute-start.6 = (bf16[16,4352]{1,0:T(8,128)(2,1)S(1)}, bf16[16,4352]{1,0:T(8,128)(2,1)S(1)}, u32[]{:S(2)}, u32[]{:S(2)}) collective-permute-start(bf16[16,4352]{1,0:T(8,128)(2,1)S(1)} %get-tuple-element.34), channel_id=1, source_target_pairs={{0,1},{1,0},{2,3},{3,2},{4,5},{5,4},{6,7},{7,6},{8,9},{9,8},{10,11... | collective-permute-start | bytes 417800 | tf_op jit(solution)/shard_map/ppermute | solution.py:503
  14.1 9.1 %collective-permute-start.7 = (bf16[16,4352]{1,0:T(8,128)(2,1)S(1)}, bf16[16,4352]{1,0:T(8,128)(2,1)S(1)}, u32[]{:S(2)}, u32[]{:S(2)}) collective-permute-start(bf16[16,4352]{1,0:T(8,128)(2,1)S(1)} %get-tuple-element.37), channel_id=1, source_target_pairs={{0,2},{1,3},{2,0},{3,1},{4,6},{5,7},{6,4},{7,5},{8,10},{9,11},{10,... | collective-permute-start | bytes 417800 | tf_op jit(solution)/shard_map/ppermute | solution.py:503
  15.3 11.9 %collective-permute-start.9 = (bf16[2,2,16,1024]{3,2,1,0:T(8,128)(2,1)S(1)}, bf16[2,2,16,1024]{3,2,1,0:T(8,128)(2,1)S(1)}, u32[]{:S(2)}, u32[]{:S(2)}) collective-permute-start(bf16[2,2,16,1024]{3,2,1,0:T(8,128)(2,1)S(1)} %get-tuple-element.45), channel_id=1, source_target_pairs={{0,4},{4,0},{8,12},{12,8},{1,5},{5,1},{9,13},{13,9},{2,6},{6,2},{1... | collective-permute-start | bytes 393224 | tf_op jit(solution)/shard_map/ppermute | solution.py:553
  16.9 12.9 %collective-permute-start.10 = (bf16[2,2,16,1024]{3,2,1,0:T(8,128)(2,1)S(1)}, bf16[2,2,16,1024]{3,2,1,0:T(8,128)(2,1)S(1)}, u32[]{:S(2)}, u32[]{:S(2)}) collective-permute-start(bf16[2,2,16,1024]{3,2,1,0:T(8,128)(2,1)S(1)} %get-tuple-element.46), channel_id=1, source_target_pairs={{0,8},{4,12},{8,0},{12,4},{1,9},{5,13},{9,1},{13,5},{2,10},{6,14},... | collective-permute-start | bytes 393224 | tf_op jit(solution)/shard_map/ppermute | solution.py:553
  19.5 10.3 %collective-permute-start.11 = (bf16[2,2,16,1024]{3,2,1,0:T(8,128)(2,1)S(1)}, bf16[2,2,16,1024]{3,2,1,0:T(8,128)(2,1)S(1)}, u32[]{:S(2)}, u32[]{:S(2)}) collective-permute-start(bf16[2,2,16,1024]{3,2,1,0:T(8,128)(2,1)S(1)} %get-tuple-element.47), channel_id=1, source_target_pairs={{0,12},{4,8},{8,4},{12,0},{1,13},{5,9},{9,5},{13,1},{2,14},{6,10},... | collective-permute-start | bytes 393224 | tf_op jit(solution)/shard_map/ppermute | solution.py:553
  23.7 6.1 %collective-permute-start.8 = (bf16[16,4096]{1,0:T(8,128)(2,1)S(1)}, bf16[16,4096]{1,0:T(8,128)(2,1)S(1)}, u32[]{:S(2)}, u32[]{:S(2)}) collective-permute-start(bf16[16,4096]{1,0:T(8,128)(2,1)S(1)} %shard_map.107.refs_1_), channel_id=1, source_target_pairs={{0,1},{1,0},{2,3},{3,2},{4,5},{5,4},{6,7},{7,6},{8,9},{9,8},{10,11... | collective-permute-start | bytes 393224 | tf_op jit(solution)/shard_map/ppermute | solution.py:503

commit v3 on v2

--- a/solution.py
+++ b/solution.py
@@ -16,7 +16,8 @@
 I32 = jnp.int32
 VMEM = pltpu.VMEM
 HBM = pltpu.HBM
-TILE = 256
+TILE = 512
+WIDE = 1024
 PARTS = 1
 CHUNKS = 8
 FLOPS = 3e8
@@ -412,10 +413,12 @@
         copy.wait()
 
 
-def column_tiles(width, body):
-    @pl.loop(0, width // TILE)
+def column_tiles(width, body, tile=TILE):
+    tile = min(tile, width)
+
+    @pl.loop(0, width // tile)
     def _(t):
-        body(pl.ds(pl.multiple_of(t * TILE, TILE), TILE))
+        body(pl.ds(pl.multiple_of(t * tile, tile), tile))
 
 
 def product(z, mixed, weights, columns, first=0):
@@ -485,7 +488,7 @@
                 first_ref[:, columns] = total[: z.rows_of].astype(BF16)
                 second_ref[:, columns] = total[z.step_rows : z.step_rows + z.rows_of].astype(BF16)
 
-        column_tiles(z.out_columns, body)
+        column_tiles(z.out_columns, body, min(WIDE, z.out_columns))
     placed(lambda copy: copy.wait())
 
 
@@ -586,11 +589,11 @@
         )
     theirs = swap(send, stages[-1])
     weights += run(
-        functools.partial(stage_kernel, (2, 3)),
+        functools.partial(stage_kernel, (2, 3, 4)),
         3,
         [HBM],
-        [chunk] * 2,
-        [dma((2,))],
+        [chunk] * 3,
+        [dma((3,))],
         [w_hbm],
         after=[stats],
     )
@@ -605,27 +608,28 @@
     )
     other = swap(mixed, 1)
     total, *held = run(
-        functools.partial(project_kernel, z, (4, 5)),
+        functools.partial(project_kernel, z, (5, 6)),
         3.4,
         [HBM] + [VMEM] * (1 + CHUNKS // 2),
         [(shape((z.all_rows, z.out_columns), F32), VMEM)] + [chunk] * 2,
         [dma((2,))],
-        [w_hbm, mixed, *weights],
-    )
+        [w_hbm, mixed, *weights[:-1]],
+    )
+    held = weights[-1:] + held
     return tuple(
         run(
-            functools.partial(last_kernel, z, 2, (6, 7)),
+            functools.partial(last_kernel, z, 3, (7,)),
             3.4,
-            [HBM] + [VMEM] * (4 + inst_count) + [HBM],
+            [HBM] + [VMEM] * (5 + inst_count) + [HBM],
             [(shape((rows_of, z.out_columns)), VMEM)] * 2 + [(shape(kv_cache.shape), HBM)],
             [
-                pltpu.VMEM((2, z.chunk_rows, z.out_columns), BF16),
+                pltpu.VMEM((1, z.chunk_rows, z.out_columns), BF16),
                 pltpu.VMEM((z.all_rows, z.out_columns), F32),
                 smem((z.plan_rows, LANES), I32),
-                dma((4,)),
+                dma((3,)),
             ],
             [w_hbm, total, other, plan, *held, *arrived, kv_mid],
-            aliases={5 + inst_count: 2},
+            aliases={6 + inst_count: 2},
             limit=12,
         )
     )

time: 36.4 us -> 34.1 us (0.937)
  waiting for transfers between devices: 5.27 us -> 4.06 us
  Pallas kernels: 20 us -> 18.9 us
    ppermute x3, waiting for transfers between devices: 2.47 us -> 1.27 us  [steps(): lax.ppermute(outgoing[s - 1], 'inst', [(i, i ^ s) for i in range(inst_cou...]
    pallas_call x7, Pallas kernels: 20 us -> 18.9 us  [run(): pl.pallas_call(body, out_shape=tuple((s for s, _ in outs)), in_specs=[spe...]
  transfers between devices with their start and end apart: 12 -> 12, of which waited for: 5 -> 5; matrix products, arithmetic and copies ran while one was open for 0% -> 0% of each run, Pallas kernels for 30% -> 35%
where the time goes in v3:
time: 34.1 us; the launch traced here: 33.9 us
  Pallas kernels  18.9 us (55%)
  starting transfers between devices  10.2 us (30%)
  waiting for transfers between devices  4.06 us (12%)
  between operations  0.71 us (2%)
    pallas_call x7, Pallas kernels, run(): pl.pallas_call(body, out_shape=tuple((s for s, _ in outs)), in_specs=[spe...  18.9 us
    ppermute x9, starting transfers between devices, swap(): return lax.ppermute(x, 'tp', [(i, i ^ d) for i in range(n)])  5.84 us
    ppermute x3, starting transfers between devices, steps(): lax.ppermute(outgoing[s - 1], 'inst', [(i, i ^ s) for i in range(inst_cou...  4.39 us
    ppermute x9, waiting for transfers between devices, swap(): return lax.ppermute(x, 'tp', [(i, i ^ d) for i in range(n)])  2.79 us
    ppermute x3, waiting for transfers between devices, steps(): lax.ppermute(outgoing[s - 1], 'inst', [(i, i ^ s) for i in range(inst_cou...  1.27 us
  transfers between devices with their start and end apart: 12, of which 5 were waited for; matrix products, arithmetic and copies ran while one was open for 0% of the time, Pallas kernels for 35%

profile of v3, /device:TPU:0, one launch (start us, length us, event | category | flops | bytes accessed | tf_op | source)
XLA Modules:
  0.0 33.9 jit_solution(3448038998729547549)
XLA Ops:
  0.6 0.6 %collective-permute-start = (bf16[6,2560]{1,0:T(8,128)(2,1)}, bf16[6,2560]{1,0:T(8,128)(2,1)S(1)}, u32[]{:S(2)}, u32[]{:S(2)}) collective-permute-start(bf16[6,2560]{1,0:T(8,128)(2,1)} %refs_6_.1), channel_id=1, source_target_pairs={{0,1},{1,0},{2,3},{3,2},{4,5},{5,4},{6,7},{7,6},{8,9},{9,8},{10,11... | collective-permute-start | bytes 92168 | tf_op jit(solution)/shard_map/ppermute | solution.py:506
  1.2 0.1 collective-permute-start.1
  1.3 2.9 %collective-permute-start.2 = (bf16[6,2560]{1,0:T(8,128)(2,1)}, bf16[6,2560]{1,0:T(8,128)(2,1)S(1)}, u32[]{:S(2)}, u32[]{:S(2)}) collective-permute-start(bf16[6,2560]{1,0:T(8,128)(2,1)} %refs_6_.1), channel_id=1, source_target_pairs={{0,2},{1,3},{2,0},{3,1},{4,6},{5,7},{6,4},{7,5},{8,10},{9,11},{10,... | collective-permute-start | bytes 92168 | tf_op jit(solution)/shard_map/ppermute | solution.py:506
  4.2 0.0 collective-permute-start.3
  4.2 0.0 collective-permute-done.refs_8_
  4.2 0.0 collective-permute-done.1.refs_9_
  4.2 3.3 %shard_map.103 = (bf16[18,2,16,1024]{3,2,1,0:T(8,128)(2,1)S(1)}, bf16[16,10240]{1,0:T(8,128)(2,1)S(1)}, s32[16,256]{1,0:T(8,128)S(1)}, s32[8,128]{1,0:T(8,128)S(...) custom-call(bf16[8192,2048]{1,0:T(8,128)(2,1)} %refs_0_.9, ...), custom_call_target="tpu_custom_call" | custom-call | flops 600000000 | tf_op jit(solution)/shard_map/pallas_call | solution.py:48
  7.5 0.9 %collective-permute-done.3.refs_6_ = bf16[6,2560]{1,0:T(8,128)(2,1)S(1)} collective-permute-done((bf16[6,2560]{1,0:T(8,128)(2,1)}, bf16[6,2560]{1,0:T(8,128)(2,1)S(1)}, u32[]{:S(2)}, u32[]{:S(2)}) %collective-permute-start.3) | collective-permute-done | bytes 30752 | tf_op jit(solution)/shard_map/ppermute | solution.py:506
  8.4 0.0 collective-permute-done.2.refs_5_
  8.4 0.0 collective-permute-start.4
  8.4 0.5 %collective-permute-start.5 = (bf16[6,2560]{1,0:T(8,128)(2,1)S(1)}, bf16[6,2560]{1,0:T(8,128)(2,1)S(1)}, u32[]{:S(2)}, u32[]{:S(2)}) collective-permute-start(bf16[6,2560]{1,0:T(8,128)(2,1)S(1)} %collective-permute-done.3.refs_6_), channel_id=1, source_target_pairs={{0,1},{1,0},{2,3},{3,2},{4,5},{5,4},{6,7},{7,6},{8,9},{9,8},{10,11... | collective-permute-start | bytes 92168 | tf_op jit(solution)/shard_map/ppermute | solution.py:506
  8.9 0.7 %collective-permute-done.4.refs_7_ = bf16[6,2560]{1,0:T(8,128)(2,1)S(1)} collective-permute-done((bf16[6,2560]{1,0:T(8,128)(2,1)S(1)}, bf16[6,2560]{1,0:T(8,128)(2,1)S(1)}, u32[]{:S(2)}, u32[]{:S(2)}) %collective-permute-start.4) | collective-permute-done | bytes 30752 | tf_op jit(solution)/shard_map/ppermute | solution.py:506
  9.6 0.2 collective-permute-done.5.refs_8_
  9.8 2.5 %shard_map.104 = (bf16[16,4352]{1,0:T(8,128)(2,1)S(1)}, f32[16,4096]{1,0:T(8,128)S(1)}, f32[16,128]{1,0:T(8,128)S(1)}, bf16[16,10240]{1,0:T(8,128)(2,1)S(1)}, bf...) custom-call(bf16[8192,2048]{1,0:T(8,128)(2,1)} %refs_0_.9, ...), custom_call_target="tpu_custom_call", output_to_operand_aliasing={{4}: (3, {}), {3}: (4, {})} | custom-call | flops 600000000 | tf_op jit(solution)/shard_map/pallas_call | solution.py:48
  12.3 0.4 %collective-permute-start.6 = (bf16[16,4352]{1,0:T(8,128)(2,1)S(1)}, bf16[16,4352]{1,0:T(8,128)(2,1)S(1)}, u32[]{:S(2)}, u32[]{:S(2)}) collective-permute-start(bf16[16,4352]{1,0:T(8,128)(2,1)S(1)} %get-tuple-element.35), channel_id=1, source_target_pairs={{0,1},{1,0},{2,3},{3,2},{4,5},{5,4},{6,7},{7,6},{8,9},{9,8},{10,11... | collective-permute-start | bytes 417800 | tf_op jit(solution)/shard_map/ppermute | solution.py:506
  12.7 1.0 %collective-permute-done.6.refs_2_ = bf16[16,4352]{1,0:T(8,128)(2,1)S(1)} collective-permute-done((bf16[16,4352]{1,0:T(8,128)(2,1)S(1)}, bf16[16,4352]{1,0:T(8,128)(2,1)S(1)}, u32[]{:S(2)}, u32[]{:S(2)}) %collective-permute-start.6) | collective-permute-done | bytes 139296 | tf_op jit(solution)/shard_map/ppermute | solution.py:506
  13.7 0.3 shard_map.105
  14.1 1.3 %collective-permute-start.7 = (bf16[16,4352]{1,0:T(8,128)(2,1)S(1)}, bf16[16,4352]{1,0:T(8,128)(2,1)S(1)}, u32[]{:S(2)}, u32[]{:S(2)}) collective-permute-start(bf16[16,4352]{1,0:T(8,128)(2,1)S(1)} %get-tuple-element.38), channel_id=1, source_target_pairs={{0,2},{1,3},{2,0},{3,1},{4,6},{5,7},{6,4},{7,5},{8,10},{9,11},{10,... | collective-permute-start | bytes 417800 | tf_op jit(solution)/shard_map/ppermute | solution.py:506
  15.3 1.5 %collective-permute-start.9 = (bf16[2,2,16,1024]{3,2,1,0:T(8,128)(2,1)S(1)}, bf16[2,2,16,1024]{3,2,1,0:T(8,128)(2,1)S(1)}, u32[]{:S(2)}, u32[]{:S(2)}) collective-permute-start(bf16[2,2,16,1024]{3,2,1,0:T(8,128)(2,1)S(1)} %get-tuple-element.47), channel_id=1, source_target_pairs={{0,4},{4,0},{8,12},{12,8},{1,5},{5,1},{9,13},{13,9},{2,6},{6,2},{1... | collective-permute-start | bytes 393224 | tf_op jit(solution)/shard_map/ppermute | solution.py:556
  16.9 2.6 %collective-permute-start.10 = (bf16[2,2,16,1024]{3,2,1,0:T(8,128)(2,1)S(1)}, bf16[2,2,16,1024]{3,2,1,0:T(8,128)(2,1)S(1)}, u32[]{:S(2)}, u32[]{:S(2)}) collective-permute-start(bf16[2,2,16,1024]{3,2,1,0:T(8,128)(2,1)S(1)} %get-tuple-element.48), channel_id=1, source_target_pairs={{0,8},{4,12},{8,0},{12,4},{1,9},{5,13},{9,1},{13,5},{2,10},{6,14},... | collective-permute-start | bytes 393224 | tf_op jit(solution)/shard_map/ppermute | solution.py:556
  19.5 0.2 collective-permute-start.11
  19.7 4.7 %shard_map.106 = (bf16[1024,2048]{1,0:T(8,128)(2,1)S(1)}, bf16[1024,2048]{1,0:T(8,128)(2,1)S(1)}, bf16[1024,2048]{1,0:T(8,128)(2,1)S(1)}) custom-call(bf16[8192,2048]{1,0:T(8,128)(2,1)} %refs_0_.9, f32[16,128]{1,0:T(8,128)S(1)} %get-tuple-element.37.refs_1_), custom_call_target="tpu_custom_call" | custom-call | flops 900000000 | tf_op jit(solution)/shard_map/pallas_call | solution.py:48
  24.4 0.0 collective-permute-done.7.refs_2_
  24.4 0.5 %shard_map.107.refs_1_ = bf16[16,4096]{1,0:T(8,128)(2,1)S(1)} custom-call(f32[16,4096]{1,0:T(8,128)S(1)} %get-tuple-element.36.refs_0_, f32[16,128]{1,0:T(8,128)S(1)} %get-tuple-element.37.refs_1_, bf16[16,4352]{1,0:T(8,128)(2,1)S(1)} %collective-permute-done.7.refs_2_, bf16[1024,2048]{1,0:T(8,128)(2,1)S(1)} %get-tuple-element.39.refs_3_.refs_4_), custom_call_target="tpu_custom_call" | custom-call | flops 90000000 | tf_op jit(solution)/shard_map/pallas_call | solution.py:48
  24.9 0.1 collective-permute-start.8
  25.0 3.5 %shard_map.108 = (f32[16,2048]{1,0:T(8,128)S(1)}, bf16[1024,2048]{1,0:T(8,128)(2,1)S(1)}, bf16[1024,2048]{1,0:T(8,128)(2,1)S(1)}) custom-call(bf16[8192,2048]{1,0:T(8,128)(2,1)} %refs_0_.9, bf16[16,4096]{1,0:T(8,128)(2,1)S(1)} %shard_map.107.refs_1_, bf16[1024,2048]{1,0:T(8,128)(2,1)S(1)} %get-tuple-element.40.refs_2_, ...), custom_call_target="tpu_custom_call" | custom-call | flops 1020000000 | tf_op jit(solution)/shard_map/pallas_call | solution.py:48
  28.5 0.0 collective-permute-done.9.refs_7_
  28.5 1.3 %collective-permute-done.10.refs_8_ = bf16[2,2,16,1024]{3,2,1,0:T(8,128)(2,1)S(1)} collective-permute-done((bf16[2,2,16,1024]{3,2,1,0:T(8,128)(2,1)S(1)}, bf16[2,2,16,1024]{3,2,1,0:T(8,128)(2,1)S(1)}, u32[]{:S(2)}, u32[]{:S(2)}) %collective-permute-start.10) | collective-permute-done | bytes 131104 | tf_op jit(solution)/shard_map/ppermute | solution.py:556
  29.8 0.0 collective-permute-done.11.refs_9_
  29.8 0.0 collective-permute-done.8.refs_2_
  29.8 4.2 %shard_map.109 = (bf16[6,2048]{1,0:T(8,128)(2,1)}, bf16[6,2048]{1,0:T(8,128)(2,1)}, bf16[16,2,16,1024]{3,2,1,0:T(8,128)(2,1)}) custom-call(bf16[8192,2048]{1,0:T(8,128)(2,1)} %refs_0_.9, f32[16,2048]{1,0:T(8,128)S(1)} %get-tuple-element.44.refs_1_, bf16[16,4096]{1,0:T(8,128)(2,1)S(1)} %collective-permute-done.8.refs_2_, ...), custom_call_target="tpu_custom_call", output_to_operand_aliasing={{2}: (10, {})} | custom-call | flops 1020000000 | tf_op jit(solution)/shard_map/pallas_call | solution.py:48
Async XLA Ops:
  0.6 3.6 %collective-permute-start = (bf16[6,2560]{1,0:T(8,128)(2,1)}, bf16[6,2560]{1,0:T(8,128)(2,1)S(1)}, u32[]{:S(2)}, u32[]{:S(2)}) collective-permute-start(bf16[6,2560]{1,0:T(8,128)(2,1)} %refs_6_.1), channel_id=1, source_target_pairs={{0,1},{1,0},{2,3},{3,2},{4,5},{5,4},{6,7},{7,6},{8,9},{9,8},{10,11... | collective-permute-start | bytes 92168 | tf_op jit(solution)/shard_map/ppermute | solution.py:506
  1.2 3.0 %collective-permute-start.1 = (bf16[6,2560]{1,0:T(8,128)(2,1)}, bf16[6,2560]{1,0:T(8,128)(2,1)S(1)}, u32[]{:S(2)}, u32[]{:S(2)}) collective-permute-start(bf16[6,2560]{1,0:T(8,128)(2,1)} %refs_7_.1), channel_id=1, source_target_pairs={{0,1},{1,0},{2,3},{3,2},{4,5},{5,4},{6,7},{7,6},{8,9},{9,8},{10,11... | collective-permute-start | bytes 92168 | tf_op jit(solution)/shard_map/ppermute | solution.py:506
  1.3 7.2 %collective-permute-start.2 = (bf16[6,2560]{1,0:T(8,128)(2,1)}, bf16[6,2560]{1,0:T(8,128)(2,1)S(1)}, u32[]{:S(2)}, u32[]{:S(2)}) collective-permute-start(bf16[6,2560]{1,0:T(8,128)(2,1)} %refs_6_.1), channel_id=1, source_target_pairs={{0,2},{1,3},{2,0},{3,1},{4,6},{5,7},{6,4},{7,5},{8,10},{9,11},{10,... | collective-permute-start | bytes 92168 | tf_op jit(solution)/shard_map/ppermute | solution.py:506
  4.2 4.2 %collective-permute-start.3 = (bf16[6,2560]{1,0:T(8,128)(2,1)}, bf16[6,2560]{1,0:T(8,128)(2,1)S(1)}, u32[]{:S(2)}, u32[]{:S(2)}) collective-permute-start(bf16[6,2560]{1,0:T(8,128)(2,1)} %refs_7_.1), channel_id=1, source_target_pairs={{0,2},{1,3},{2,0},{3,1},{4,6},{5,7},{6,4},{7,5},{8,10},{9,11},{10,... | collective-permute-start | bytes 92168 | tf_op jit(solution)/shard_map/ppermute | solution.py:506
  8.4 1.2 %collective-permute-start.4 = (bf16[6,2560]{1,0:T(8,128)(2,1)S(1)}, bf16[6,2560]{1,0:T(8,128)(2,1)S(1)}, u32[]{:S(2)}, u32[]{:S(2)}) collective-permute-start(bf16[6,2560]{1,0:T(8,128)(2,1)S(1)} %collective-permute-done.2.refs_5_), channel_id=1, source_target_pairs={{0,1},{1,0},{2,3},{3,2},{4,5},{5,4},{6,7},{7,6},{8,9},{9,8},{10,11... | collective-permute-start | bytes 92168 | tf_op jit(solution)/shard_map/ppermute | solution.py:506
  8.4 1.4 %collective-permute-start.5 = (bf16[6,2560]{1,0:T(8,128)(2,1)S(1)}, bf16[6,2560]{1,0:T(8,128)(2,1)S(1)}, u32[]{:S(2)}, u32[]{:S(2)}) collective-permute-start(bf16[6,2560]{1,0:T(8,128)(2,1)S(1)} %collective-permute-done.3.refs_6_), channel_id=1, source_target_pairs={{0,1},{1,0},{2,3},{3,2},{4,5},{5,4},{6,7},{7,6},{8,9},{9,8},{10,11... | collective-permute-start | bytes 92168 | tf_op jit(solution)/shard_map/ppermute | solution.py:506
  12.3 1.4 %collective-permute-start.6 = (bf16[16,4352]{1,0:T(8,128)(2,1)S(1)}, bf16[16,4352]{1,0:T(8,128)(2,1)S(1)}, u32[]{:S(2)}, u32[]{:S(2)}) collective-permute-start(bf16[16,4352]{1,0:T(8,128)(2,1)S(1)} %get-tuple-element.35), channel_id=1, source_target_pairs={{0,1},{1,0},{2,3},{3,2},{4,5},{5,4},{6,7},{7,6},{8,9},{9,8},{10,11... | collective-permute-start | bytes 417800 | tf_op jit(solution)/shard_map/ppermute | solution.py:506
  14.1 10.3 %collective-permute-start.7 = (bf16[16,4352]{1,0:T(8,128)(2,1)S(1)}, bf16[16,4352]{1,0:T(8,128)(2,1)S(1)}, u32[]{:S(2)}, u32[]{:S(2)}) collective-permute-start(bf16[16,4352]{1,0:T(8,128)(2,1)S(1)} %get-tuple-element.38), channel_id=1, source_target_pairs={{0,2},{1,3},{2,0},{3,1},{4,6},{5,7},{6,4},{7,5},{8,10},{9,11},{10,... | collective-permute-start | bytes 417800 | tf_op jit(solution)/shard_map/ppermute | solution.py:506
  15.3 13.1 %collective-permute-start.9 = (bf16[2,2,16,1024]{3,2,1,0:T(8,128)(2,1)S(1)}, bf16[2,2,16,1024]{3,2,1,0:T(8,128)(2,1)S(1)}, u32[]{:S(2)}, u32[]{:S(2)}) collective-permute-start(bf16[2,2,16,1024]{3,2,1,0:T(8,128)(2,1)S(1)} %get-tuple-element.47), channel_id=1, source_target_pairs={{0,4},{4,0},{8,12},{12,8},{1,5},{5,1},{9,13},{13,9},{2,6},{6,2},{1... | collective-permute-start | bytes 393224 | tf_op jit(solution)/shard_map/ppermute | solution.py:556
  16.9 12.9 %collective-permute-start.10 = (bf16[2,2,16,1024]{3,2,1,0:T(8,128)(2,1)S(1)}, bf16[2,2,16,1024]{3,2,1,0:T(8,128)(2,1)S(1)}, u32[]{:S(2)}, u32[]{:S(2)}) collective-permute-start(bf16[2,2,16,1024]{3,2,1,0:T(8,128)(2,1)S(1)} %get-tuple-element.48), channel_id=1, source_target_pairs={{0,8},{4,12},{8,0},{12,4},{1,9},{5,13},{9,1},{13,5},{2,10},{6,14},... | collective-permute-start | bytes 393224 | tf_op jit(solution)/shard_map/ppermute | solution.py:556
  19.5 10.3 %collective-permute-start.11 = (bf16[2,2,16,1024]{3,2,1,0:T(8,128)(2,1)S(1)}, bf16[2,2,16,1024]{3,2,1,0:T(8,128)(2,1)S(1)}, u32[]{:S(2)}, u32[]{:S(2)}) collective-permute-start(bf16[2,2,16,1024]{3,2,1,0:T(8,128)(2,1)S(1)} %get-tuple-element.49), channel_id=1, source_target_pairs={{0,12},{4,8},{8,4},{12,0},{1,13},{5,9},{9,5},{13,1},{2,14},{6,10},... | collective-permute-start | bytes 393224 | tf_op jit(solution)/shard_map/ppermute | solution.py:556
  24.9 4.9 %collective-permute-start.8 = (bf16[16,4096]{1,0:T(8,128)(2,1)S(1)}, bf16[16,4096]{1,0:T(8,128)(2,1)S(1)}, u32[]{:S(2)}, u32[]{:S(2)}) collective-permute-start(bf16[16,4096]{1,0:T(8,128)(2,1)S(1)} %shard_map.107.refs_1_), channel_id=1, source_target_pairs={{0,1},{1,0},{2,3},{3,2},{4,5},{5,4},{6,7},{7,6},{8,9},{9,8},{10,11... | collective-permute-start | bytes 393224 | tf_op jit(solution)/shard_map/ppermute | solution.py:506

commit v4 on v3

--- a/solution.py
+++ b/solution.py
@@ -19,6 +19,7 @@
 TILE = 512
 WIDE = 1024
 PARTS = 1
+PREPARE = 0.05
 CHUNKS = 8
 FLOPS = 3e8
 BYTES = 0
@@ -460,7 +461,6 @@
     loads = w_copies(w_hbm, chunks, late_refs, sems, 2)
     for copy in loads:
         copy.start()
-    plan_copy.wait()
 
     def placed(act):
         for s in range(z.inst_count - 1):
@@ -471,12 +471,12 @@
                 def _():
                     act(copy_of(arrived[s].at[j], kv_out.at[slot], sems.at[1]))
 
-    placed(lambda copy: copy.start())
-
     def early(columns):
         acc[:, columns] = acc_in[:, columns] + product(z, mixed, weights, columns)
 
     column_tiles(z.out_columns, early)
+    plan_copy.wait()
+    placed(lambda copy: copy.start())
     for i, copy in enumerate(loads):
         copy.wait()
 
@@ -519,7 +519,7 @@
         have[d] = tuple(swap(x, d) for x in have[0])
     pages, rows, visible, plan, *more = run(
         functools.partial(prepare_kernel, z, (0,)),
-        2,
+        PREPARE,
         [HBM] * 8 + [VMEM] * (2 * z.early - 2),
         [
             (shape((z.pool + 2,) + page), VMEM),
@@ -575,6 +575,7 @@
     )
     weights += loaded
     for d in stages[:-1]:
+        theirs = swap(send, d)
         acc, stats, send = run(
             functools.partial(merge_kernel, z),
             0.2,
@@ -585,7 +586,7 @@
                 (shape((z.all_rows, z.packed)), VMEM),
             ],
             [],
-            [acc, stats, swap(send, d)],
+            [acc, stats, theirs],
         )
     theirs = swap(send, stages[-1])
     weights += run(

time: 34.1 us -> 33.6 us (0.985)
  Pallas kernels: 18.9 us -> 18.4 us
    pallas_call x7, Pallas kernels: 18.9 us -> 18.4 us  [run(): pl.pallas_call(body, out_shape=tuple((s for s, _ in outs)), in_specs=[spe...]
  transfers between devices with their start and end apart: 12 -> 12, of which waited for: 5 -> 5; matrix products, arithmetic and copies ran while one was open for 0% -> 0% of each run, Pallas kernels for 35% -> 36%
where the time goes in v4:
time: 33.6 us; the launch traced here: 33.4 us
  Pallas kernels  18.4 us (55%)
  starting transfers between devices  10.2 us (30%)
  waiting for transfers between devices  4.05 us (12%)
  between operations  0.72 us (2%)
    pallas_call x7, Pallas kernels, run(): pl.pallas_call(body, out_shape=tuple((s for s, _ in outs)), in_specs=[spe...  18.4 us
    ppermute x9, starting transfers between devices, swap(): return lax.ppermute(x, 'tp', [(i, i ^ d) for i in range(n)])  5.84 us
    ppermute x3, starting transfers between devices, steps(): lax.ppermute(outgoing[s - 1], 'inst', [(i, i ^ s) for i in range(inst_cou...  4.39 us
    ppermute x9, waiting for transfers between devices, swap(): return lax.ppermute(x, 'tp', [(i, i ^ d) for i in range(n)])  2.78 us
    ppermute x3, waiting for transfers between devices, steps(): lax.ppermute(outgoing[s - 1], 'inst', [(i, i ^ s) for i in range(inst_cou...  1.27 us
  transfers between devices with their start and end apart: 12, of which 5 were waited for; matrix products, arithmetic and copies ran while one was open for 0% of the time, Pallas kernels for 36%

profile of v4, /device:TPU:0, one launch (start us, length us, event | category | flops | bytes accessed | tf_op | source)
XLA Modules:
  0.0 33.4 jit_solution(11510795060166183609)
XLA Ops:
  0.6 0.6 %collective-permute-start = (bf16[6,2560]{1,0:T(8,128)(2,1)}, bf16[6,2560]{1,0:T(8,128)(2,1)S(1)}, u32[]{:S(2)}, u32[]{:S(2)}) collective-permute-start(bf16[6,2560]{1,0:T(8,128)(2,1)} %refs_6_.1), channel_id=1, source_target_pairs={{0,1},{1,0},{2,3},{3,2},{4,5},{5,4},{6,7},{7,6},{8,9},{9,8},{10,11... | collective-permute-start | bytes 92168 | tf_op jit(solution)/shard_map/ppermute | solution.py:506
  1.2 0.1 collective-permute-start.1
  1.3 2.9 %collective-permute-start.3 = (bf16[6,2560]{1,0:T(8,128)(2,1)}, bf16[6,2560]{1,0:T(8,128)(2,1)S(1)}, u32[]{:S(2)}, u32[]{:S(2)}) collective-permute-start(bf16[6,2560]{1,0:T(8,128)(2,1)} %refs_7_.1), channel_id=1, source_target_pairs={{0,2},{1,3},{2,0},{3,1},{4,6},{5,7},{6,4},{7,5},{8,10},{9,11},{10,... | collective-permute-start | bytes 92168 | tf_op jit(solution)/shard_map/ppermute | solution.py:506
  4.2 0.0 collective-permute-start.2
  4.2 0.0 collective-permute-done.refs_8_
  4.2 0.0 collective-permute-done.1.refs_9_
  4.2 3.3 %shard_map.103 = (bf16[18,2,16,1024]{3,2,1,0:T(8,128)(2,1)S(1)}, bf16[16,10240]{1,0:T(8,128)(2,1)S(1)}, s32[16,256]{1,0:T(8,128)S(1)}, s32[8,128]{1,0:T(8,128)S(...) custom-call(bf16[8192,2048]{1,0:T(8,128)(2,1)} %refs_0_.9, ...), custom_call_target="tpu_custom_call" | custom-call | flops 15000000 | tf_op jit(solution)/shard_map/pallas_call | solution.py:49
  7.5 0.0 collective-permute-done.3.refs_6_
  7.5 0.9 %collective-permute-done.2.refs_5_ = bf16[6,2560]{1,0:T(8,128)(2,1)S(1)} collective-permute-done((bf16[6,2560]{1,0:T(8,128)(2,1)}, bf16[6,2560]{1,0:T(8,128)(2,1)S(1)}, u32[]{:S(2)}, u32[]{:S(2)}) %collective-permute-start.2) | collective-permute-done | bytes 30752 | tf_op jit(solution)/shard_map/ppermute | solution.py:506
  8.4 0.0 collective-permute-start.4
  8.4 0.5 %collective-permute-start.5 = (bf16[6,2560]{1,0:T(8,128)(2,1)S(1)}, bf16[6,2560]{1,0:T(8,128)(2,1)S(1)}, u32[]{:S(2)}, u32[]{:S(2)}) collective-permute-start(bf16[6,2560]{1,0:T(8,128)(2,1)S(1)} %collective-permute-done.3.refs_6_), channel_id=1, source_target_pairs={{0,1},{1,0},{2,3},{3,2},{4,5},{5,4},{6,7},{7,6},{8,9},{9,8},{10,11... | collective-permute-start | bytes 92168 | tf_op jit(solution)/shard_map/ppermute | solution.py:506
  8.9 0.7 %collective-permute-done.4.refs_7_ = bf16[6,2560]{1,0:T(8,128)(2,1)S(1)} collective-permute-done((bf16[6,2560]{1,0:T(8,128)(2,1)S(1)}, bf16[6,2560]{1,0:T(8,128)(2,1)S(1)}, u32[]{:S(2)}, u32[]{:S(2)}) %collective-permute-start.4) | collective-permute-done | bytes 30752 | tf_op jit(solution)/shard_map/ppermute | solution.py:506
  9.6 0.2 collective-permute-done.5.refs_8_
  9.8 2.5 %shard_map.104 = (bf16[16,4352]{1,0:T(8,128)(2,1)S(1)}, f32[16,4096]{1,0:T(8,128)S(1)}, f32[16,128]{1,0:T(8,128)S(1)}, bf16[16,10240]{1,0:T(8,128)(2,1)S(1)}, bf...) custom-call(bf16[8192,2048]{1,0:T(8,128)(2,1)} %refs_0_.9, ...), custom_call_target="tpu_custom_call", output_to_operand_aliasing={{4}: (3, {}), {3}: (4, {})} | custom-call | flops 600000000 | tf_op jit(solution)/shard_map/pallas_call | solution.py:49
  12.3 0.4 %collective-permute-start.6 = (bf16[16,4352]{1,0:T(8,128)(2,1)S(1)}, bf16[16,4352]{1,0:T(8,128)(2,1)S(1)}, u32[]{:S(2)}, u32[]{:S(2)}) collective-permute-start(bf16[16,4352]{1,0:T(8,128)(2,1)S(1)} %get-tuple-element.35), channel_id=1, source_target_pairs={{0,1},{1,0},{2,3},{3,2},{4,5},{5,4},{6,7},{7,6},{8,9},{9,8},{10,11... | collective-permute-start | bytes 417800 | tf_op jit(solution)/shard_map/ppermute | solution.py:506
  12.7 1.0 %collective-permute-done.6.refs_2_ = bf16[16,4352]{1,0:T(8,128)(2,1)S(1)} collective-permute-done((bf16[16,4352]{1,0:T(8,128)(2,1)S(1)}, bf16[16,4352]{1,0:T(8,128)(2,1)S(1)}, u32[]{:S(2)}, u32[]{:S(2)}) %collective-permute-start.6) | collective-permute-done | bytes 139296 | tf_op jit(solution)/shard_map/ppermute | solution.py:506
  13.7 0.3 %shard_map.105 = (f32[16,4096]{1,0:T(8,128)S(1)}, f32[16,128]{1,0:T(8,128)S(1)}, bf16[16,4352]{1,0:T(8,128)(2,1)S(1)}) custom-call(f32[16,4096]{1,0:T(8,128)S(1)} %get-tuple-element.33.refs_0_, f32[16,128]{1,0:T(8,128)S(1)} %get-tuple-element.34.refs_1_, bf16[16,4352]{1,0:T(8,128)(2,1)S(1)} %collective-permute-done.6.refs_2_), custom_call_target="tpu_custom_call" | custom-call | flops 60000000 | tf_op jit(solution)/shard_map/pallas_call | solution.py:49
  14.1 1.3 %collective-permute-start.7 = (bf16[16,4352]{1,0:T(8,128)(2,1)S(1)}, bf16[16,4352]{1,0:T(8,128)(2,1)S(1)}, u32[]{:S(2)}, u32[]{:S(2)}) collective-permute-start(bf16[16,4352]{1,0:T(8,128)(2,1)S(1)} %get-tuple-element.38), channel_id=1, source_target_pairs={{0,2},{1,3},{2,0},{3,1},{4,6},{5,7},{6,4},{7,5},{8,10},{9,11},{10,... | collective-permute-start | bytes 417800 | tf_op jit(solution)/shard_map/ppermute | solution.py:506
  15.3 1.5 %collective-permute-start.9 = (bf16[2,2,16,1024]{3,2,1,0:T(8,128)(2,1)S(1)}, bf16[2,2,16,1024]{3,2,1,0:T(8,128)(2,1)S(1)}, u32[]{:S(2)}, u32[]{:S(2)}) collective-permute-start(bf16[2,2,16,1024]{3,2,1,0:T(8,128)(2,1)S(1)} %get-tuple-element.47), channel_id=1, source_target_pairs={{0,4},{4,0},{8,12},{12,8},{1,5},{5,1},{9,13},{13,9},{2,6},{6,2},{1... | collective-permute-start | bytes 393224 | tf_op jit(solution)/shard_map/ppermute | solution.py:556
  16.9 2.6 %collective-permute-start.10 = (bf16[2,2,16,1024]{3,2,1,0:T(8,128)(2,1)S(1)}, bf16[2,2,16,1024]{3,2,1,0:T(8,128)(2,1)S(1)}, u32[]{:S(2)}, u32[]{:S(2)}) collective-permute-start(bf16[2,2,16,1024]{3,2,1,0:T(8,128)(2,1)S(1)} %get-tuple-element.48), channel_id=1, source_target_pairs={{0,8},{4,12},{8,0},{12,4},{1,9},{5,13},{9,1},{13,5},{2,10},{6,14},... | collective-permute-start | bytes 393224 | tf_op jit(solution)/shard_map/ppermute | solution.py:556
  19.5 0.2 collective-permute-start.11
  19.7 4.7 %shard_map.106 = (bf16[1024,2048]{1,0:T(8,128)(2,1)S(1)}, bf16[1024,2048]{1,0:T(8,128)(2,1)S(1)}, bf16[1024,2048]{1,0:T(8,128)(2,1)S(1)}) custom-call(bf16[8192,2048]{1,0:T(8,128)(2,1)} %refs_0_.9, f32[16,128]{1,0:T(8,128)S(1)} %get-tuple-element.37.refs_1_), custom_call_target="tpu_custom_call" | custom-call | flops 900000000 | tf_op jit(solution)/shard_map/pallas_call | solution.py:49
  24.4 0.0 collective-permute-done.7.refs_2_
  24.4 0.5 %shard_map.107.refs_1_ = bf16[16,4096]{1,0:T(8,128)(2,1)S(1)} custom-call(f32[16,4096]{1,0:T(8,128)S(1)} %get-tuple-element.36.refs_0_, f32[16,128]{1,0:T(8,128)S(1)} %get-tuple-element.37.refs_1_, bf16[16,4352]{1,0:T(8,128)(2,1)S(1)} %collective-permute-done.7.refs_2_, bf16[1024,2048]{1,0:T(8,128)(2,1)S(1)} %get-tuple-element.39.refs_3_.refs_4_), custom_call_target="tpu_custom_call" | custom-call | flops 90000000 | tf_op jit(solution)/shard_map/pallas_call | solution.py:49
  24.9 0.1 collective-permute-start.8
  25.0 3.5 %shard_map.108 = (f32[16,2048]{1,0:T(8,128)S(1)}, bf16[1024,2048]{1,0:T(8,128)(2,1)S(1)}, bf16[1024,2048]{1,0:T(8,128)(2,1)S(1)}) custom-call(bf16[8192,2048]{1,0:T(8,128)(2,1)} %refs_0_.9, bf16[16,4096]{1,0:T(8,128)(2,1)S(1)} %shard_map.107.refs_1_, bf16[1024,2048]{1,0:T(8,128)(2,1)S(1)} %get-tuple-element.40.refs_2_, ...), custom_call_target="tpu_custom_call" | custom-call | flops 1020000000 | tf_op jit(solution)/shard_map/pallas_call | solution.py:49
  28.5 0.0 collective-permute-done.9.refs_7_
  28.5 1.3 %collective-permute-done.10.refs_8_ = bf16[2,2,16,1024]{3,2,1,0:T(8,128)(2,1)S(1)} collective-permute-done((bf16[2,2,16,1024]{3,2,1,0:T(8,128)(2,1)S(1)}, bf16[2,2,16,1024]{3,2,1,0:T(8,128)(2,1)S(1)}, u32[]{:S(2)}, u32[]{:S(2)}) %collective-permute-start.10) | collective-permute-done | bytes 131104 | tf_op jit(solution)/shard_map/ppermute | solution.py:556
  29.8 0.0 collective-permute-done.11.refs_9_
  29.8 0.0 collective-permute-done.8.refs_2_
  29.8 3.6 %shard_map.109 = (bf16[6,2048]{1,0:T(8,128)(2,1)}, bf16[6,2048]{1,0:T(8,128)(2,1)}, bf16[16,2,16,1024]{3,2,1,0:T(8,128)(2,1)}) custom-call(bf16[8192,2048]{1,0:T(8,128)(2,1)} %refs_0_.9, f32[16,2048]{1,0:T(8,128)S(1)} %get-tuple-element.44.refs_1_, bf16[16,4096]{1,0:T(8,128)(2,1)S(1)} %collective-permute-done.8.refs_2_, ...), custom_call_target="tpu_custom_call", output_to_operand_aliasing={{2}: (10, {})} | custom-call | flops 1020000000 | tf_op jit(solution)/shard_map/pallas_call | solution.py:49
Async XLA Ops:
  0.6 3.6 %collective-permute-start = (bf16[6,2560]{1,0:T(8,128)(2,1)}, bf16[6,2560]{1,0:T(8,128)(2,1)S(1)}, u32[]{:S(2)}, u32[]{:S(2)}) collective-permute-start(bf16[6,2560]{1,0:T(8,128)(2,1)} %refs_6_.1), channel_id=1, source_target_pairs={{0,1},{1,0},{2,3},{3,2},{4,5},{5,4},{6,7},{7,6},{8,9},{9,8},{10,11... | collective-permute-start | bytes 92168 | tf_op jit(solution)/shard_map/ppermute | solution.py:506
  1.2 3.0 %collective-permute-start.1 = (bf16[6,2560]{1,0:T(8,128)(2,1)}, bf16[6,2560]{1,0:T(8,128)(2,1)S(1)}, u32[]{:S(2)}, u32[]{:S(2)}) collective-permute-start(bf16[6,2560]{1,0:T(8,128)(2,1)} %refs_7_.1), channel_id=1, source_target_pairs={{0,1},{1,0},{2,3},{3,2},{4,5},{5,4},{6,7},{7,6},{8,9},{9,8},{10,11... | collective-permute-start | bytes 92168 | tf_op jit(solution)/shard_map/ppermute | solution.py:506
  1.3 6.3 %collective-permute-start.3 = (bf16[6,2560]{1,0:T(8,128)(2,1)}, bf16[6,2560]{1,0:T(8,128)(2,1)S(1)}, u32[]{:S(2)}, u32[]{:S(2)}) collective-permute-start(bf16[6,2560]{1,0:T(8,128)(2,1)} %refs_7_.1), channel_id=1, source_target_pairs={{0,2},{1,3},{2,0},{3,1},{4,6},{5,7},{6,4},{7,5},{8,10},{9,11},{10,... | collective-permute-start | bytes 92168 | tf_op jit(solution)/shard_map/ppermute | solution.py:506
  4.2 4.2 %collective-permute-start.2 = (bf16[6,2560]{1,0:T(8,128)(2,1)}, bf16[6,2560]{1,0:T(8,128)(2,1)S(1)}, u32[]{:S(2)}, u32[]{:S(2)}) collective-permute-start(bf16[6,2560]{1,0:T(8,128)(2,1)} %refs_6_.1), channel_id=1, source_target_pairs={{0,2},{1,3},{2,0},{3,1},{4,6},{5,7},{6,4},{7,5},{8,10},{9,11},{10,... | collective-permute-start | bytes 92168 | tf_op jit(solution)/shard_map/ppermute | solution.py:506
  8.4 1.2 %collective-permute-start.4 = (bf16[6,2560]{1,0:T(8,128)(2,1)S(1)}, bf16[6,2560]{1,0:T(8,128)(2,1)S(1)}, u32[]{:S(2)}, u32[]{:S(2)}) collective-permute-start(bf16[6,2560]{1,0:T(8,128)(2,1)S(1)} %collective-permute-done.2.refs_5_), channel_id=1, source_target_pairs={{0,1},{1,0},{2,3},{3,2},{4,5},{5,4},{6,7},{7,6},{8,9},{9,8},{10,11... | collective-permute-start | bytes 92168 | tf_op jit(solution)/shard_map/ppermute | solution.py:506
  8.4 1.4 %collective-permute-start.5 = (bf16[6,2560]{1,0:T(8,128)(2,1)S(1)}, bf16[6,2560]{1,0:T(8,128)(2,1)S(1)}, u32[]{:S(2)}, u32[]{:S(2)}) collective-permute-start(bf16[6,2560]{1,0:T(8,128)(2,1)S(1)} %collective-permute-done.3.refs_6_), channel_id=1, source_target_pairs={{0,1},{1,0},{2,3},{3,2},{4,5},{5,4},{6,7},{7,6},{8,9},{9,8},{10,11... | collective-permute-start | bytes 92168 | tf_op jit(solution)/shard_map/ppermute | solution.py:506
  12.3 1.4 %collective-permute-start.6 = (bf16[16,4352]{1,0:T(8,128)(2,1)S(1)}, bf16[16,4352]{1,0:T(8,128)(2,1)S(1)}, u32[]{:S(2)}, u32[]{:S(2)}) collective-permute-start(bf16[16,4352]{1,0:T(8,128)(2,1)S(1)} %get-tuple-element.35), channel_id=1, source_target_pairs={{0,1},{1,0},{2,3},{3,2},{4,5},{5,4},{6,7},{7,6},{8,9},{9,8},{10,11... | collective-permute-start | bytes 417800 | tf_op jit(solution)/shard_map/ppermute | solution.py:506
  14.1 10.3 %collective-permute-start.7 = (bf16[16,4352]{1,0:T(8,128)(2,1)S(1)}, bf16[16,4352]{1,0:T(8,128)(2,1)S(1)}, u32[]{:S(2)}, u32[]{:S(2)}) collective-permute-start(bf16[16,4352]{1,0:T(8,128)(2,1)S(1)} %get-tuple-element.38), channel_id=1, source_target_pairs={{0,2},{1,3},{2,0},{3,1},{4,6},{5,7},{6,4},{7,5},{8,10},{9,11},{10,... | collective-permute-start | bytes 417800 | tf_op jit(solution)/shard_map/ppermute | solution.py:506
  15.3 13.1 %collective-permute-start.9 = (bf16[2,2,16,1024]{3,2,1,0:T(8,128)(2,1)S(1)}, bf16[2,2,16,1024]{3,2,1,0:T(8,128)(2,1)S(1)}, u32[]{:S(2)}, u32[]{:S(2)}) collective-permute-start(bf16[2,2,16,1024]{3,2,1,0:T(8,128)(2,1)S(1)} %get-tuple-element.47), channel_id=1, source_target_pairs={{0,4},{4,0},{8,12},{12,8},{1,5},{5,1},{9,13},{13,9},{2,6},{6,2},{1... | collective-permute-start | bytes 393224 | tf_op jit(solution)/shard_map/ppermute | solution.py:556
  16.9 12.9 %collective-permute-start.10 = (bf16[2,2,16,1024]{3,2,1,0:T(8,128)(2,1)S(1)}, bf16[2,2,16,1024]{3,2,1,0:T(8,128)(2,1)S(1)}, u32[]{:S(2)}, u32[]{:S(2)}) collective-permute-start(bf16[2,2,16,1024]{3,2,1,0:T(8,128)(2,1)S(1)} %get-tuple-element.48), channel_id=1, source_target_pairs={{0,8},{4,12},{8,0},{12,4},{1,9},{5,13},{9,1},{13,5},{2,10},{6,14},... | collective-permute-start | bytes 393224 | tf_op jit(solution)/shard_map/ppermute | solution.py:556
  19.5 10.3 %collective-permute-start.11 = (bf16[2,2,16,1024]{3,2,1,0:T(8,128)(2,1)S(1)}, bf16[2,2,16,1024]{3,2,1,0:T(8,128)(2,1)S(1)}, u32[]{:S(2)}, u32[]{:S(2)}) collective-permute-start(bf16[2,2,16,1024]{3,2,1,0:T(8,128)(2,1)S(1)} %get-tuple-element.49), channel_id=1, source_target_pairs={{0,12},{4,8},{8,4},{12,0},{1,13},{5,9},{9,5},{13,1},{2,14},{6,10},... | collective-permute-start | bytes 393224 | tf_op jit(solution)/shard_map/ppermute | solution.py:556
  24.9 4.9 %collective-permute-start.8 = (bf16[16,4096]{1,0:T(8,128)(2,1)S(1)}, bf16[16,4096]{1,0:T(8,128)(2,1)S(1)}, u32[]{:S(2)}, u32[]{:S(2)}) collective-permute-start(bf16[16,4096]{1,0:T(8,128)(2,1)S(1)} %shard_map.107.refs_1_), channel_id=1, source_target_pairs={{0,1},{1,0},{2,3},{3,2},{4,5},{5,4},{6,7},{7,6},{8,9},{9,8},{10,11... | collective-permute-start | bytes 393224 | tf_op jit(solution)/shard_map/ppermute | solution.py:506

commit v5 on v4

--- a/solution.py
+++ b/solution.py
@@ -20,7 +20,14 @@
 WIDE = 1024
 PARTS = 1
 PREPARE = 0.05
-CHUNKS = 8
+UNITS = 16
+READS = {
+    "prepare": ((0, 2), (2, 2)),
+    "attend": ((4, 1),),
+    "stage": ((5, 3), (8, 3)),
+    "project": ((11, 3),),
+    "last": ((14, 2),),
+}
 FLOPS = 3e8
 BYTES = 0
 copy_of = pltpu.make_async_copy
@@ -87,7 +94,7 @@
         self.part_width = self.part_heads * HEAD_SIZE
         self.per_tile = LANES // (2 * self.part_heads)
         self.packed = self.part_width + LANES * -(-3 // self.per_tile)
-        self.chunk_rows = self.q_width // CHUNKS
+        self.unit_rows = self.q_width // UNITS
         self.early = 2
         while self.early * (self.q_width + 2 * self.kv_width) < n * 2 * self.kv_width:
             self.early *= 2
@@ -99,14 +106,14 @@
         )
 
 
-def w_copies(w_hbm, chunks, refs, sems, first=0):
-    rows = w_hbm.shape[0] // CHUNKS
+def w_copies(w_hbm, reads, refs, sems, first=0):
+    rows = w_hbm.shape[0] // UNITS
     side = lax.rem(lax.axis_index("tp"), 2)
     copies = []
-    for i, k in enumerate(chunks):
-        half = side if k < CHUNKS // 2 else 1 - side
-        start = half * (w_hbm.shape[0] // 2) + (k % (CHUNKS // 2)) * rows
-        source = w_hbm.at[pl.ds(pl.multiple_of(start, LANES), rows)]
+    for i, (unit, count) in enumerate(reads):
+        half = side if unit < UNITS // 2 else 1 - side
+        start = half * (w_hbm.shape[0] // 2) + (unit % (UNITS // 2)) * rows
+        source = w_hbm.at[pl.ds(pl.multiple_of(start, LANES), count * rows)]
         copies.append(copy_of(source, refs[i], sems.at[first + i]))
     return copies
 
@@ -129,7 +136,8 @@
     ]
     own = [copy_of(first_hbm, first, sems.at[5]), copy_of(second_hbm, second, sems.at[6])]
     kv_copy = copy_of(kv_hbm, pages.at[pl.ds(0, z.pool)], sems.at[4])
-    for copy in small + own + [kv_copy]:
+    w_loads = w_copies(w_hbm, chunks, w_refs, sems, 8)
+    for copy in small + own + [kv_copy] + w_loads[:1]:
         copy.start()
     pages[z.pool] = jnp.zeros_like(pages[z.pool])
     rows[...] = jnp.zeros_like(rows)
@@ -151,8 +159,7 @@
 
     for i in range(moves.shape[1]):
         sends(i, lambda copy: copy.start())
-    w_loads = w_copies(w_hbm, chunks, w_refs, sems, 8)
-    for copy in w_loads:
+    for copy in w_loads[1:]:
         copy.start()
 
     grid = (z.all_rows, z.positions)
@@ -422,28 +429,26 @@
         body(pl.ds(pl.multiple_of(t * tile, tile), tile))
 
 
-def product(z, mixed, weights, columns, first=0):
+def product(mixed, weights, columns, begin=0):
     total = None
-    for i, w in enumerate(weights):
-        begin = (first + i) * z.chunk_rows
-        term = jnp.dot(
-            mixed[:, begin : begin + z.chunk_rows], w[:, columns], preferred_element_type=F32
-        )
+    for w in weights:
+        rows = w.shape[0]
+        term = jnp.dot(mixed[:, begin : begin + rows], w[:, columns], preferred_element_type=F32)
         total = term if total is None else total + term
+        begin += rows
     return total
 
 
-def project_kernel(z, chunks, *refs):
-    half = CHUNKS // 2
+def project_kernel(z, held, chunks, *refs):
     w_hbm, mixed = refs[:2]
-    weights = refs[2 : 2 + half]
-    acc_ref = refs[2 + half]
-    loads = w_copies(w_hbm, chunks, refs[3 + half :], refs[-1])
+    weights = refs[2 : 2 + held]
+    acc_ref = refs[2 + held]
+    loads = w_copies(w_hbm, chunks, refs[3 + held :], refs[-1])
     for copy in loads:
         copy.start()
 
     def body(columns):
-        acc_ref[:, columns] = product(z, mixed, weights, columns)
+        acc_ref[:, columns] = product(mixed, weights, columns)
 
     column_tiles(z.out_columns, body)
     for copy in loads:
@@ -457,10 +462,8 @@
     first_ref, second_ref, kv_out, late, acc, plan, sems = refs[4 + held + z.inst_count :]
     plan_copy = copy_of(plan_vmem, plan, sems.at[0])
     plan_copy.start()
-    late_refs = [late.at[i] for i in range(len(chunks))]
-    loads = w_copies(w_hbm, chunks, late_refs, sems, 2)
-    for copy in loads:
-        copy.start()
+    (load,) = w_copies(w_hbm, chunks, [late], sems, 2)
+    load.start()
 
     def placed(act):
         for s in range(z.inst_count - 1):
@@ -472,23 +475,20 @@
                     act(copy_of(arrived[s].at[j], kv_out.at[slot], sems.at[1]))
 
     def early(columns):
-        acc[:, columns] = acc_in[:, columns] + product(z, mixed, weights, columns)
+        acc[:, columns] = acc_in[:, columns] + product(mixed, weights, columns)
 
     column_tiles(z.out_columns, early)
     plan_copy.wait()
     placed(lambda copy: copy.start())
-    for i, copy in enumerate(loads):
-        copy.wait()
-
-        def body(columns):
-            total = acc[:, columns] + product(z, mixed, [late_refs[i]], columns, held + i)
-            if i < len(loads) - 1:
-                acc[:, columns] = total
-            else:
-                first_ref[:, columns] = total[: z.rows_of].astype(BF16)
-                second_ref[:, columns] = total[z.step_rows : z.step_rows + z.rows_of].astype(BF16)
-
-        column_tiles(z.out_columns, body, min(WIDE, z.out_columns))
+    load.wait()
+
+    def body(columns):
+        begin = mixed.shape[1] - late.shape[0]
+        total = acc[:, columns] + product(mixed, [late], columns, begin)
+        first_ref[:, columns] = total[: z.rows_of].astype(BF16)
+        second_ref[:, columns] = total[z.step_rows : z.step_rows + z.rows_of].astype(BF16)
+
+    column_tiles(z.out_columns, body, WIDE)
     placed(lambda copy: copy.wait())
 
 
@@ -510,7 +510,10 @@
         stages.append(1 << len(stages))
 
     w_hbm = in_hbm(w_out)
-    chunk = (shape((z.chunk_rows, z.out_columns)), VMEM)
+    parts = {
+        name: [(shape((count * z.unit_rows, z.out_columns)), VMEM) for _, count in reads]
+        for name, reads in READS.items()
+    }
     have = {0: (qkv_first, qkv_second)}
     for d in range(1, z.early):
         have[d] = tuple(swap(x, d) for x in have[0])
@@ -518,7 +521,7 @@
     for d in far:
         have[d] = tuple(swap(x, d) for x in have[0])
     pages, rows, visible, plan, *more = run(
-        functools.partial(prepare_kernel, z, (0,)),
+        functools.partial(prepare_kernel, z, READS["prepare"]),
         PREPARE,
         [HBM] * 8 + [VMEM] * (2 * z.early - 2),
         [
@@ -528,7 +531,7 @@
             (shape((z.plan_rows, LANES), I32), VMEM),
         ]
         + [(shape((z.per_rank,) + page), VMEM)] * (inst_count - 1)
-        + [chunk],
+        + parts["prepare"],
         [
             pltpu.VMEM(qkv_first.shape, BF16),
             pltpu.VMEM(qkv_second.shape, BF16),
@@ -537,7 +540,7 @@
             smem(moves.shape, I32),
             smem(dest_pages.shape, I32),
             smem((z.plan_rows * LANES,), I32),
-            dma((9,)),
+            dma((8 + len(READS["prepare"]),)),
         ],
         [w_hbm]
         + [
@@ -546,7 +549,7 @@
         ]
         + [x for d in range(1, z.early) for x in have[d]],
     )
-    outgoing, weights = more[:-1], more[-1:]
+    outgoing, weights = more[: inst_count - 1], more[inst_count - 1 :]
     for d in far:
         for e in range(1, d):
             have[d ^ e] = tuple(swap(behind(x, plan), e) for x in have[d])
@@ -557,7 +560,7 @@
         )
 
     send, acc, stats, _, _, kv_mid, *loaded = run(
-        functools.partial(attend_kernel, z, (1,)),
+        functools.partial(attend_kernel, z, READS["attend"]),
         2,
         [HBM] + [VMEM] * (4 + 2 * (n - z.early)),
         [
@@ -567,9 +570,9 @@
             (shape(rows.shape), VMEM),
             (shape(pages.shape), VMEM),
             (shape(kv_cache.shape), HBM),
-            chunk,
-        ],
-        [smem((z.plan_rows, LANES), I32), dma((3,))],
+        ]
+        + parts["attend"],
+        [smem((z.plan_rows, LANES), I32), dma((2 + len(READS["attend"]),))],
         [w_hbm, plan, visible, pages, rows] + [x for d in range(z.early, n) for x in have[d]],
         aliases={3: 4, 4: 3},
     )
@@ -590,11 +593,11 @@
         )
     theirs = swap(send, stages[-1])
     weights += run(
-        functools.partial(stage_kernel, (2, 3, 4)),
+        functools.partial(stage_kernel, READS["stage"]),
         3,
         [HBM],
-        [chunk] * 3,
-        [dma((3,))],
+        parts["stage"],
+        [dma((len(READS["stage"]),))],
         [w_hbm],
         after=[stats],
     )
@@ -608,29 +611,30 @@
         after=weights[-1:],
     )
     other = swap(mixed, 1)
+    near, far = weights[:-1], weights[-1:]
     total, *held = run(
-        functools.partial(project_kernel, z, (5, 6)),
-        3.4,
-        [HBM] + [VMEM] * (1 + CHUNKS // 2),
-        [(shape((z.all_rows, z.out_columns), F32), VMEM)] + [chunk] * 2,
-        [dma((2,))],
-        [w_hbm, mixed, *weights[:-1]],
-    )
-    held = weights[-1:] + held
+        functools.partial(project_kernel, z, len(near), READS["project"]),
+        3,
+        [HBM] + [VMEM] * (1 + len(near)),
+        [(shape((z.all_rows, z.out_columns), F32), VMEM)] + parts["project"],
+        [dma((len(READS["project"]),))],
+        [w_hbm, mixed, *near],
+    )
+    held = far + held
     return tuple(
         run(
-            functools.partial(last_kernel, z, 3, (7,)),
+            functools.partial(last_kernel, z, len(held), READS["last"]),
             3.4,
-            [HBM] + [VMEM] * (5 + inst_count) + [HBM],
+            [HBM] + [VMEM] * (2 + len(held) + inst_count) + [HBM],
             [(shape((rows_of, z.out_columns)), VMEM)] * 2 + [(shape(kv_cache.shape), HBM)],
             [
-                pltpu.VMEM((1, z.chunk_rows, z.out_columns), BF16),
+                pltpu.VMEM(parts["last"][0][0].shape, BF16),
                 pltpu.VMEM((z.all_rows, z.out_columns), F32),
                 smem((z.plan_rows, LANES), I32),
                 dma((3,)),
             ],
             [w_hbm, total, other, plan, *held, *arrived, kv_mid],
-            aliases={6 + inst_count: 2},
+            aliases={3 + len(held) + inst_count: 2},
             limit=12,
         )
     )

time: 33.6 us -> 34.5 us (1.027)
  starting transfers between devices: 10.2 us -> 11.1 us
    ppermute x9, waiting for transfers between devices: 2.78 us -> 1.89 us  [swap(): return lax.ppermute(x, 'tp', [(i, i ^ d) for i in range(n)])]
    ppermute x9, starting transfers between devices: 5.84 us -> 6.72 us  [swap(): return lax.ppermute(x, 'tp', [(i, i ^ d) for i in range(n)])]
    ppermute x3, waiting for transfers between devices: 1.27 us -> 2 us  [steps(): lax.ppermute(outgoing[s - 1], 'inst', [(i, i ^ s) for i in range(inst_cou...]
  transfers between devices with their start and end apart: 12 -> 12, of which waited for: 5 -> 4; matrix products, arithmetic and copies ran while one was open for 0% -> 0% of each run, Pallas kernels for 36% -> 35%
where the time goes in v5:
time: 34.5 us; the launch traced here: 34.3 us
  Pallas kernels  18.5 us (54%)
  starting transfers between devices  11.1 us (32%)
  waiting for transfers between devices  3.89 us (11%)
  between operations  0.73 us (2%)
    pallas_call x7, Pallas kernels, run(): pl.pallas_call(body, out_shape=tuple((s for s, _ in outs)), in_specs=[spe...  18.5 us
    ppermute x9, starting transfers between devices, swap(): return lax.ppermute(x, 'tp', [(i, i ^ d) for i in range(n)])  6.72 us
    ppermute x3, starting transfers between devices, steps(): lax.ppermute(outgoing[s - 1], 'inst', [(i, i ^ s) for i in range(inst_cou...  4.39 us
    ppermute x3, waiting for transfers between devices, steps(): lax.ppermute(outgoing[s - 1], 'inst', [(i, i ^ s) for i in range(inst_cou...  2 us
    ppermute x9, waiting for transfers between devices, swap(): return lax.ppermute(x, 'tp', [(i, i ^ d) for i in range(n)])  1.89 us
  transfers between devices with their start and end apart: 12, of which 4 were waited for; matrix products, arithmetic and copies ran while one was open for 0% of the time, Pallas kernels for 35%

profile of v5, /device:TPU:0, one launch (start us, length us, event | category | flops | bytes accessed | tf_op | source)
XLA Modules:
  0.0 34.3 jit_solution(8959032969342571446)
XLA Ops:
  0.6 0.6 %collective-permute-start = (bf16[6,2560]{1,0:T(8,128)(2,1)}, bf16[6,2560]{1,0:T(8,128)(2,1)S(1)}, u32[]{:S(2)}, u32[]{:S(2)}) collective-permute-start(bf16[6,2560]{1,0:T(8,128)(2,1)} %refs_6_.1), channel_id=1, source_target_pairs={{0,1},{1,0},{2,3},{3,2},{4,5},{5,4},{6,7},{7,6},{8,9},{9,8},{10,11... | collective-permute-start | bytes 92168 | tf_op jit(solution)/shard_map/ppermute | solution.py:506
  1.2 0.1 collective-permute-start.1
  1.3 2.9 %collective-permute-start.3 = (bf16[6,2560]{1,0:T(8,128)(2,1)}, bf16[6,2560]{1,0:T(8,128)(2,1)S(1)}, u32[]{:S(2)}, u32[]{:S(2)}) collective-permute-start(bf16[6,2560]{1,0:T(8,128)(2,1)} %refs_7_.1), channel_id=1, source_target_pairs={{0,2},{1,3},{2,0},{3,1},{4,6},{5,7},{6,4},{7,5},{8,10},{9,11},{10,... | collective-permute-start | bytes 92168 | tf_op jit(solution)/shard_map/ppermute | solution.py:506
  4.2 0.0 collective-permute-start.2
  4.2 0.0 collective-permute-done.refs_8_
  4.2 0.0 collective-permute-done.1.refs_9_
  4.2 4.2 %shard_map.103 = (bf16[18,2,16,1024]{3,2,1,0:T(8,128)(2,1)S(1)}, bf16[16,10240]{1,0:T(8,128)(2,1)S(1)}, s32[16,256]{1,0:T(8,128)S(1)}, s32[8,128]{1,0:T(8,128)S(...) custom-call(bf16[8192,2048]{1,0:T(8,128)(2,1)} %refs_0_.9, ...), custom_call_target="tpu_custom_call" | custom-call | flops 15000000 | tf_op jit(solution)/shard_map/pallas_call | solution.py:56
  8.4 0.0 collective-permute-done.3.refs_6_
  8.4 0.0 collective-permute-done.2.refs_5_
  8.4 0.1 collective-permute-start.4
  8.5 0.5 %collective-permute-start.5 = (bf16[6,2560]{1,0:T(8,128)(2,1)S(1)}, bf16[6,2560]{1,0:T(8,128)(2,1)S(1)}, u32[]{:S(2)}, u32[]{:S(2)}) collective-permute-start(bf16[6,2560]{1,0:T(8,128)(2,1)S(1)} %collective-permute-done.3.refs_6_), channel_id=1, source_target_pairs={{0,1},{1,0},{2,3},{3,2},{4,5},{5,4},{6,7},{7,6},{8,9},{9,8},{10,11... | collective-permute-start | bytes 92168 | tf_op jit(solution)/shard_map/ppermute | solution.py:506
  9.0 0.7 %collective-permute-done.4.refs_7_ = bf16[6,2560]{1,0:T(8,128)(2,1)S(1)} collective-permute-done((bf16[6,2560]{1,0:T(8,128)(2,1)S(1)}, bf16[6,2560]{1,0:T(8,128)(2,1)S(1)}, u32[]{:S(2)}, u32[]{:S(2)}) %collective-permute-start.4) | collective-permute-done | bytes 30752 | tf_op jit(solution)/shard_map/ppermute | solution.py:506
  9.7 0.2 collective-permute-done.5.refs_8_
  9.9 2.5 %shard_map.104 = (bf16[16,4352]{1,0:T(8,128)(2,1)S(1)}, f32[16,4096]{1,0:T(8,128)S(1)}, f32[16,128]{1,0:T(8,128)S(1)}, bf16[16,10240]{1,0:T(8,128)(2,1)S(1)}, bf...) custom-call(bf16[8192,2048]{1,0:T(8,128)(2,1)} %refs_0_.9, ...), custom_call_target="tpu_custom_call", output_to_operand_aliasing={{4}: (3, {}), {3}: (4, {})} | custom-call | flops 600000000 | tf_op jit(solution)/shard_map/pallas_call | solution.py:56
  12.4 0.4 %collective-permute-start.6 = (bf16[16,4352]{1,0:T(8,128)(2,1)S(1)}, bf16[16,4352]{1,0:T(8,128)(2,1)S(1)}, u32[]{:S(2)}, u32[]{:S(2)}) collective-permute-start(bf16[16,4352]{1,0:T(8,128)(2,1)S(1)} %get-tuple-element.34), channel_id=1, source_target_pairs={{0,1},{1,0},{2,3},{3,2},{4,5},{5,4},{6,7},{7,6},{8,9},{9,8},{10,11... | collective-permute-start | bytes 417800 | tf_op jit(solution)/shard_map/ppermute | solution.py:506
  12.8 1.0 %collective-permute-done.6.refs_2_ = bf16[16,4352]{1,0:T(8,128)(2,1)S(1)} collective-permute-done((bf16[16,4352]{1,0:T(8,128)(2,1)S(1)}, bf16[16,4352]{1,0:T(8,128)(2,1)S(1)}, u32[]{:S(2)}, u32[]{:S(2)}) %collective-permute-start.6) | collective-permute-done | bytes 139296 | tf_op jit(solution)/shard_map/ppermute | solution.py:506
  13.8 0.3 shard_map.105
  14.2 2.1 %collective-permute-start.7 = (bf16[16,4352]{1,0:T(8,128)(2,1)S(1)}, bf16[16,4352]{1,0:T(8,128)(2,1)S(1)}, u32[]{:S(2)}, u32[]{:S(2)}) collective-permute-start(bf16[16,4352]{1,0:T(8,128)(2,1)S(1)} %get-tuple-element.37), channel_id=1, source_target_pairs={{0,2},{1,3},{2,0},{3,1},{4,6},{5,7},{6,4},{7,5},{8,10},{9,11},{10,... | collective-permute-start | bytes 417800 | tf_op jit(solution)/shard_map/ppermute | solution.py:506
  16.2 1.5 %collective-permute-start.9 = (bf16[2,2,16,1024]{3,2,1,0:T(8,128)(2,1)S(1)}, bf16[2,2,16,1024]{3,2,1,0:T(8,128)(2,1)S(1)}, u32[]{:S(2)}, u32[]{:S(2)}) collective-permute-start(bf16[2,2,16,1024]{3,2,1,0:T(8,128)(2,1)S(1)} %get-tuple-element.45), channel_id=1, source_target_pairs={{0,4},{4,0},{8,12},{12,8},{1,5},{5,1},{9,13},{13,9},{2,6},{6,2},{1... | collective-permute-start | bytes 393224 | tf_op jit(solution)/shard_map/ppermute | solution.py:559
  17.7 2.7 %collective-permute-start.10 = (bf16[2,2,16,1024]{3,2,1,0:T(8,128)(2,1)S(1)}, bf16[2,2,16,1024]{3,2,1,0:T(8,128)(2,1)S(1)}, u32[]{:S(2)}, u32[]{:S(2)}) collective-permute-start(bf16[2,2,16,1024]{3,2,1,0:T(8,128)(2,1)S(1)} %get-tuple-element.46), channel_id=1, source_target_pairs={{0,8},{4,12},{8,0},{12,4},{1,9},{5,13},{9,1},{13,5},{2,10},{6,14},... | collective-permute-start | bytes 393224 | tf_op jit(solution)/shard_map/ppermute | solution.py:559
  20.4 0.2 collective-permute-start.11
  20.6 4.6 %shard_map.106 = (bf16[1536,2048]{1,0:T(8,128)(2,1)S(1)}, bf16[1536,2048]{1,0:T(8,128)(2,1)S(1)}) custom-call(bf16[8192,2048]{1,0:T(8,128)(2,1)} %refs_0_.9, f32[16,128]{1,0:T(8,128)S(1)} %get-tuple-element.36.refs_1_), custom_call_target="tpu_custom_call" | custom-call | flops 900000000 | tf_op jit(solution)/shard_map/pallas_call | solution.py:56
  25.2 0.0 collective-permute-done.7.refs_2_
  25.3 0.5 %shard_map.107.refs_1_ = bf16[16,4096]{1,0:T(8,128)(2,1)S(1)} custom-call(f32[16,4096]{1,0:T(8,128)S(1)} %get-tuple-element.35.refs_0_, f32[16,128]{1,0:T(8,128)S(1)} %get-tuple-element.36.refs_1_, bf16[16,4352]{1,0:T(8,128)(2,1)S(1)} %collective-permute-done.7.refs_2_, bf16[1536,2048]{1,0:T(8,128)(2,1)S(1)} %get-tuple-element.38.refs_3_.refs_4_), custom_call_target="tpu_custom_call" | custom-call | flops 90000000 | tf_op jit(solution)/shard_map/pallas_call | solution.py:56
  25.7 0.1 collective-permute-start.8
  25.8 2.8 %shard_map.108 = (f32[16,2048]{1,0:T(8,128)S(1)}, bf16[1536,2048]{1,0:T(8,128)(2,1)S(1)}) custom-call(bf16[8192,2048]{1,0:T(8,128)(2,1)} %refs_0_.9, bf16[16,4096]{1,0:T(8,128)(2,1)S(1)} %shard_map.107.refs_1_, bf16[1024,2048]{1,0:T(8,128)(2,1)S(1)} %get-tuple-element.39.refs_2_, bf16[1024,2048]{1,0:T(8,128)(2,1)S(1)} %get-tuple-element.40.refs_3_, ...), custom_call_target="tpu_custom_call" | custom-call | flops 900000000 | tf_op jit(solution)/shard_map/pallas_call | solution.py:56
  28.6 0.0 collective-permute-done.9.refs_6_
  28.6 2.0 %collective-permute-done.10.refs_7_ = bf16[2,2,16,1024]{3,2,1,0:T(8,128)(2,1)S(1)} collective-permute-done((bf16[2,2,16,1024]{3,2,1,0:T(8,128)(2,1)S(1)}, bf16[2,2,16,1024]{3,2,1,0:T(8,128)(2,1)S(1)}, u32[]{:S(2)}, u32[]{:S(2)}) %collective-permute-start.10) | collective-permute-done | bytes 131104 | tf_op jit(solution)/shard_map/ppermute | solution.py:559
  30.6 0.0 collective-permute-done.11.refs_8_
  30.6 0.0 collective-permute-done.8.refs_2_
  30.6 3.6 %shard_map.109 = (bf16[6,2048]{1,0:T(8,128)(2,1)}, bf16[6,2048]{1,0:T(8,128)(2,1)}, bf16[16,2,16,1024]{3,2,1,0:T(8,128)(2,1)}) custom-call(bf16[8192,2048]{1,0:T(8,128)(2,1)} %refs_0_.9, f32[16,2048]{1,0:T(8,128)S(1)} %get-tuple-element.43.refs_1_, bf16[16,4096]{1,0:T(8,128)(2,1)S(1)} %collective-permute-done.8.refs_2_, ...), custom_call_target="tpu_custom_call", output_to_operand_aliasing={{2}: (9, {})} | custom-call | flops 1020000000 | tf_op jit(solution)/shard_map/pallas_call | solution.py:56
Async XLA Ops:
  0.6 3.6 %collective-permute-start = (bf16[6,2560]{1,0:T(8,128)(2,1)}, bf16[6,2560]{1,0:T(8,128)(2,1)S(1)}, u32[]{:S(2)}, u32[]{:S(2)}) collective-permute-start(bf16[6,2560]{1,0:T(8,128)(2,1)} %refs_6_.1), channel_id=1, source_target_pairs={{0,1},{1,0},{2,3},{3,2},{4,5},{5,4},{6,7},{7,6},{8,9},{9,8},{10,11... | collective-permute-start | bytes 92168 | tf_op jit(solution)/shard_map/ppermute | solution.py:506
  1.2 3.0 %collective-permute-start.1 = (bf16[6,2560]{1,0:T(8,128)(2,1)}, bf16[6,2560]{1,0:T(8,128)(2,1)S(1)}, u32[]{:S(2)}, u32[]{:S(2)}) collective-permute-start(bf16[6,2560]{1,0:T(8,128)(2,1)} %refs_7_.1), channel_id=1, source_target_pairs={{0,1},{1,0},{2,3},{3,2},{4,5},{5,4},{6,7},{7,6},{8,9},{9,8},{10,11... | collective-permute-start | bytes 92168 | tf_op jit(solution)/shard_map/ppermute | solution.py:506
  1.3 7.2 %collective-permute-start.3 = (bf16[6,2560]{1,0:T(8,128)(2,1)}, bf16[6,2560]{1,0:T(8,128)(2,1)S(1)}, u32[]{:S(2)}, u32[]{:S(2)}) collective-permute-start(bf16[6,2560]{1,0:T(8,128)(2,1)} %refs_7_.1), channel_id=1, source_target_pairs={{0,2},{1,3},{2,0},{3,1},{4,6},{5,7},{6,4},{7,5},{8,10},{9,11},{10,... | collective-permute-start | bytes 92168 | tf_op jit(solution)/shard_map/ppermute | solution.py:506
  4.2 4.2 %collective-permute-start.2 = (bf16[6,2560]{1,0:T(8,128)(2,1)}, bf16[6,2560]{1,0:T(8,128)(2,1)S(1)}, u32[]{:S(2)}, u32[]{:S(2)}) collective-permute-start(bf16[6,2560]{1,0:T(8,128)(2,1)} %refs_6_.1), channel_id=1, source_target_pairs={{0,2},{1,3},{2,0},{3,1},{4,6},{5,7},{6,4},{7,5},{8,10},{9,11},{10,... | collective-permute-start | bytes 92168 | tf_op jit(solution)/shard_map/ppermute | solution.py:506
  8.4 1.3 %collective-permute-start.4 = (bf16[6,2560]{1,0:T(8,128)(2,1)S(1)}, bf16[6,2560]{1,0:T(8,128)(2,1)S(1)}, u32[]{:S(2)}, u32[]{:S(2)}) collective-permute-start(bf16[6,2560]{1,0:T(8,128)(2,1)S(1)} %collective-permute-done.2.refs_5_), channel_id=1, source_target_pairs={{0,1},{1,0},{2,3},{3,2},{4,5},{5,4},{6,7},{7,6},{8,9},{9,8},{10,11... | collective-permute-start | bytes 92168 | tf_op jit(solution)/shard_map/ppermute | solution.py:506
  8.5 1.4 %collective-permute-start.5 = (bf16[6,2560]{1,0:T(8,128)(2,1)S(1)}, bf16[6,2560]{1,0:T(8,128)(2,1)S(1)}, u32[]{:S(2)}, u32[]{:S(2)}) collective-permute-start(bf16[6,2560]{1,0:T(8,128)(2,1)S(1)} %collective-permute-done.3.refs_6_), channel_id=1, source_target_pairs={{0,1},{1,0},{2,3},{3,2},{4,5},{5,4},{6,7},{7,6},{8,9},{9,8},{10,11... | collective-permute-start | bytes 92168 | tf_op jit(solution)/shard_map/ppermute | solution.py:506
  12.4 1.4 %collective-permute-start.6 = (bf16[16,4352]{1,0:T(8,128)(2,1)S(1)}, bf16[16,4352]{1,0:T(8,128)(2,1)S(1)}, u32[]{:S(2)}, u32[]{:S(2)}) collective-permute-start(bf16[16,4352]{1,0:T(8,128)(2,1)S(1)} %get-tuple-element.34), channel_id=1, source_target_pairs={{0,1},{1,0},{2,3},{3,2},{4,5},{5,4},{6,7},{7,6},{8,9},{9,8},{10,11... | collective-permute-start | bytes 417800 | tf_op jit(solution)/shard_map/ppermute | solution.py:506
  14.2 11.1 %collective-permute-start.7 = (bf16[16,4352]{1,0:T(8,128)(2,1)S(1)}, bf16[16,4352]{1,0:T(8,128)(2,1)S(1)}, u32[]{:S(2)}, u32[]{:S(2)}) collective-permute-start(bf16[16,4352]{1,0:T(8,128)(2,1)S(1)} %get-tuple-element.37), channel_id=1, source_target_pairs={{0,2},{1,3},{2,0},{3,1},{4,6},{5,7},{6,4},{7,5},{8,10},{9,11},{10,... | collective-permute-start | bytes 417800 | tf_op jit(solution)/shard_map/ppermute | solution.py:506
  16.2 12.4 %collective-permute-start.9 = (bf16[2,2,16,1024]{3,2,1,0:T(8,128)(2,1)S(1)}, bf16[2,2,16,1024]{3,2,1,0:T(8,128)(2,1)S(1)}, u32[]{:S(2)}, u32[]{:S(2)}) collective-permute-start(bf16[2,2,16,1024]{3,2,1,0:T(8,128)(2,1)S(1)} %get-tuple-element.45), channel_id=1, source_target_pairs={{0,4},{4,0},{8,12},{12,8},{1,5},{5,1},{9,13},{13,9},{2,6},{6,2},{1... | collective-permute-start | bytes 393224 | tf_op jit(solution)/shard_map/ppermute | solution.py:559
  17.7 12.9 %collective-permute-start.10 = (bf16[2,2,16,1024]{3,2,1,0:T(8,128)(2,1)S(1)}, bf16[2,2,16,1024]{3,2,1,0:T(8,128)(2,1)S(1)}, u32[]{:S(2)}, u32[]{:S(2)}) collective-permute-start(bf16[2,2,16,1024]{3,2,1,0:T(8,128)(2,1)S(1)} %get-tuple-element.46), channel_id=1, source_target_pairs={{0,8},{4,12},{8,0},{12,4},{1,9},{5,13},{9,1},{13,5},{2,10},{6,14},... | collective-permute-start | bytes 393224 | tf_op jit(solution)/shard_map/ppermute | solution.py:559
  20.4 10.2 %collective-permute-start.11 = (bf16[2,2,16,1024]{3,2,1,0:T(8,128)(2,1)S(1)}, bf16[2,2,16,1024]{3,2,1,0:T(8,128)(2,1)S(1)}, u32[]{:S(2)}, u32[]{:S(2)}) collective-permute-start(bf16[2,2,16,1024]{3,2,1,0:T(8,128)(2,1)S(1)} %get-tuple-element.47), channel_id=1, source_target_pairs={{0,12},{4,8},{8,4},{12,0},{1,13},{5,9},{9,5},{13,1},{2,14},{6,10},... | collective-permute-start | bytes 393224 | tf_op jit(solution)/shard_map/ppermute | solution.py:559
  25.7 4.9 %collective-permute-start.8 = (bf16[16,4096]{1,0:T(8,128)(2,1)S(1)}, bf16[16,4096]{1,0:T(8,128)(2,1)S(1)}, u32[]{:S(2)}, u32[]{:S(2)}) collective-permute-start(bf16[16,4096]{1,0:T(8,128)(2,1)S(1)} %shard_map.107.refs_1_), channel_id=1, source_target_pairs={{0,1},{1,0},{2,3},{3,2},{4,5},{5,4},{6,7},{7,6},{8,9},{9,8},{10,11... | collective-permute-start | bytes 393224 | tf_op jit(solution)/shard_map/ppermute | solution.py:506

commit v6 on v5

--- a/solution.py
+++ b/solution.py
@@ -22,8 +22,8 @@
 PREPARE = 0.05
 UNITS = 16
 READS = {
-    "prepare": ((0, 2), (2, 2)),
-    "attend": ((4, 1),),
+    "prepare": ((0, 2), (2, 1)),
+    "attend": ((3, 2),),
     "stage": ((5, 3), (8, 3)),
     "project": ((11, 3),),
     "last": ((14, 2),),
@@ -343,10 +343,10 @@
     m = 2 * (z.n - z.early)
     w_hbm, plan_vmem, visible_ref, _, _ = refs[:5]
     pieces = refs[5 : 5 + m]
-    send_ref, keep_ref, stats_ref, rows, pages, kv_out = refs[5 + m : 11 + m]
-    w_refs = refs[11 + m : 11 + m + len(chunks)]
-    plan, sems = refs[11 + m + len(chunks) :]
-    w_loads = w_copies(w_hbm, chunks, w_refs, sems, 2)
+    send_ref, keep_ref, stats_ref, rows, pages = refs[5 + m : 10 + m]
+    w_refs = refs[10 + m : 10 + m + len(chunks)]
+    plan, sems = refs[10 + m + len(chunks) :]
+    w_loads = w_copies(w_hbm, chunks, w_refs, sems, 1)
     for copy in w_loads:
         copy.start()
     plan_copy = copy_of(plan_vmem, plan, sems.at[0])
@@ -366,15 +366,9 @@
                 old = pages[slot, kv].astype(F32)
                 pages[slot, kv] = jnp.where(here, new, old).astype(BF16)
 
-    writes = [
-        copy_of(pages.at[read(plan, z.at_source + p)], kv_out.at[p], sems.at[1])
-        for p in range(z.pool)
-    ]
-    for copy in writes:
-        copy.start()
     visible = (visible_ref[...] > 0)[None]
     attend_part(z, 0, rows, pages, visible, send_ref, keep_ref, stats_ref)
-    for copy in writes + w_loads:
+    for copy in w_loads:
         copy.wait()
 
 
@@ -413,11 +407,20 @@
         mixed_ref[:, columns] = (piece / total).astype(BF16)
 
 
-def stage_kernel(chunks, w_hbm, *refs):
-    loads = w_copies(w_hbm, chunks, refs, refs[-1])
-    for copy in loads:
+def stage_kernel(z, reads, *refs):
+    w_hbm, pages, plan_vmem, kv_out = refs[:4]
+    plan, sems = refs[4 + len(reads) :]
+    plan_copy = copy_of(plan_vmem, plan, sems.at[0])
+    plan_copy.start()
+    copies = w_copies(w_hbm, reads, refs[4:], sems, 2)
+    for copy in copies:
         copy.start()
-    for copy in loads:
+    plan_copy.wait()
+    for p in range(z.pool):
+        write = copy_of(pages.at[read(plan, z.at_source + p)], kv_out.at[p], sems.at[1])
+        write.start()
+        copies.append(write)
+    for copy in copies:
         copy.wait()
 
 
@@ -474,12 +477,16 @@
                 def _():
                     act(copy_of(arrived[s].at[j], kv_out.at[slot], sems.at[1]))
 
-    def early(columns):
-        acc[:, columns] = acc_in[:, columns] + product(mixed, weights, columns)
-
-    column_tiles(z.out_columns, early)
+    def first_product(columns):
+        acc[:, columns] = acc_in[:, columns] + product(mixed, weights[:1], columns)
+
+    def next_product(columns):
+        acc[:, columns] += product(mixed, weights[1:], columns, weights[0].shape[0])
+
+    column_tiles(z.out_columns, first_product)
     plan_copy.wait()
     placed(lambda copy: copy.start())
+    column_tiles(z.out_columns, next_product)
     load.wait()
 
     def body(columns):
@@ -559,7 +566,7 @@
             lax.ppermute(outgoing[s - 1], "inst", [(i, i ^ s) for i in range(inst_count)])
         )
 
-    send, acc, stats, _, _, kv_mid, *loaded = run(
+    send, acc, stats, _, pages, *loaded = run(
         functools.partial(attend_kernel, z, READS["attend"]),
         2,
         [HBM] + [VMEM] * (4 + 2 * (n - z.early)),
@@ -569,10 +576,9 @@
             (shape((z.all_rows, LANES), F32), VMEM),
             (shape(rows.shape), VMEM),
             (shape(pages.shape), VMEM),
-            (shape(kv_cache.shape), HBM),
         ]
         + parts["attend"],
-        [smem((z.plan_rows, LANES), I32), dma((2 + len(READS["attend"]),))],
+        [smem((z.plan_rows, LANES), I32), dma((1 + len(READS["attend"]),))],
         [w_hbm, plan, visible, pages, rows] + [x for d in range(z.early, n) for x in have[d]],
         aliases={3: 4, 4: 3},
     )
@@ -592,15 +598,16 @@
             [acc, stats, theirs],
         )
     theirs = swap(send, stages[-1])
-    weights += run(
-        functools.partial(stage_kernel, READS["stage"]),
+    kv_mid, *loaded = run(
+        functools.partial(stage_kernel, z, READS["stage"]),
         3,
-        [HBM],
-        parts["stage"],
-        [dma((len(READS["stage"]),))],
-        [w_hbm],
+        [HBM, VMEM, VMEM],
+        [(shape(kv_cache.shape), HBM)] + parts["stage"],
+        [smem((z.plan_rows, LANES), I32), dma((2 + len(READS["stage"]),))],
+        [w_hbm, pages, plan],
         after=[stats],
     )
+    weights += loaded
     (mixed,) = run(
         functools.partial(finish_kernel, z),
         0.3,

time: 34.5 us -> 34 us (0.986)
  starting transfers between devices: 11.1 us -> 10.5 us
    ppermute x9, waiting for transfers between devices: 1.89 us -> 2.48 us  [swap(): return lax.ppermute(x, 'tp', [(i, i ^ d) for i in range(n)])]
    ppermute x9, starting transfers between devices: 6.72 us -> 6.15 us  [swap(): return lax.ppermute(x, 'tp', [(i, i ^ d) for i in range(n)])]
    ppermute x3, waiting for transfers between devices: 2 us -> 1.61 us  [steps(): lax.ppermute(outgoing[s - 1], 'inst', [(i, i ^ s) for i in range(inst_cou...]
  transfers between devices with their start and end apart: 12 -> 12, of which waited for: 4 -> 5; matrix products, arithmetic and copies ran while one was open for 0% -> 0% of each run, Pallas kernels for 35% -> 35%
where the time goes in v6:
time: 34 us; the launch traced here: 33.8 us
  Pallas kernels  18.5 us (54%)
  starting transfers between devices  10.5 us (31%)
  waiting for transfers between devices  4.08 us (12%)
  between operations  0.72 us (2%)
    pallas_call x7, Pallas kernels, run(): pl.pallas_call(body, out_shape=tuple((s for s, _ in outs)), in_specs=[spe...  18.5 us
    ppermute x9, starting transfers between devices, swap(): return lax.ppermute(x, 'tp', [(i, i ^ d) for i in range(n)])  6.15 us
    ppermute x3, starting transfers between devices, steps(): lax.ppermute(outgoing[s - 1], 'inst', [(i, i ^ s) for i in range(inst_cou...  4.39 us
    ppermute x9, waiting for transfers between devices, swap(): return lax.ppermute(x, 'tp', [(i, i ^ d) for i in range(n)])  2.48 us
    ppermute x3, waiting for transfers between devices, steps(): lax.ppermute(outgoing[s - 1], 'inst', [(i, i ^ s) for i in range(inst_cou...  1.61 us
  transfers between devices with their start and end apart: 12, of which 5 were waited for; matrix products, arithmetic and copies ran while one was open for 0% of the time, Pallas kernels for 35%

profile of v6, /device:TPU:0, one launch (start us, length us, event | category | flops | bytes accessed | tf_op | source)
XLA Modules:
  0.0 33.8 jit_solution(11350602967639357118)
XLA Ops:
  0.6 0.6 %collective-permute-start = (bf16[6,2560]{1,0:T(8,128)(2,1)}, bf16[6,2560]{1,0:T(8,128)(2,1)S(1)}, u32[]{:S(2)}, u32[]{:S(2)}) collective-permute-start(bf16[6,2560]{1,0:T(8,128)(2,1)} %refs_6_.1), channel_id=1, source_target_pairs={{0,1},{1,0},{2,3},{3,2},{4,5},{5,4},{6,7},{7,6},{8,9},{9,8},{10,11... | collective-permute-start | bytes 92168 | tf_op jit(solution)/shard_map/ppermute | solution.py:513
  1.2 0.1 collective-permute-start.1
  1.3 2.9 %collective-permute-start.3 = (bf16[6,2560]{1,0:T(8,128)(2,1)}, bf16[6,2560]{1,0:T(8,128)(2,1)S(1)}, u32[]{:S(2)}, u32[]{:S(2)}) collective-permute-start(bf16[6,2560]{1,0:T(8,128)(2,1)} %refs_7_.1), channel_id=1, source_target_pairs={{0,2},{1,3},{2,0},{3,1},{4,6},{5,7},{6,4},{7,5},{8,10},{9,11},{10,... | collective-permute-start | bytes 92168 | tf_op jit(solution)/shard_map/ppermute | solution.py:513
  4.2 0.0 collective-permute-start.2
  4.2 0.0 collective-permute-done.refs_8_
  4.2 0.0 collective-permute-done.1.refs_9_
  4.2 3.6 %shard_map.103 = (bf16[18,2,16,1024]{3,2,1,0:T(8,128)(2,1)S(1)}, bf16[16,10240]{1,0:T(8,128)(2,1)S(1)}, s32[16,256]{1,0:T(8,128)S(1)}, s32[8,128]{1,0:T(8,128)S(...) custom-call(bf16[8192,2048]{1,0:T(8,128)(2,1)} %refs_0_.9, ...), custom_call_target="tpu_custom_call" | custom-call | flops 15000000 | tf_op jit(solution)/shard_map/pallas_call | solution.py:56
  7.8 0.0 collective-permute-done.3.refs_6_
  7.8 0.6 %collective-permute-done.2.refs_5_ = bf16[6,2560]{1,0:T(8,128)(2,1)S(1)} collective-permute-done((bf16[6,2560]{1,0:T(8,128)(2,1)}, bf16[6,2560]{1,0:T(8,128)(2,1)S(1)}, u32[]{:S(2)}, u32[]{:S(2)}) %collective-permute-start.2) | collective-permute-done | bytes 30752 | tf_op jit(solution)/shard_map/ppermute | solution.py:513
  8.4 0.0 collective-permute-start.4
  8.4 0.5 %collective-permute-start.5 = (bf16[6,2560]{1,0:T(8,128)(2,1)S(1)}, bf16[6,2560]{1,0:T(8,128)(2,1)S(1)}, u32[]{:S(2)}, u32[]{:S(2)}) collective-permute-start(bf16[6,2560]{1,0:T(8,128)(2,1)S(1)} %collective-permute-done.3.refs_6_), channel_id=1, source_target_pairs={{0,1},{1,0},{2,3},{3,2},{4,5},{5,4},{6,7},{7,6},{8,9},{9,8},{10,11... | collective-permute-start | bytes 92168 | tf_op jit(solution)/shard_map/ppermute | solution.py:513
  8.9 0.7 %collective-permute-done.4.refs_7_ = bf16[6,2560]{1,0:T(8,128)(2,1)S(1)} collective-permute-done((bf16[6,2560]{1,0:T(8,128)(2,1)S(1)}, bf16[6,2560]{1,0:T(8,128)(2,1)S(1)}, u32[]{:S(2)}, u32[]{:S(2)}) %collective-permute-start.4) | collective-permute-done | bytes 30752 | tf_op jit(solution)/shard_map/ppermute | solution.py:513
  9.6 0.2 collective-permute-done.5.refs_8_
  9.8 2.2 %shard_map.104 = (bf16[16,4352]{1,0:T(8,128)(2,1)S(1)}, f32[16,4096]{1,0:T(8,128)S(1)}, f32[16,128]{1,0:T(8,128)S(1)}, bf16[16,10240]{1,0:T(8,128)(2,1)S(1)}, bf...) custom-call(bf16[8192,2048]{1,0:T(8,128)(2,1)} %refs_0_.9, ...), custom_call_target="tpu_custom_call", output_to_operand_aliasing={{4}: (3, {}), {3}: (4, {})} | custom-call | flops 600000000 | tf_op jit(solution)/shard_map/pallas_call | solution.py:56
  12.0 0.4 %collective-permute-start.6 = (bf16[16,4352]{1,0:T(8,128)(2,1)S(1)}, bf16[16,4352]{1,0:T(8,128)(2,1)S(1)}, u32[]{:S(2)}, u32[]{:S(2)}) collective-permute-start(bf16[16,4352]{1,0:T(8,128)(2,1)S(1)} %get-tuple-element.35), channel_id=1, source_target_pairs={{0,1},{1,0},{2,3},{3,2},{4,5},{5,4},{6,7},{7,6},{8,9},{9,8},{10,11... | collective-permute-start | bytes 417800 | tf_op jit(solution)/shard_map/ppermute | solution.py:513
  12.4 1.0 %collective-permute-done.6.refs_2_ = bf16[16,4352]{1,0:T(8,128)(2,1)S(1)} collective-permute-done((bf16[16,4352]{1,0:T(8,128)(2,1)S(1)}, bf16[16,4352]{1,0:T(8,128)(2,1)S(1)}, u32[]{:S(2)}, u32[]{:S(2)}) %collective-permute-start.6) | collective-permute-done | bytes 139296 | tf_op jit(solution)/shard_map/ppermute | solution.py:513
  13.4 0.3 shard_map.105
  13.8 1.6 %collective-permute-start.7 = (bf16[16,4352]{1,0:T(8,128)(2,1)S(1)}, bf16[16,4352]{1,0:T(8,128)(2,1)S(1)}, u32[]{:S(2)}, u32[]{:S(2)}) collective-permute-start(bf16[16,4352]{1,0:T(8,128)(2,1)S(1)} %get-tuple-element.38), channel_id=1, source_target_pairs={{0,2},{1,3},{2,0},{3,1},{4,6},{5,7},{6,4},{7,5},{8,10},{9,11},{10,... | collective-permute-start | bytes 417800 | tf_op jit(solution)/shard_map/ppermute | solution.py:513
  15.4 1.5 %collective-permute-start.9 = (bf16[2,2,16,1024]{3,2,1,0:T(8,128)(2,1)S(1)}, bf16[2,2,16,1024]{3,2,1,0:T(8,128)(2,1)S(1)}, u32[]{:S(2)}, u32[]{:S(2)}) collective-permute-start(bf16[2,2,16,1024]{3,2,1,0:T(8,128)(2,1)S(1)} %get-tuple-element.47), channel_id=1, source_target_pairs={{0,4},{4,0},{8,12},{12,8},{1,5},{5,1},{9,13},{13,9},{2,6},{6,2},{1... | collective-permute-start | bytes 393224 | tf_op jit(solution)/shard_map/ppermute | solution.py:566
  16.9 2.7 %collective-permute-start.10 = (bf16[2,2,16,1024]{3,2,1,0:T(8,128)(2,1)S(1)}, bf16[2,2,16,1024]{3,2,1,0:T(8,128)(2,1)S(1)}, u32[]{:S(2)}, u32[]{:S(2)}) collective-permute-start(bf16[2,2,16,1024]{3,2,1,0:T(8,128)(2,1)S(1)} %get-tuple-element.48), channel_id=1, source_target_pairs={{0,8},{4,12},{8,0},{12,4},{1,9},{5,13},{9,1},{13,5},{2,10},{6,14},... | collective-permute-start | bytes 393224 | tf_op jit(solution)/shard_map/ppermute | solution.py:566
  19.5 0.2 collective-permute-start.11
  19.7 5.0 %shard_map.106 = (bf16[16,2,16,1024]{3,2,1,0:T(8,128)(2,1)}, bf16[1536,2048]{1,0:T(8,128)(2,1)S(1)}, bf16[1536,2048]{1,0:T(8,128)(2,1)S(1)}) custom-call(bf16[8192,2048]{1,0:T(8,128)(2,1)} %refs_0_.9, bf16[18,2,16,1024]{3,2,1,0:T(8,128)(2,1)S(1)} %get-tuple-element.39.refs_1_, s32[8,128]{1,0:T(8,128)S(1)} %get-tuple-element.27.refs_1_.refs_2_.refs_3_, ...), custom_call_target="tpu_custom_call" | custom-call | flops 900000000 | tf_op jit(solution)/shard_map/pallas_call | solution.py:56
  24.8 0.0 collective-permute-done.7.refs_2_
  24.8 0.5 %shard_map.107.refs_1_ = bf16[16,4096]{1,0:T(8,128)(2,1)S(1)} custom-call(f32[16,4096]{1,0:T(8,128)S(1)} %get-tuple-element.36.refs_0_, f32[16,128]{1,0:T(8,128)S(1)} %get-tuple-element.37.refs_3_.refs_1_, bf16[16,4352]{1,0:T(8,128)(2,1)S(1)} %collective-permute-done.7.refs_2_, bf16[1536,2048]{1,0:T(8,128)(2,1)S(1)} %get-tuple-element.40.refs_3_.refs_4_), custom_call_target="tpu_custom_call" | custom-call | flops 90000000 | tf_op jit(solution)/shard_map/pallas_call | solution.py:56
  25.2 0.1 collective-permute-start.8
  25.3 2.8 %shard_map.108 = (f32[16,2048]{1,0:T(8,128)S(1)}, bf16[1536,2048]{1,0:T(8,128)(2,1)S(1)}) custom-call(bf16[8192,2048]{1,0:T(8,128)(2,1)} %refs_0_.9, bf16[16,4096]{1,0:T(8,128)(2,1)S(1)} %shard_map.107.refs_1_, bf16[1024,2048]{1,0:T(8,128)(2,1)S(1)} %get-tuple-element.41.refs_2_, bf16[512,2048]{1,0:T(8,128)(2,1)S(1)} %get-tuple-element.42.refs_3_, ...), custom_call_target="tpu_custom_call" | custom-call | flops 900000000 | tf_op jit(solution)/shard_map/pallas_call | solution.py:56
  28.1 0.0 collective-permute-done.9.refs_6_
  28.1 1.6 %collective-permute-done.10.refs_7_ = bf16[2,2,16,1024]{3,2,1,0:T(8,128)(2,1)S(1)} collective-permute-done((bf16[2,2,16,1024]{3,2,1,0:T(8,128)(2,1)S(1)}, bf16[2,2,16,1024]{3,2,1,0:T(8,128)(2,1)S(1)}, u32[]{:S(2)}, u32[]{:S(2)}) %collective-permute-start.10) | collective-permute-done | bytes 131104 | tf_op jit(solution)/shard_map/ppermute | solution.py:566
  29.7 0.0 collective-permute-done.11.refs_8_
  29.7 0.0 collective-permute-done.8.refs_2_
  29.7 4.1 %shard_map.109 = (bf16[6,2048]{1,0:T(8,128)(2,1)}, bf16[6,2048]{1,0:T(8,128)(2,1)}, bf16[16,2,16,1024]{3,2,1,0:T(8,128)(2,1)}) custom-call(bf16[8192,2048]{1,0:T(8,128)(2,1)} %refs_0_.9, f32[16,2048]{1,0:T(8,128)S(1)} %get-tuple-element.45.refs_1_, bf16[16,4096]{1,0:T(8,128)(2,1)S(1)} %collective-permute-done.8.refs_2_, ...), custom_call_target="tpu_custom_call", output_to_operand_aliasing={{2}: (9, {})} | custom-call | flops 1020000000 | tf_op jit(solution)/shard_map/pallas_call | solution.py:56
Async XLA Ops:
  0.6 3.6 %collective-permute-start = (bf16[6,2560]{1,0:T(8,128)(2,1)}, bf16[6,2560]{1,0:T(8,128)(2,1)S(1)}, u32[]{:S(2)}, u32[]{:S(2)}) collective-permute-start(bf16[6,2560]{1,0:T(8,128)(2,1)} %refs_6_.1), channel_id=1, source_target_pairs={{0,1},{1,0},{2,3},{3,2},{4,5},{5,4},{6,7},{7,6},{8,9},{9,8},{10,11... | collective-permute-start | bytes 92168 | tf_op jit(solution)/shard_map/ppermute | solution.py:513
  1.2 3.0 %collective-permute-start.1 = (bf16[6,2560]{1,0:T(8,128)(2,1)}, bf16[6,2560]{1,0:T(8,128)(2,1)S(1)}, u32[]{:S(2)}, u32[]{:S(2)}) collective-permute-start(bf16[6,2560]{1,0:T(8,128)(2,1)} %refs_7_.1), channel_id=1, source_target_pairs={{0,1},{1,0},{2,3},{3,2},{4,5},{5,4},{6,7},{7,6},{8,9},{9,8},{10,11... | collective-permute-start | bytes 92168 | tf_op jit(solution)/shard_map/ppermute | solution.py:513
  1.3 6.6 %collective-permute-start.3 = (bf16[6,2560]{1,0:T(8,128)(2,1)}, bf16[6,2560]{1,0:T(8,128)(2,1)S(1)}, u32[]{:S(2)}, u32[]{:S(2)}) collective-permute-start(bf16[6,2560]{1,0:T(8,128)(2,1)} %refs_7_.1), channel_id=1, source_target_pairs={{0,2},{1,3},{2,0},{3,1},{4,6},{5,7},{6,4},{7,5},{8,10},{9,11},{10,... | collective-permute-start | bytes 92168 | tf_op jit(solution)/shard_map/ppermute | solution.py:513
  4.2 4.2 %collective-permute-start.2 = (bf16[6,2560]{1,0:T(8,128)(2,1)}, bf16[6,2560]{1,0:T(8,128)(2,1)S(1)}, u32[]{:S(2)}, u32[]{:S(2)}) collective-permute-start(bf16[6,2560]{1,0:T(8,128)(2,1)} %refs_6_.1), channel_id=1, source_target_pairs={{0,2},{1,3},{2,0},{3,1},{4,6},{5,7},{6,4},{7,5},{8,10},{9,11},{10,... | collective-permute-start | bytes 92168 | tf_op jit(solution)/shard_map/ppermute | solution.py:513
  8.4 1.2 %collective-permute-start.4 = (bf16[6,2560]{1,0:T(8,128)(2,1)S(1)}, bf16[6,2560]{1,0:T(8,128)(2,1)S(1)}, u32[]{:S(2)}, u32[]{:S(2)}) collective-permute-start(bf16[6,2560]{1,0:T(8,128)(2,1)S(1)} %collective-permute-done.2.refs_5_), channel_id=1, source_target_pairs={{0,1},{1,0},{2,3},{3,2},{4,5},{5,4},{6,7},{7,6},{8,9},{9,8},{10,11... | collective-permute-start | bytes 92168 | tf_op jit(solution)/shard_map/ppermute | solution.py:513
  8.4 1.4 %collective-permute-start.5 = (bf16[6,2560]{1,0:T(8,128)(2,1)S(1)}, bf16[6,2560]{1,0:T(8,128)(2,1)S(1)}, u32[]{:S(2)}, u32[]{:S(2)}) collective-permute-start(bf16[6,2560]{1,0:T(8,128)(2,1)S(1)} %collective-permute-done.3.refs_6_), channel_id=1, source_target_pairs={{0,1},{1,0},{2,3},{3,2},{4,5},{5,4},{6,7},{7,6},{8,9},{9,8},{10,11... | collective-permute-start | bytes 92168 | tf_op jit(solution)/shard_map/ppermute | solution.py:513
  12.0 1.4 %collective-permute-start.6 = (bf16[16,4352]{1,0:T(8,128)(2,1)S(1)}, bf16[16,4352]{1,0:T(8,128)(2,1)S(1)}, u32[]{:S(2)}, u32[]{:S(2)}) collective-permute-start(bf16[16,4352]{1,0:T(8,128)(2,1)S(1)} %get-tuple-element.35), channel_id=1, source_target_pairs={{0,1},{1,0},{2,3},{3,2},{4,5},{5,4},{6,7},{7,6},{8,9},{9,8},{10,11... | collective-permute-start | bytes 417800 | tf_op jit(solution)/shard_map/ppermute | solution.py:513
  13.8 11.0 %collective-permute-start.7 = (bf16[16,4352]{1,0:T(8,128)(2,1)S(1)}, bf16[16,4352]{1,0:T(8,128)(2,1)S(1)}, u32[]{:S(2)}, u32[]{:S(2)}) collective-permute-start(bf16[16,4352]{1,0:T(8,128)(2,1)S(1)} %get-tuple-element.38), channel_id=1, source_target_pairs={{0,2},{1,3},{2,0},{3,1},{4,6},{5,7},{6,4},{7,5},{8,10},{9,11},{10,... | collective-permute-start | bytes 417800 | tf_op jit(solution)/shard_map/ppermute | solution.py:513
  15.4 12.8 %collective-permute-start.9 = (bf16[2,2,16,1024]{3,2,1,0:T(8,128)(2,1)S(1)}, bf16[2,2,16,1024]{3,2,1,0:T(8,128)(2,1)S(1)}, u32[]{:S(2)}, u32[]{:S(2)}) collective-permute-start(bf16[2,2,16,1024]{3,2,1,0:T(8,128)(2,1)S(1)} %get-tuple-element.47), channel_id=1, source_target_pairs={{0,4},{4,0},{8,12},{12,8},{1,5},{5,1},{9,13},{13,9},{2,6},{6,2},{1... | collective-permute-start | bytes 393224 | tf_op jit(solution)/shard_map/ppermute | solution.py:566
  16.9 12.9 %collective-permute-start.10 = (bf16[2,2,16,1024]{3,2,1,0:T(8,128)(2,1)S(1)}, bf16[2,2,16,1024]{3,2,1,0:T(8,128)(2,1)S(1)}, u32[]{:S(2)}, u32[]{:S(2)}) collective-permute-start(bf16[2,2,16,1024]{3,2,1,0:T(8,128)(2,1)S(1)} %get-tuple-element.48), channel_id=1, source_target_pairs={{0,8},{4,12},{8,0},{12,4},{1,9},{5,13},{9,1},{13,5},{2,10},{6,14},... | collective-permute-start | bytes 393224 | tf_op jit(solution)/shard_map/ppermute | solution.py:566
  19.5 10.2 %collective-permute-start.11 = (bf16[2,2,16,1024]{3,2,1,0:T(8,128)(2,1)S(1)}, bf16[2,2,16,1024]{3,2,1,0:T(8,128)(2,1)S(1)}, u32[]{:S(2)}, u32[]{:S(2)}) collective-permute-start(bf16[2,2,16,1024]{3,2,1,0:T(8,128)(2,1)S(1)} %get-tuple-element.49), channel_id=1, source_target_pairs={{0,12},{4,8},{8,4},{12,0},{1,13},{5,9},{9,5},{13,1},{2,14},{6,10},... | collective-permute-start | bytes 393224 | tf_op jit(solution)/shard_map/ppermute | solution.py:566
  25.2 4.5 %collective-permute-start.8 = (bf16[16,4096]{1,0:T(8,128)(2,1)S(1)}, bf16[16,4096]{1,0:T(8,128)(2,1)S(1)}, u32[]{:S(2)}, u32[]{:S(2)}) collective-permute-start(bf16[16,4096]{1,0:T(8,128)(2,1)S(1)} %shard_map.107.refs_1_), channel_id=1, source_target_pairs={{0,1},{1,0},{2,3},{3,2},{4,5},{5,4},{6,7},{7,6},{8,9},{9,8},{10,11... | collective-permute-start | bytes 393224 | tf_op jit(solution)/shard_map/ppermute | solution.py:513

commit v7 on v6

--- a/solution.py
+++ b/solution.py
@@ -477,16 +477,12 @@
                 def _():
                     act(copy_of(arrived[s].at[j], kv_out.at[slot], sems.at[1]))
 
-    def first_product(columns):
-        acc[:, columns] = acc_in[:, columns] + product(mixed, weights[:1], columns)
-
-    def next_product(columns):
-        acc[:, columns] += product(mixed, weights[1:], columns, weights[0].shape[0])
-
-    column_tiles(z.out_columns, first_product)
+    def early(columns):
+        acc[:, columns] = acc_in[:, columns] + product(mixed, weights, columns)
+
+    column_tiles(z.out_columns, early, WIDE)
     plan_copy.wait()
     placed(lambda copy: copy.start())
-    column_tiles(z.out_columns, next_product)
     load.wait()
 
     def body(columns):
@@ -495,7 +491,7 @@
         first_ref[:, columns] = total[: z.rows_of].astype(BF16)
         second_ref[:, columns] = total[z.step_rows : z.step_rows + z.rows_of].astype(BF16)
 
-    column_tiles(z.out_columns, body, WIDE)
+    column_tiles(z.out_columns, body, 2 * WIDE)
     placed(lambda copy: copy.wait())
 
 

time: 34 us -> 33.5 us (0.985)
  Pallas kernels: 18.5 us -> 17.9 us
    pallas_call x7, Pallas kernels: 18.5 us -> 17.9 us  [run(): pl.pallas_call(body, out_shape=tuple((s for s, _ in outs)), in_specs=[spe...]
  transfers between devices with their start and end apart: 12 -> 12, of which waited for: 5 -> 5; matrix products, arithmetic and copies ran while one was open for 0% -> 0% of each run, Pallas kernels for 35% -> 36%
where the time goes in v7:
time: 33.5 us; the launch traced here: 33.3 us
  Pallas kernels  17.9 us (53%)
  starting transfers between devices  10.5 us (31%)
  waiting for transfers between devices  4.08 us (12%)
  between operations  0.72 us (2%)
    pallas_call x7, Pallas kernels, run(): pl.pallas_call(body, out_shape=tuple((s for s, _ in outs)), in_specs=[spe...  17.9 us
    ppermute x9, starting transfers between devices, swap(): return lax.ppermute(x, 'tp', [(i, i ^ d) for i in range(n)])  6.15 us
    ppermute x3, starting transfers between devices, steps(): lax.ppermute(outgoing[s - 1], 'inst', [(i, i ^ s) for i in range(inst_cou...  4.39 us
    ppermute x9, waiting for transfers between devices, swap(): return lax.ppermute(x, 'tp', [(i, i ^ d) for i in range(n)])  2.48 us
    ppermute x3, waiting for transfers between devices, steps(): lax.ppermute(outgoing[s - 1], 'inst', [(i, i ^ s) for i in range(inst_cou...  1.61 us
  transfers between devices with their start and end apart: 12, of which 5 were waited for; matrix products, arithmetic and copies ran while one was open for 0% of the time, Pallas kernels for 36%

profile of v7, /device:TPU:0, one launch (start us, length us, event | category | flops | bytes accessed | tf_op | source)
XLA Modules:
  0.0 33.3 jit_solution(2643238201540578946)
XLA Ops:
  0.6 0.6 %collective-permute-start = (bf16[6,2560]{1,0:T(8,128)(2,1)}, bf16[6,2560]{1,0:T(8,128)(2,1)S(1)}, u32[]{:S(2)}, u32[]{:S(2)}) collective-permute-start(bf16[6,2560]{1,0:T(8,128)(2,1)} %refs_6_.1), channel_id=1, source_target_pairs={{0,1},{1,0},{2,3},{3,2},{4,5},{5,4},{6,7},{7,6},{8,9},{9,8},{10,11... | collective-permute-start | bytes 92168 | tf_op jit(solution)/shard_map/ppermute | solution.py:509
  1.2 0.1 collective-permute-start.1
  1.3 2.9 %collective-permute-start.3 = (bf16[6,2560]{1,0:T(8,128)(2,1)}, bf16[6,2560]{1,0:T(8,128)(2,1)S(1)}, u32[]{:S(2)}, u32[]{:S(2)}) collective-permute-start(bf16[6,2560]{1,0:T(8,128)(2,1)} %refs_7_.1), channel_id=1, source_target_pairs={{0,2},{1,3},{2,0},{3,1},{4,6},{5,7},{6,4},{7,5},{8,10},{9,11},{10,... | collective-permute-start | bytes 92168 | tf_op jit(solution)/shard_map/ppermute | solution.py:509
  4.2 0.0 collective-permute-start.2
  4.2 0.0 collective-permute-done.refs_8_
  4.2 0.0 collective-permute-done.1.refs_9_
  4.2 3.6 %shard_map.103 = (bf16[18,2,16,1024]{3,2,1,0:T(8,128)(2,1)S(1)}, bf16[16,10240]{1,0:T(8,128)(2,1)S(1)}, s32[16,256]{1,0:T(8,128)S(1)}, s32[8,128]{1,0:T(8,128)S(...) custom-call(bf16[8192,2048]{1,0:T(8,128)(2,1)} %refs_0_.9, ...), custom_call_target="tpu_custom_call" | custom-call | flops 15000000 | tf_op jit(solution)/shard_map/pallas_call | solution.py:56
  7.8 0.0 collective-permute-done.3.refs_6_
  7.8 0.6 %collective-permute-done.2.refs_5_ = bf16[6,2560]{1,0:T(8,128)(2,1)S(1)} collective-permute-done((bf16[6,2560]{1,0:T(8,128)(2,1)}, bf16[6,2560]{1,0:T(8,128)(2,1)S(1)}, u32[]{:S(2)}, u32[]{:S(2)}) %collective-permute-start.2) | collective-permute-done | bytes 30752 | tf_op jit(solution)/shard_map/ppermute | solution.py:509
  8.4 0.0 collective-permute-start.4
  8.4 0.5 %collective-permute-start.5 = (bf16[6,2560]{1,0:T(8,128)(2,1)S(1)}, bf16[6,2560]{1,0:T(8,128)(2,1)S(1)}, u32[]{:S(2)}, u32[]{:S(2)}) collective-permute-start(bf16[6,2560]{1,0:T(8,128)(2,1)S(1)} %collective-permute-done.3.refs_6_), channel_id=1, source_target_pairs={{0,1},{1,0},{2,3},{3,2},{4,5},{5,4},{6,7},{7,6},{8,9},{9,8},{10,11... | collective-permute-start | bytes 92168 | tf_op jit(solution)/shard_map/ppermute | solution.py:509
  8.9 0.7 %collective-permute-done.4.refs_7_ = bf16[6,2560]{1,0:T(8,128)(2,1)S(1)} collective-permute-done((bf16[6,2560]{1,0:T(8,128)(2,1)S(1)}, bf16[6,2560]{1,0:T(8,128)(2,1)S(1)}, u32[]{:S(2)}, u32[]{:S(2)}) %collective-permute-start.4) | collective-permute-done | bytes 30752 | tf_op jit(solution)/shard_map/ppermute | solution.py:509
  9.6 0.2 collective-permute-done.5.refs_8_
  9.8 2.2 %shard_map.104 = (bf16[16,4352]{1,0:T(8,128)(2,1)S(1)}, f32[16,4096]{1,0:T(8,128)S(1)}, f32[16,128]{1,0:T(8,128)S(1)}, bf16[16,10240]{1,0:T(8,128)(2,1)S(1)}, bf...) custom-call(bf16[8192,2048]{1,0:T(8,128)(2,1)} %refs_0_.9, ...), custom_call_target="tpu_custom_call", output_to_operand_aliasing={{4}: (3, {}), {3}: (4, {})} | custom-call | flops 600000000 | tf_op jit(solution)/shard_map/pallas_call | solution.py:56
  12.0 0.4 %collective-permute-start.6 = (bf16[16,4352]{1,0:T(8,128)(2,1)S(1)}, bf16[16,4352]{1,0:T(8,128)(2,1)S(1)}, u32[]{:S(2)}, u32[]{:S(2)}) collective-permute-start(bf16[16,4352]{1,0:T(8,128)(2,1)S(1)} %get-tuple-element.35), channel_id=1, source_target_pairs={{0,1},{1,0},{2,3},{3,2},{4,5},{5,4},{6,7},{7,6},{8,9},{9,8},{10,11... | collective-permute-start | bytes 417800 | tf_op jit(solution)/shard_map/ppermute | solution.py:509
  12.4 1.0 %collective-permute-done.6.refs_2_ = bf16[16,4352]{1,0:T(8,128)(2,1)S(1)} collective-permute-done((bf16[16,4352]{1,0:T(8,128)(2,1)S(1)}, bf16[16,4352]{1,0:T(8,128)(2,1)S(1)}, u32[]{:S(2)}, u32[]{:S(2)}) %collective-permute-start.6) | collective-permute-done | bytes 139296 | tf_op jit(solution)/shard_map/ppermute | solution.py:509
  13.4 0.3 %shard_map.105 = (f32[16,4096]{1,0:T(8,128)S(1)}, f32[16,128]{1,0:T(8,128)S(1)}, bf16[16,4352]{1,0:T(8,128)(2,1)S(1)}) custom-call(f32[16,4096]{1,0:T(8,128)S(1)} %get-tuple-element.33.refs_0_, f32[16,128]{1,0:T(8,128)S(1)} %get-tuple-element.34.refs_1_, bf16[16,4352]{1,0:T(8,128)(2,1)S(1)} %collective-permute-done.6.refs_2_), custom_call_target="tpu_custom_call" | custom-call | flops 60000000 | tf_op jit(solution)/shard_map/pallas_call | solution.py:56
  13.8 1.6 %collective-permute-start.7 = (bf16[16,4352]{1,0:T(8,128)(2,1)S(1)}, bf16[16,4352]{1,0:T(8,128)(2,1)S(1)}, u32[]{:S(2)}, u32[]{:S(2)}) collective-permute-start(bf16[16,4352]{1,0:T(8,128)(2,1)S(1)} %get-tuple-element.38), channel_id=1, source_target_pairs={{0,2},{1,3},{2,0},{3,1},{4,6},{5,7},{6,4},{7,5},{8,10},{9,11},{10,... | collective-permute-start | bytes 417800 | tf_op jit(solution)/shard_map/ppermute | solution.py:509
  15.4 1.5 %collective-permute-start.9 = (bf16[2,2,16,1024]{3,2,1,0:T(8,128)(2,1)S(1)}, bf16[2,2,16,1024]{3,2,1,0:T(8,128)(2,1)S(1)}, u32[]{:S(2)}, u32[]{:S(2)}) collective-permute-start(bf16[2,2,16,1024]{3,2,1,0:T(8,128)(2,1)S(1)} %get-tuple-element.47), channel_id=1, source_target_pairs={{0,4},{4,0},{8,12},{12,8},{1,5},{5,1},{9,13},{13,9},{2,6},{6,2},{1... | collective-permute-start | bytes 393224 | tf_op jit(solution)/shard_map/ppermute | solution.py:562
  16.9 2.7 %collective-permute-start.10 = (bf16[2,2,16,1024]{3,2,1,0:T(8,128)(2,1)S(1)}, bf16[2,2,16,1024]{3,2,1,0:T(8,128)(2,1)S(1)}, u32[]{:S(2)}, u32[]{:S(2)}) collective-permute-start(bf16[2,2,16,1024]{3,2,1,0:T(8,128)(2,1)S(1)} %get-tuple-element.48), channel_id=1, source_target_pairs={{0,8},{4,12},{8,0},{12,4},{1,9},{5,13},{9,1},{13,5},{2,10},{6,14},... | collective-permute-start | bytes 393224 | tf_op jit(solution)/shard_map/ppermute | solution.py:562
  19.5 0.2 collective-permute-start.11
  19.7 5.0 %shard_map.106 = (bf16[16,2,16,1024]{3,2,1,0:T(8,128)(2,1)}, bf16[1536,2048]{1,0:T(8,128)(2,1)S(1)}, bf16[1536,2048]{1,0:T(8,128)(2,1)S(1)}) custom-call(bf16[8192,2048]{1,0:T(8,128)(2,1)} %refs_0_.9, bf16[18,2,16,1024]{3,2,1,0:T(8,128)(2,1)S(1)} %get-tuple-element.39.refs_1_, s32[8,128]{1,0:T(8,128)S(1)} %get-tuple-element.27.refs_1_.refs_2_.refs_3_, ...), custom_call_target="tpu_custom_call" | custom-call | flops 900000000 | tf_op jit(solution)/shard_map/pallas_call | solution.py:56
  24.8 0.0 collective-permute-done.7.refs_2_
  24.8 0.5 %shard_map.107.refs_1_ = bf16[16,4096]{1,0:T(8,128)(2,1)S(1)} custom-call(f32[16,4096]{1,0:T(8,128)S(1)} %get-tuple-element.36.refs_0_, f32[16,128]{1,0:T(8,128)S(1)} %get-tuple-element.37.refs_3_.refs_1_, bf16[16,4352]{1,0:T(8,128)(2,1)S(1)} %collective-permute-done.7.refs_2_, bf16[1536,2048]{1,0:T(8,128)(2,1)S(1)} %get-tuple-element.40.refs_3_.refs_4_), custom_call_target="tpu_custom_call" | custom-call | flops 90000000 | tf_op jit(solution)/shard_map/pallas_call | solution.py:56
  25.2 0.1 collective-permute-start.8
  25.3 2.8 %shard_map.108 = (f32[16,2048]{1,0:T(8,128)S(1)}, bf16[1536,2048]{1,0:T(8,128)(2,1)S(1)}) custom-call(bf16[8192,2048]{1,0:T(8,128)(2,1)} %refs_0_.9, bf16[16,4096]{1,0:T(8,128)(2,1)S(1)} %shard_map.107.refs_1_, bf16[1024,2048]{1,0:T(8,128)(2,1)S(1)} %get-tuple-element.41.refs_2_, bf16[512,2048]{1,0:T(8,128)(2,1)S(1)} %get-tuple-element.42.refs_3_, ...), custom_call_target="tpu_custom_call" | custom-call | flops 900000000 | tf_op jit(solution)/shard_map/pallas_call | solution.py:56
  28.1 0.0 collective-permute-done.9.refs_6_
  28.1 1.6 %collective-permute-done.10.refs_7_ = bf16[2,2,16,1024]{3,2,1,0:T(8,128)(2,1)S(1)} collective-permute-done((bf16[2,2,16,1024]{3,2,1,0:T(8,128)(2,1)S(1)}, bf16[2,2,16,1024]{3,2,1,0:T(8,128)(2,1)S(1)}, u32[]{:S(2)}, u32[]{:S(2)}) %collective-permute-start.10) | collective-permute-done | bytes 131104 | tf_op jit(solution)/shard_map/ppermute | solution.py:562
  29.7 0.0 collective-permute-done.11.refs_8_
  29.7 0.0 collective-permute-done.8.refs_2_
  29.7 3.5 %shard_map.109 = (bf16[6,2048]{1,0:T(8,128)(2,1)}, bf16[6,2048]{1,0:T(8,128)(2,1)}, bf16[16,2,16,1024]{3,2,1,0:T(8,128)(2,1)}) custom-call(bf16[8192,2048]{1,0:T(8,128)(2,1)} %refs_0_.9, f32[16,2048]{1,0:T(8,128)S(1)} %get-tuple-element.45.refs_1_, bf16[16,4096]{1,0:T(8,128)(2,1)S(1)} %collective-permute-done.8.refs_2_, ...), custom_call_target="tpu_custom_call", output_to_operand_aliasing={{2}: (9, {})} | custom-call | flops 1020000000 | tf_op jit(solution)/shard_map/pallas_call | solution.py:56
Async XLA Ops:
  0.6 3.6 %collective-permute-start = (bf16[6,2560]{1,0:T(8,128)(2,1)}, bf16[6,2560]{1,0:T(8,128)(2,1)S(1)}, u32[]{:S(2)}, u32[]{:S(2)}) collective-permute-start(bf16[6,2560]{1,0:T(8,128)(2,1)} %refs_6_.1), channel_id=1, source_target_pairs={{0,1},{1,0},{2,3},{3,2},{4,5},{5,4},{6,7},{7,6},{8,9},{9,8},{10,11... | collective-permute-start | bytes 92168 | tf_op jit(solution)/shard_map/ppermute | solution.py:509
  1.2 3.0 %collective-permute-start.1 = (bf16[6,2560]{1,0:T(8,128)(2,1)}, bf16[6,2560]{1,0:T(8,128)(2,1)S(1)}, u32[]{:S(2)}, u32[]{:S(2)}) collective-permute-start(bf16[6,2560]{1,0:T(8,128)(2,1)} %refs_7_.1), channel_id=1, source_target_pairs={{0,1},{1,0},{2,3},{3,2},{4,5},{5,4},{6,7},{7,6},{8,9},{9,8},{10,11... | collective-permute-start | bytes 92168 | tf_op jit(solution)/shard_map/ppermute | solution.py:509
  1.3 6.6 %collective-permute-start.3 = (bf16[6,2560]{1,0:T(8,128)(2,1)}, bf16[6,2560]{1,0:T(8,128)(2,1)S(1)}, u32[]{:S(2)}, u32[]{:S(2)}) collective-permute-start(bf16[6,2560]{1,0:T(8,128)(2,1)} %refs_7_.1), channel_id=1, source_target_pairs={{0,2},{1,3},{2,0},{3,1},{4,6},{5,7},{6,4},{7,5},{8,10},{9,11},{10,... | collective-permute-start | bytes 92168 | tf_op jit(solution)/shard_map/ppermute | solution.py:509
  4.2 4.2 %collective-permute-start.2 = (bf16[6,2560]{1,0:T(8,128)(2,1)}, bf16[6,2560]{1,0:T(8,128)(2,1)S(1)}, u32[]{:S(2)}, u32[]{:S(2)}) collective-permute-start(bf16[6,2560]{1,0:T(8,128)(2,1)} %refs_6_.1), channel_id=1, source_target_pairs={{0,2},{1,3},{2,0},{3,1},{4,6},{5,7},{6,4},{7,5},{8,10},{9,11},{10,... | collective-permute-start | bytes 92168 | tf_op jit(solution)/shard_map/ppermute | solution.py:509
  8.4 1.2 %collective-permute-start.4 = (bf16[6,2560]{1,0:T(8,128)(2,1)S(1)}, bf16[6,2560]{1,0:T(8,128)(2,1)S(1)}, u32[]{:S(2)}, u32[]{:S(2)}) collective-permute-start(bf16[6,2560]{1,0:T(8,128)(2,1)S(1)} %collective-permute-done.2.refs_5_), channel_id=1, source_target_pairs={{0,1},{1,0},{2,3},{3,2},{4,5},{5,4},{6,7},{7,6},{8,9},{9,8},{10,11... | collective-permute-start | bytes 92168 | tf_op jit(solution)/shard_map/ppermute | solution.py:509
  8.4 1.4 %collective-permute-start.5 = (bf16[6,2560]{1,0:T(8,128)(2,1)S(1)}, bf16[6,2560]{1,0:T(8,128)(2,1)S(1)}, u32[]{:S(2)}, u32[]{:S(2)}) collective-permute-start(bf16[6,2560]{1,0:T(8,128)(2,1)S(1)} %collective-permute-done.3.refs_6_), channel_id=1, source_target_pairs={{0,1},{1,0},{2,3},{3,2},{4,5},{5,4},{6,7},{7,6},{8,9},{9,8},{10,11... | collective-permute-start | bytes 92168 | tf_op jit(solution)/shard_map/ppermute | solution.py:509
  12.0 1.4 %collective-permute-start.6 = (bf16[16,4352]{1,0:T(8,128)(2,1)S(1)}, bf16[16,4352]{1,0:T(8,128)(2,1)S(1)}, u32[]{:S(2)}, u32[]{:S(2)}) collective-permute-start(bf16[16,4352]{1,0:T(8,128)(2,1)S(1)} %get-tuple-element.35), channel_id=1, source_target_pairs={{0,1},{1,0},{2,3},{3,2},{4,5},{5,4},{6,7},{7,6},{8,9},{9,8},{10,11... | collective-permute-start | bytes 417800 | tf_op jit(solution)/shard_map/ppermute | solution.py:509
  13.8 11.0 %collective-permute-start.7 = (bf16[16,4352]{1,0:T(8,128)(2,1)S(1)}, bf16[16,4352]{1,0:T(8,128)(2,1)S(1)}, u32[]{:S(2)}, u32[]{:S(2)}) collective-permute-start(bf16[16,4352]{1,0:T(8,128)(2,1)S(1)} %get-tuple-element.38), channel_id=1, source_target_pairs={{0,2},{1,3},{2,0},{3,1},{4,6},{5,7},{6,4},{7,5},{8,10},{9,11},{10,... | collective-permute-start | bytes 417800 | tf_op jit(solution)/shard_map/ppermute | solution.py:509
  15.4 12.8 %collective-permute-start.9 = (bf16[2,2,16,1024]{3,2,1,0:T(8,128)(2,1)S(1)}, bf16[2,2,16,1024]{3,2,1,0:T(8,128)(2,1)S(1)}, u32[]{:S(2)}, u32[]{:S(2)}) collective-permute-start(bf16[2,2,16,1024]{3,2,1,0:T(8,128)(2,1)S(1)} %get-tuple-element.47), channel_id=1, source_target_pairs={{0,4},{4,0},{8,12},{12,8},{1,5},{5,1},{9,13},{13,9},{2,6},{6,2},{1... | collective-permute-start | bytes 393224 | tf_op jit(solution)/shard_map/ppermute | solution.py:562
  16.9 12.9 %collective-permute-start.10 = (bf16[2,2,16,1024]{3,2,1,0:T(8,128)(2,1)S(1)}, bf16[2,2,16,1024]{3,2,1,0:T(8,128)(2,1)S(1)}, u32[]{:S(2)}, u32[]{:S(2)}) collective-permute-start(bf16[2,2,16,1024]{3,2,1,0:T(8,128)(2,1)S(1)} %get-tuple-element.48), channel_id=1, source_target_pairs={{0,8},{4,12},{8,0},{12,4},{1,9},{5,13},{9,1},{13,5},{2,10},{6,14},... | collective-permute-start | bytes 393224 | tf_op jit(solution)/shard_map/ppermute | solution.py:562
  19.5 10.2 %collective-permute-start.11 = (bf16[2,2,16,1024]{3,2,1,0:T(8,128)(2,1)S(1)}, bf16[2,2,16,1024]{3,2,1,0:T(8,128)(2,1)S(1)}, u32[]{:S(2)}, u32[]{:S(2)}) collective-permute-start(bf16[2,2,16,1024]{3,2,1,0:T(8,128)(2,1)S(1)} %get-tuple-element.49), channel_id=1, source_target_pairs={{0,12},{4,8},{8,4},{12,0},{1,13},{5,9},{9,5},{13,1},{2,14},{6,10},... | collective-permute-start | bytes 393224 | tf_op jit(solution)/shard_map/ppermute | solution.py:562
  25.2 4.5 %collective-permute-start.8 = (bf16[16,4096]{1,0:T(8,128)(2,1)S(1)}, bf16[16,4096]{1,0:T(8,128)(2,1)S(1)}, u32[]{:S(2)}, u32[]{:S(2)}) collective-permute-start(bf16[16,4096]{1,0:T(8,128)(2,1)S(1)} %shard_map.107.refs_1_), channel_id=1, source_target_pairs={{0,1},{1,0},{2,3},{3,2},{4,5},{5,4},{6,7},{7,6},{8,9},{9,8},{10,11... | collective-permute-start | bytes 393224 | tf_op jit(solution)/shard_map/ppermute | solution.py:509
